TPU v7x, 512 devices: a whole 4x8x8 slice. The times are simulated.
512 devices in a mesh: front: 8 (over y), row: 8 (over z), col: 8 (over x, core).
Axes of the slice: x: 4, y: 8, z: 8, core: 2. Of those that a mesh axis runs over, the one named last changes fastest.
Arguments:
- pivot: float32 [8, 512, 512], P('front', ('row', 'col')), may hold values from -1 to 8
- col_ut: bfloat16 [8, 8, 96, 512], P('front', 'row', None, 'col'), may hold values from -6 to 6
- col_vt: bfloat16 [8, 8, 96, 512], P('front', 'row', None, 'col'), may hold values from -0.25 to 0.25
- col_rank: int32 [8, 8], P('front', 'row'), may hold values from 32 to 96
- row_ut: bfloat16 [8, 8, 96, 512], P('front', 'col', None, 'row'), may hold values from -6 to 6
- row_vt: bfloat16 [8, 8, 96, 512], P('front', 'col', None, 'row'), may hold values from -0.625 to 0.625
- row_rank: int32 [8, 8], P('front', 'col'), may hold values from 32 to 96
- cb_ut: bfloat16 [8, 8, 8, 96, 512], P('front', 'row', 'col'), may hold values from -6 to 6
- cb_vt: bfloat16 [8, 8, 8, 96, 512], P('front', 'row', 'col'), may hold values from -0.625 to 0.625
- cb_rank: int32 [8, 8, 8], P('front', 'row', 'col'), may hold values from 32 to 96
- parent_map: int32 [8, 8], P('front'), may hold values from 0 to 15, as said below
Outputs:
- parent_tiles: bfloat16 [8, 16, 8, 512, 512], P('front', 'row', 'col')
Inputs may be any that keep to these rules, and one draw needn't show every extreme that they name: `parent_map`: for every front the entries are distinct; entry 0 is 8, and 0 and 15 both appear.
All inputs are finite; a program needn't handle non-finite values.
Results may differ from a plain program's by a relative error of at most 0.0062.
Values may be sent and summed in bfloat16 or wider, within the bound.
No kernel may reach another device: no remote copies, remote signals or barrier semaphores. Data moves between devices by JAX's collectives and lax.ppermute only.
A program may use at most 64 MiB of HBM per device.

v0:
```python
import jax
import jax.numpy as jnp
from jax import lax
from jax.sharding import PartitionSpec as P

NS_ITERS = 2


HIGH = lax.Precision.HIGHEST


def in_order(blocks, dim):
    blocks = jnp.moveaxis(blocks, 0, dim)
    shape = blocks.shape
    return blocks.reshape(*shape[:dim], shape[dim] * shape[dim + 1], *shape[dim + 2 :])


def copy_for_each(x, axis):
    copies = jnp.broadcast_to(x, (lax.axis_size(axis), *x.shape))
    return lax.all_to_all(copies, axis, split_axis=0, concat_axis=0, tiled=True)


def gather_directly(x, axis, dim):
    return in_order(copy_for_each(x, axis), dim)


def gather_turned(arrays, axis, dims):
    turned = [jnp.moveaxis(a, dim, 0) for a, dim in zip(arrays, dims)]
    widths = [t[0].size for t in turned]
    both = jnp.concatenate([t.reshape(-1, w) for t, w in zip(turned, widths)], axis=1)
    result = lax.all_gather(both, axis, axis=0, tiled=True)
    blocks = jnp.split(result, [sum(widths[:k]) for k in range(1, len(widths))], axis=1)
    return tuple(
        (
            jnp.moveaxis(b.reshape(-1, *t.shape[1:]), 0, dim)
            for b, t, dim in zip(blocks, turned, dims)
        )
    )


def sent_together(arrays, axis, dim, along):
    widths = [a.shape[along] for a in arrays]
    both = jnp.concatenate(arrays, axis=along)
    result = lax.all_gather(both, axis, axis=dim, tiled=True)
    return tuple(jnp.split(result, [sum(widths[:k]) for k in range(1, len(widths))], axis=along))


def swapped(x, axis, bit):
    return lax.ppermute(x, axis, [(i, i ^ 1 << bit) for i in range(lax.axis_size(axis))])


def ranked(factor, rank):
    levels = jnp.arange(factor.shape[-2], dtype=jnp.int32)[:, None]
    keep = levels < rank[..., None, None]
    return jnp.where(keep, factor, jnp.zeros_like(factor))


def densify(left, right):
    return jnp.einsum("ijkx,ijky->ijxy", left, right, preferred_element_type=jnp.float32).astype(
        jnp.bfloat16
    )


def selector(mapping, first, count):
    wanted = first + jnp.arange(count, dtype=jnp.int32)
    return (mapping[None, :] == wanted[:, None]).astype(jnp.bfloat16)


def fold_rows(select_rows, carry, pieces):
    results = []
    for total, piece in zip(carry, pieces):
        count = piece.shape[0]
        flat = piece.reshape(count, -1)
        moved = jnp.dot(select_rows, flat, preferred_element_type=jnp.float32).astype(jnp.bfloat16)
        results.append(moved.reshape(total.shape))
    return tuple(results)


def fold_cols(select_cols, carry, pieces):
    results = []
    for total, piece in zip(carry, pieces):
        count = piece.shape[1]
        flat = piece.reshape(piece.shape[0], count, -1)
        moved = jnp.einsum(
            "bj,ajx->abx", select_cols, flat, preferred_element_type=jnp.float32
        ).astype(jnp.bfloat16)
        results.append(moved.reshape(total.shape))
    return tuple(results)


def shards(
    pivot, col_ut, col_vt, col_rank, row_ut, row_vt, row_rank, cb_ut, cb_vt, cb_rank, parent_map
):
    whole = gather_directly(pivot[0], ("row", "col"), 0)
    eye = jnp.eye(whole.shape[0], dtype=jnp.float32)
    approx = eye / jnp.diagonal(whole)[None, :]
    for step in range(NS_ITERS):
        approx = jnp.dot(approx, 2.0 * eye - jnp.dot(whole, approx, precision=HIGH), precision=HIGH)
    column_left, column_right = gather_turned((col_ut[0], col_vt[0]), "col", (2, 2))
    column_left = ranked(column_left, col_rank[0])
    column_right = ranked(column_right, col_rank[0])
    lower = jnp.einsum(
        "atx,xy->aty", column_right.astype(jnp.float32), approx, precision=HIGH
    ).astype(jnp.bfloat16)
    upper_left, upper_right = gather_turned((row_ut[0], row_vt[0]), "row", (2, 2))
    upper_left = ranked(upper_left, row_rank[0])
    upper_right = ranked(upper_right, row_rank[0])
    core = jnp.einsum(
        "iax,jbx->ijab", lower, upper_left, preferred_element_type=jnp.float32
    ).astype(jnp.bfloat16)
    update = jnp.einsum(
        "ijab,iax->ijbx", core, column_left, preferred_element_type=jnp.float32
    ).astype(jnp.bfloat16)
    block_left = ranked(cb_ut[0], cb_rank[0])
    block_right = ranked(cb_vt[0], cb_rank[0])
    rows_here = block_left.shape[0]
    cols_here = block_left.shape[1]
    left = jnp.concatenate([block_left, -update], axis=2)
    right = jnp.concatenate([block_right, upper_right[None]], axis=2)
    parent_rows = 2 * rows_here
    select_rows = selector(parent_map[0], lax.axis_index("row") * parent_rows, parent_rows)
    select_cols = selector(parent_map[0], lax.axis_index("col") * parent_rows, parent_rows)
    factor_shape = left.shape[2:]
    empty_rows = jnp.zeros((parent_rows, cols_here) + factor_shape, jnp.bfloat16)
    rows_left, rows_right = fold_rows(
        select_rows, (empty_rows, empty_rows), sent_together((left, right), "row", 0, 1)
    )
    empty_cols = jnp.zeros((parent_rows, parent_rows) + factor_shape, jnp.bfloat16)
    both_left, both_right = fold_cols(
        select_cols, (empty_cols, empty_cols), sent_together((rows_left, rows_right), "col", 1, 0)
    )
    placed = densify(both_left, both_right)
    side = lax.axis_index("front") % 2
    mine = lax.dynamic_slice_in_dim(placed, side * cols_here, cols_here, 1)
    other = lax.dynamic_slice_in_dim(placed, (1 - side) * cols_here, cols_here, 1)
    received = swapped(other, "front", 0)
    total = mine.astype(jnp.float32) + received.astype(jnp.float32)
    return total.astype(jnp.bfloat16)[None]


def solution(mesh):
    placed = (
        P("front", ("row", "col"), None),
        P("front", "row", None, "col"),
        P("front", "row", None, "col"),
        P("front", "row"),
        P("front", "col", None, "row"),
        P("front", "col", None, "row"),
        P("front", "col"),
        P("front", "row", "col", None, None),
        P("front", "row", "col", None, None),
        P("front", "row", "col"),
        P("front", None),
    )
    return jax.shard_map(
        shards,
        mesh=mesh,
        in_specs=placed,
        out_specs=P("front", "row", "col", None, None),
        check_vma=False,
    )
```

profile of v0, /device:TPU:1, one launch (start us, length us, event | category | flops | bytes accessed | tf_op | source)
XLA Modules:
  0.0 238.1 jit_solution(16976337831034606800)
XLA Ops:
  6.5 1.8 broadcast_in_dim.49
  8.4 15.0 %all-to-all-start = ((f32[64,8,512]{2,1,0:T(8,128)}), f32[64,8,512]{2,1,0:T(8,128)S(1)}, u32[]{:S(2)}, u32[]{:S(2)}) async-start(f32[64,8,512]{2,1,0:T(8,128)} %broadcast_in_dim.49), calls=%async_computation | async-start | bytes 2097152 | tf_op jit(solution)/shard_map/all_to_all | solution.py:20
  23.5 13.7 %all_gather.13 = bf16[512,192]{1,0:T(8,128)(2,1)S(1)} all-gather(bf16[64,192]{1,0:T(8,128)(2,1)S(1)} %pad_maximum_fusion.2), channel_id=1, replica_groups=mesh['front'=8,'row'=8,'col'=8] {'col'}, dimensions={0}, use_global_device_ids=true | all-gather | bytes 221184 | tf_op jit(solution)/shard_map/all_gather | solution.py:31
  38.2 24.5 %all_gather.12 = bf16[512,192]{1,0:T(8,128)(2,1)S(1)} all-gather(bf16[64,192]{1,0:T(8,128)(2,1)S(1)} %pad_maximum_fusion.1), channel_id=1, replica_groups=mesh['front'=8,'row'=8,'col'=8] {'row'}, dimensions={0}, use_global_device_ids=true | all-gather | bytes 221184 | tf_op jit(solution)/shard_map/all_gather | solution.py:31
  64.7 4.7 %gather_fusion = f32[512]{0:T(512)S(1)} fusion(f32[512,512]{1,0:T(8,128)S(1)} %bitcast.142, s32[512]{0:T(512)S(1)} %bitcast.141), kind=kCustom, calls=%fused_computation | custom fusion | bytes 8192 | tf_op jit(solution)/shard_map/jit(diagonal)/cond/branch_0_fun/gather | solution.py:96
  69.4 1.9 select_subtract_fusion.1
  71.3 3.6 %fusion.6 = f32[512,512]{1,0:T(8,128)S(1)} fusion(f32[512,512]{0,1:T(8,128)S(1)} %select_subtract_fusion.1, f32[512]{0:T(512)S(1)} %gather_fusion), kind=kOutput, calls=%fused_computation.24 | convolution fusion | flops 1611399168 | bytes 2099200 | tf_op jit(solution)/shard_map/dot_general | solution.py:98
  74.9 3.5 %select_subtract_fusion = f32[512,512]{0,1:T(8,128)S(1)} fusion(f32[512,512]{1,0:T(8,128)S(1)} %fusion.6, f32[64,8,512]{2,1,0:T(8,128)S(1)} %all-to-all-done), kind=kOutput, calls=%fused_computation.11 | convolution fusion | flops 1611399168 | bytes 3145728 | tf_op jit(solution)/shard_map/dot_general | solution.py:98
  78.3 1.9 fusion.43
  80.2 0.5 convolution_convert_fusion.5
  80.8 0.4 fusion.3
  81.1 0.8 maximum_maximum_fusion
  81.9 0.3 all-gather.5.cloned.1.call-start
  82.2 53.2 %all-gather.3.cloned.1.call-done = bf16[8,2,192,512]{3,2,1,0:T(8,128)(2,1)} async-done(((bf16[1,2,192,512]{3,2,1,0:T(8,128)(2,1)}), bf16[8,2,192,512]{3,2,1,0:T(8,128)(2,1)}) %all-gather.3.cloned.1.call-update) | async-done | bytes 3145744 | tf_op jit(solution)/shard_map/all_gather | solution.py:44
  135.4 2.1 slice_bitcast_fusion.1
  137.5 0.9 copy.37
  138.4 0.9 copy.39
  139.3 0.6 convolution_convert_fusion.3
  139.9 0.6 convolution_convert_fusion.2
  140.6 0.9 pad_maximum_fusion
  141.6 44.9 %all-gather.5.cloned.1.call-done = bf16[4,8,192,512]{3,2,0,1:T(8,128)(2,1)} async-done(((bf16[4,1,192,512]{3,2,0,1:T(8,128)(2,1)}), bf16[4,8,192,512]{3,2,0,1:T(8,128)(2,1)}) %all-gather.5.cloned.1.call-update) | async-done | bytes 6291472 | tf_op jit(solution)/shard_map/all_gather | solution.py:44
  186.6 3.4 %fusion.40 = (bf16[2,8,192,512]{3,2,0,1:T(8,128)(2,1)S(1)}, bf16[2,8,192,512]{3,2,0,1:T(8,128)(2,1)S(1)}) fusion(bf16[4,8,192,512]{3,2,0,1:T(8,128)(2,1)} %all-gather.5.cloned.1.call-done), kind=kLoop, calls=%fused_computation.73 | loop fusion | bytes 12582912 | tf_op jit(solution)/shard_map/split | solution.py:45
  189.9 1.8 copy.31
  191.7 1.9 fusion.1
  193.6 2.4 %reshape.193 = bf16[2,2,192,512]{3,2,1,0:T(8,128)(2,1)} reshape(bf16[2,2,98304]{2,1,0:T(2,128)(2,1)} %fusion.1) | data formatting | bytes 1572864 | tf_op jit(solution)/shard_map/reshape | solution.py:87
  196.0 1.8 copy.30
  197.8 1.0 fusion
  198.8 1.4 reshape.191
  200.3 1.9 convolution_convert_fusion.4
  202.3 3.1 %collective-permute-start = (bf16[2,1,512,512]{3,2,1,0:T(8,128)(2,1)S(1)}, bf16[2,1,512,512]{3,2,1,0:T(8,128)(2,1)}, u32[]{:S(2)}, u32[]{:S(2)}) collective-permute-start(bf16[2,1,512,512]{3,2,1,0:T(8,128)(2,1)S(1)} %constant_dynamic-slice_fusion), channel_id=1, source_target_pairs={{0,64},{64,0},{128,192},{192,128},{256,320},{320,256},{384,448},{4... | collective-permute-start | bytes 3145736 | tf_op jit(solution)/shard_map/ppermute | solution.py:49
  205.5 23.3 %collective-permute-done = bf16[2,1,512,512]{3,2,1,0:T(8,128)(2,1)} collective-permute-done((bf16[2,1,512,512]{3,2,1,0:T(8,128)(2,1)S(1)}, bf16[2,1,512,512]{3,2,1,0:T(8,128)(2,1)}, u32[]{:S(2)}, u32[]{:S(2)}) %collective-permute-start) | collective-permute-done | bytes 1048608 | tf_op jit(solution)/shard_map/ppermute | solution.py:49
  228.8 2.5 %fusion.5 = bf16[1,2,1,512,512]{4,3,2,1,0:T(8,128)(2,1)} fusion(bf16[2,1,512,512]{3,2,1,0:T(8,128)(2,1)} %collective-permute-done, bf16[2,2,512,512]{3,2,1,0:T(8,128)(2,1)S(1)} %convolution_convert_fusion.4, s32[]{:T(128)S(6)} %select_n.76), kind=kLoop, calls=%fused_computation.21 | loop fusion | flops 2097152 | bytes 3145732 | tf_op jit(solution)/shard_map/broadcast_in_dim | solution.py:138
  (38 shorter events, 1.3 us)
Async XLA Ops:
  6.5 16.9 %copy-start.4 = (bf16[1,1,96,64]{2,3,1,0:T(8,128)(2,1)S(1)}, bf16[1,1,96,64]{2,3,1,0:T(8,128)(2,1)}, u32[]{:S(2)}) copy-start(bf16[1,1,96,64]{2,3,1,0:T(8,128)(2,1)} %param.12) | copy-start | bytes 36868
  6.5 16.9 %copy-start.3 = (bf16[1,1,96,64]{2,3,1,0:T(8,128)(2,1)S(1)}, bf16[1,1,96,64]{2,3,1,0:T(8,128)(2,1)}, u32[]{:S(2)}) copy-start(bf16[1,1,96,64]{2,3,1,0:T(8,128)(2,1)} %param.13) | copy-start | bytes 36868
  6.5 31.6 %copy-start.5 = (bf16[1,1,96,64]{2,3,1,0:T(8,128)(2,1)S(1)}, bf16[1,1,96,64]{2,3,1,0:T(8,128)(2,1)}, u32[]{:S(2)}) copy-start(bf16[1,1,96,64]{2,3,1,0:T(8,128)(2,1)} %param.16) | copy-start | bytes 36868
  6.5 31.6 %copy-start.6 = (bf16[1,1,96,64]{2,3,1,0:T(8,128)(2,1)S(1)}, bf16[1,1,96,64]{2,3,1,0:T(8,128)(2,1)}, u32[]{:S(2)}) copy-start(bf16[1,1,96,64]{2,3,1,0:T(8,128)(2,1)} %param.15) | copy-start | bytes 36868
  8.4 56.2 %copy-start.1 = (bf16[1,1,1,96,512]{4,3,2,1,0:T(8,128)(2,1)S(1)}, bf16[1,1,1,96,512]{4,3,2,1,0:T(8,128)(2,1)}, u32[]{:S(2)}) copy-start(bf16[1,1,1,96,512]{4,3,2,1,0:T(8,128)(2,1)} %param.18) | copy-start | bytes 294916
  8.4 56.2 %copy-start.2 = (bf16[1,1,1,96,512]{4,3,2,1,0:T(8,128)(2,1)S(1)}, bf16[1,1,1,96,512]{4,3,2,1,0:T(8,128)(2,1)}, u32[]{:S(2)}) copy-start(bf16[1,1,1,96,512]{4,3,2,1,0:T(8,128)(2,1)} %param.19) | copy-start | bytes 294916
  8.4 56.3 %all-to-all-start = ((f32[64,8,512]{2,1,0:T(8,128)}), f32[64,8,512]{2,1,0:T(8,128)S(1)}, u32[]{:S(2)}, u32[]{:S(2)}) async-start(f32[64,8,512]{2,1,0:T(8,128)} %broadcast_in_dim.49), calls=%async_computation | async-start | bytes 2097152 | tf_op jit(solution)/shard_map/all_to_all | solution.py:20
  23.4 112.1 %all-gather.3.cloned.1.call-start = ((), (), s32[]{:S(2)}) async-start(), calls=%async_computation.1 | async-start | bytes 3538944 | tf_op jit(solution)/shard_map/all_gather | solution.py:44
  81.9 104.6 %all-gather.5.cloned.1.call-start = ((), (), s32[]{:S(2)}) async-start(), calls=%async_computation.2 | async-start | bytes 7077888 | tf_op jit(solution)/shard_map/all_gather | solution.py:44
  138.4 0.9 copy-start.7
  197.8 2.5 %copy-start = (bf16[2,2,192,512]{3,2,1,0:T(8,128)(2,1)S(1)}, bf16[2,2,192,512]{3,2,1,0:T(8,128)(2,1)}, u32[]{:S(2)}) copy-start(bf16[2,2,192,512]{3,2,1,0:T(8,128)(2,1)} %reshape.193) | copy-start | bytes 2359300
  202.3 26.5 %collective-permute-start = (bf16[2,1,512,512]{3,2,1,0:T(8,128)(2,1)S(1)}, bf16[2,1,512,512]{3,2,1,0:T(8,128)(2,1)}, u32[]{:S(2)}, u32[]{:S(2)}) collective-permute-start(bf16[2,1,512,512]{3,2,1,0:T(8,128)(2,1)S(1)} %constant_dynamic-slice_fusion), channel_id=1, source_target_pairs={{0,64},{64,0},{128,192},{192,128},{256,320},{320,256},{384,448},{4... | collective-permute-start | bytes 3145736 | tf_op jit(solution)/shard_map/ppermute | solution.py:49
Sparse Core Ops, SparseCore 0:
  82.1 53.3 all-gather.2
  141.7 44.8 all-gather.4
where the time goes:
time: 239 us; the launch traced here: 238 us
  waiting for transfers between devices  121 us (51%)
  blocking collectives  38.2 us (16%)
  local copies, waits for them, and re-layouts  21.9 us (9%)
  starting transfers between devices  18.4 us (8%)
  matrix products  17.8 us (7%)
  between operations  15.7 us (7%)
  other arithmetic  4.56 us (2%)
    all_gather x2, waiting for transfers between devices, sent_together(): result = lax.all_gather(both, axis, axis=dim, tiled=True)  98.1 us
    all_gather x2, blocking collectives, gather_turned(): result = lax.all_gather(both, axis, axis=0, tiled=True)  38.2 us
    ppermute x1, waiting for transfers between devices, swapped(): lax.ppermute(x, axis, [(i, i ^ 1 << bit) for i in range(lax.axis_size(axi...  23.3 us
    all_to_all x1, starting transfers between devices, copy_for_each(): return lax.all_to_all(copies, axis, split_axis=0, concat_axis=0, tiled=True)  15 us
    split x3, local copies, waits for them, and re-layouts, sent_together(): jnp.split(result, [sum(widths[:k]) for k in range(1, len(widths))], axis=...  6.87 us
    dot_general x2, matrix products, shards(): jnp.dot(approx, 2.0 * eye - jnp.dot(whole, approx, precision=HIGH), preci...  5.44 us
    dot_general x2, matrix products, shards(): jnp.dot(whole, approx, precision=HIGH)  5.34 us
  transfers between devices with their start and end apart: 4, of which 3 were waited for; matrix products, arithmetic and copies ran while one was open for 0% of the time, Pallas kernels for 0%

commit v1 on v0

v1 whole, which is shorter than its diff:
```python
import jax
import jax.numpy as jnp
from jax import lax
from jax.experimental import pallas as pl
from jax.experimental.pallas import tpu as pltpu
from jax.sharding import Mesh, PartitionSpec as P

F32 = jnp.float32
BF16 = jnp.bfloat16
RANK = 96
TILE = 512
N = 8
SMEM = pltpu.SMEM
VMEM = pltpu.VMEM


def iota(shape, dim):
    return lax.broadcasted_iota(jnp.int32, shape, dim)


def dot(a, b, contract, precision=None):
    return lax.dot_general(
        a, b, ((contract[:1], contract[1:]), ((), ())), precision=precision, preferred_element_type=F32
    )


def call(body, outs, args, specs, scratch=(), name=None):
    return pl.pallas_call(
        body,
        out_shape=outs,
        in_specs=[pl.BlockSpec(memory_space=s) for s in specs],
        out_specs=[pl.BlockSpec(memory_space=VMEM) for _ in outs],
        scratch_shapes=scratch,
        name=name,
    )(*args)


def fill_inverse(mapping, inverse):
    for k in range(2 * N):
        inverse[k] = N
    for k in range(N):
        inverse[mapping[0, k]] = k


def onehot(first, step, offset):
    row = iota((64, RANK), 0)
    level = iota((64, RANK), 1)
    t = row % 8
    keep = (t >= first) & (t < first + 6)
    return (keep & (level == step * (row // 8) + offset + t - first)).astype(BF16)


def pack(
    piv, cu, cv, ru, rv, cbu, cbv, rank_c, rank_r, rank_b, send, first, row_v
):
    level = iota((RANK, 64), 0)
    even = onehot(0, 12, 0)
    odd = onehot(0, 12, 6)

    def panel(ref, rank):
        x = jnp.where(level < rank, ref[...].astype(F32), 0.0).astype(BF16)
        return jnp.concatenate([dot(even, x, (1, 0)), dot(odd, x, (1, 0))], axis=1)

    col_u = panel(cu, rank_c[0, 0])
    col_v = panel(cv, rank_c[0, 0])
    row_u = panel(ru, rank_r[0, 0])
    row_v[...] = panel(rv, rank_r[0, 0])
    pieces = [piv[:, 128 * m : 128 * m + 128] for m in range(4)]
    both = jnp.concatenate(pieces + [col_u], axis=0)
    for k in range(N):
        first[k] = both
    wide = iota((RANK, TILE), 0)
    row = iota((64, RANK), 0)
    lev = iota((64, RANK), 1)
    t = row % 8
    extra = [
        ((t >= 6) & (lev == 64 + 4 * (row // 8) + 2 * e + t - 6)).astype(BF16) for e in range(2)
    ]
    for side, ref in enumerate((cbu, cbv)):
        x = jnp.where(wide < rank_b[0, 0], ref[...].astype(F32), 0.0)
        low = x.astype(BF16)
        x1 = dot(extra[0], low, (1, 0))
        x2 = dot(extra[1], low, (1, 0))
        for g in range(N):
            rows = slice(8 * g, 8 * g + 8)
            for m in range(4):
                lanes = slice(128 * m, 128 * m + 128)
                c = 2 * m + side
                send[g * N + c] = jnp.concatenate(
                    [
                        x[rows, lanes],
                        col_v[rows] + x1[rows, lanes],
                        row_u[8 * c : 8 * c + 8] + x2[rows, lanes],
                    ],
                    axis=0,
                ).astype(BF16)


def second(got, row_v, mapping, send_p, send_u, inverse):
    fill_inverse(mapping, inverse)
    for g in range(N):
        block = got[g, 0:32, :]
        for k in range(N):
            send_p[k, 32 * g : 32 * g + 32, :] = block
    tail = row_v[...]
    for k in range(N):
        send_p[k, 256:320, :] = tail
    here = lax.axis_index("row")
    for s in range(2):
        at = inverse[2 * here + s]
        x = got[jnp.minimum(at, N - 1), 32:96, :]
        x = jnp.where(at < N, x, jnp.zeros_like(x)).astype(BF16)
        for k in range(2 * N):
            send_u[k, 64 * s : 64 * s + 64, :] = x


def select(got, mapping, send, inverse, t0, g0, g1):
    fill_inverse(mapping, inverse)
    row = iota((8, 128), 0)
    zero = jnp.zeros((8, 128), F32)
    t0[64] = zero
    g0[64] = zero
    g1[64] = zero
    for k in range(64):
        x = got[k].astype(F32)
        a, b = x[8:16], x[16:24]
        t0[k] = x[0:8]
        g0[k] = jnp.where(row >= 6, a, jnp.where(row >= 4, pltpu.roll(b, 6, 0), 0.0))
        g1[k] = jnp.where(
            row >= 4, 0.0, jnp.where(row >= 2, pltpu.roll(a, 4, 0), pltpu.roll(b, 2, 0))
        )

    def place(r, _):
        i0 = inverse[2 * r]
        i1 = inverse[2 * r + 1]
        for h in range(2):
            for c in range(N):
                j = inverse[2 * c + h]
                at0 = jnp.where((i0 < N) & (j < N), i0 * N + j, 64)
                at1 = jnp.where((i1 < N) & (j < N), i1 * N + j, 64)
                send[(h * N + r) * N + c] = jnp.concatenate(
                    [t0[at0], t0[at1], g0[at0] + g1[at1]], axis=0
                ).astype(BF16)
        return 0

    lax.fori_loop(0, N, place, 0)


def spread(tiles):
    lane = iota(tiles[0].shape, 1)
    halves = ([], [])
    for m in range(N // 2):
        x, y = tiles[2 * m], tiles[2 * m + 1]
        halves[0].append(jnp.where(lane < 64, x, pltpu.roll(y, 64, 1)))
        halves[1].append(jnp.where(lane < 64, pltpu.roll(x, 64, 1), y))
    return [jnp.concatenate(h, axis=1) for h in halves]


def cores(got, pieces, mapping, send_c, send_v, inverse, pivot, lower_ref, right_ref):
    fill_inverse(mapping, inverse)
    for c in range(N):
        for g in range(N):
            for m in range(4):
                at = 32 * g + 8 * m
                pivot[64 * g + 8 * c : 64 * g + 8 * c + 8, 128 * m : 128 * m + 128] = pieces[
                    c, at : at + 8, :
                ]
    here = lax.axis_index("col")
    for h in range(2):
        at = inverse[2 * here + h]
        x = pieces[jnp.minimum(at, N - 1), 256:320, :]
        x = jnp.where(at < N, x, jnp.zeros_like(x)).astype(BF16)
        for r in range(N):
            send_v[h * N + r] = x
    full = pivot[...]
    eye = iota((TILE, TILE), 0) == iota((TILE, TILE), 1)
    inv = 1.0 / jnp.sum(jnp.where(eye, full, 0.0), axis=0, keepdims=True)
    valid = iota((8, 128), 0) < 6

    def tile(i, j, at):
        return jnp.where(valid, got[i * N + j, at : at + 8, :].astype(F32), 0.0)

    left = [[], []]
    for i in range(N):
        parts = spread([tile(i, j, 8) for j in range(N)])
        left[0].append(parts[0])
        left[1].append(parts[1])
    v = jnp.concatenate(left[0] + left[1], axis=0)
    high = lax.Precision.HIGHEST
    v0 = v * inv
    y = 2.0 * v0 - dot(v0, full, (1, 0), high) * inv
    z = dot(y, full, (1, 0), high) * inv
    lower = 2.0 * y - (2.0 * z - dot(z, full, (1, 0), high) * inv)
    for k in range(2 * N):
        lower_ref[k] = lower[8 * k : 8 * k + 8]
    lower_ref[2 * N] = jnp.zeros((8, TILE), F32)
    right_ref[2 * N] = jnp.zeros((8, TILE), F32)
    for j in range(N):
        parts = spread([tile(i, j, 16) for i in range(N)])
        right_ref[2 * j] = parts[0]
        right_ref[2 * j + 1] = parts[1]
    rows = []
    for half in range(2):
        for s in range(2):
            for r in range(N):
                i = inverse[2 * r + s]
                rows.append(lower_ref[jnp.where(i < N, half * N + i, 2 * N)])
    cols = []
    for k in range(2 * N):
        j = inverse[k]
        for half in range(2):
            cols.append(right_ref[jnp.where(j < N, 2 * j + half, 2 * N)])
    core = dot(
        jnp.concatenate(rows, axis=0).astype(BF16), jnp.concatenate(cols, axis=0).astype(BF16), (1, 1)
    )
    core = core.astype(BF16).astype(F32)
    lane = iota((64, 128), 1) // 16
    for k in range(2 * N):
        c, h = k // 2, k % 2
        total = jnp.zeros((64, 128), F32)
        for combo in range(4):
            x = core[64 * combo : 64 * combo + 64, 128 * (k // 8) : 128 * (k // 8) + 128]
            shift = (16 * combo - 16 * (k % 8)) % 128
            total = jnp.where(lane == combo, pltpu.roll(x, shift, 1) if shift else x, total)
        for r in range(N):
            send_c[(h * N + r) * N + c] = total[8 * r : 8 * r + 8].astype(BF16)


def finish(blocks, core_in, col_in, row_in, out):
    lefts, rights = [], []
    for f in range(2):
        for side, into in ((0, lefts), (1, rights)):
            lanes = []
            for m in range(4):
                c = 2 * m + side
                lanes.append(
                    jnp.concatenate(
                        [blocks[f * 64 + g * N + c].astype(F32) for g in range(N)], axis=0
                    )
                )
            into.append(jnp.concatenate(lanes, axis=1))
    left = jnp.concatenate(lefts, axis=0)
    row = iota(left.shape, 0) % 24
    slots = (
        (row < 8) | (row >= 20),
        (row >= 8) & (row < 20),
    )
    lane = iota((64, 128), 1) // 16
    updates = [[], []]
    for f in range(2):
        parts = [
            jnp.concatenate(
                [core_in[f * 64 + g * N + c].astype(F32) for g in range(N)], axis=0
            )
            for c in range(N)
        ]
        for s in range(2):
            halves = []
            for half in range(2):
                total = jnp.zeros((64, 128), F32)
                combo = 2 * half + s
                for c in range(N):
                    shift = (16 * c - 16 * combo) % 128
                    x = pltpu.roll(parts[c], shift, 1) if shift else parts[c]
                    total = jnp.where(lane == c, x, total)
                halves.append(total)
            core = jnp.concatenate(halves, axis=0).astype(BF16)
            col_u = spread(
                [col_in[f * N + c, 64 * s : 64 * s + 64, :].astype(F32) for c in range(N)]
            )
            col_u = jnp.concatenate(col_u, axis=0).astype(BF16)
            updates[s].append(-dot(core, col_u, (0, 0)))
        v0, v1 = spread([row_in[f * N + r].astype(F32) for r in range(N)])
        mixed = []
        for g in range(N):
            mixed += [v0[8 * g : 8 * g + 8], v1[8 * g : 8 * g + 8]]
        rights.append(jnp.concatenate(mixed, axis=0))
    right = jnp.concatenate(rights, axis=0).astype(BF16)
    for s in range(2):
        both = jnp.concatenate([jnp.where(slots[s], left, 0.0)] + updates[s], axis=0).astype(BF16)
        out[s] = dot(both, right, (0, 0)).astype(BF16)


def exchange(x, axes):
    return lax.all_to_all(x, axes, split_axis=0, concat_axis=0, tiled=True)


def shards(
    pivot, col_ut, col_vt, col_rank, row_ut, row_vt, row_rank, cb_ut, cb_vt, cb_rank, parent_map
):
    sds = jax.ShapeDtypeStruct
    send, first, row_v = call(
        pack,
        (sds((64, 24, 128), BF16), sds((N, 96, 128), F32), sds((64, 128), F32)),
        (
            pivot[0],
            col_ut[0, 0],
            col_vt[0, 0],
            row_ut[0, 0],
            row_vt[0, 0],
            cb_ut[0, 0, 0],
            cb_vt[0, 0, 0],
            col_rank,
            row_rank,
            cb_rank[0],
        ),
        (VMEM,) * 7 + (SMEM,) * 3,
        name="pack",
    )
    got_first = exchange(first, "row")
    got = exchange(send, ("row", "col"))
    send_p, send_u = call(
        second,
        (sds((N, 320, 128), F32), sds((2 * N, 128, 128), BF16)),
        (got_first, row_v, parent_map),
        (VMEM, VMEM, SMEM),
        (pltpu.SMEM((2 * N,), jnp.int32),),
        name="second",
    )
    pieces = exchange(send_p, "col")
    col_in = exchange(send_u, ("side", "col"))
    (send_b,) = call(
        select,
        (sds((128, 24, 128), BF16),),
        (got, parent_map),
        (VMEM, SMEM),
        (pltpu.SMEM((2 * N,), jnp.int32),) + (VMEM((65, 8, 128), F32),) * 3,
        name="select",
    )
    blocks = exchange(send_b, ("side", "row", "col"))
    send_c, send_v = call(
        cores,
        (sds((128, 8, 128), BF16), sds((2 * N, 64, 128), BF16)),
        (got, pieces, parent_map),
        (VMEM, VMEM, SMEM),
        (
            pltpu.SMEM((2 * N,), jnp.int32),
            VMEM((TILE, TILE), F32),
            VMEM((2 * N + 1, 8, TILE), F32),
            VMEM((2 * N + 1, 8, TILE), F32),
        ),
        name="cores",
    )
    core_in = exchange(send_c, ("side", "row", "col"))
    row_in = exchange(send_v, ("side", "row"))
    (out,) = call(
        finish,
        (sds((2, TILE, TILE), BF16),),
        (blocks, core_in, col_in, row_in),
        (VMEM,) * 4,
        name="finish",
    )
    return out[None, :, None]


def solution(mesh):
    front = ("pair", "side")
    split = Mesh(mesh.devices.reshape(4, 2, N, N), ("pair", "side", "row", "col"))
    placed = (
        P(front, ("row", "col"), None),
        P(front, "row", None, "col"),
        P(front, "row", None, "col"),
        P(front, "row"),
        P(front, "col", None, "row"),
        P(front, "col", None, "row"),
        P(front, "col"),
        P(front, "row", "col", None, None),
        P(front, "row", "col", None, None),
        P(front, "row", "col"),
        P(front, None),
    )
    return jax.shard_map(
        shards,
        mesh=split,
        in_specs=placed,
        out_specs=P(front, "row", "col", None, None),
        check_vma=False,
    )
```

time: 239 us -> 165 us (0.69)
  waiting for transfers between devices: 121 us -> 23.7 us
  blocking collectives: 38.2 us -> 101 us
  matrix products: 17.8 us -> 0 us
  local copies, waits for them, and re-layouts: 21.9 us -> 5.71 us
  Pallas kernels: 0 us -> 15.7 us
  between operations: 15.7 us -> 1.98 us
  other arithmetic: 4.56 us -> 0 us
    all_to_all x0 -> x4, blocking collectives: none -> 101 us  [exchange(): return lax.all_to_all(x, axes, split_axis=0, concat_axis=0, tiled=True)]
    all_gather x2 -> x0, waiting for transfers between devices: 98.1 us -> none  [sent_together(): result = lax.all_gather(both, axis, axis=dim, tiled=True)]
    all_gather x2 -> x0, blocking collectives: 38.2 us -> none  [gather_turned(): result = lax.all_gather(both, axis, axis=0, tiled=True)]
    all_to_all x1 -> x3, waiting for transfers between devices: 0.01 us -> 23.7 us  [exchange(): return lax.all_to_all(x, axes, split_axis=0, concat_axis=0, tiled=True)]
    ppermute x1 -> x0, waiting for transfers between devices: 23.3 us -> none  [swapped(): lax.ppermute(x, axis, [(i, i ^ 1 << bit) for i in range(lax.axis_size(axi...]
    dot_general x11 -> x0, matrix products: 17.8 us -> none  [the longest x2 5.44 us: shards(): jnp.dot(approx, 2.0 * eye - jnp.dot(whole, approx, precision=HIGH), preci...]
    pallas_call x0 -> x5, Pallas kernels: none -> 15.7 us  [call(): pl.pallas_call(body, out_shape=outs, in_specs=[pl.BlockSpec(memory_space=...]
    split x5 -> x0, local copies, waits for them, and re-layouts: 7.09 us -> none  [the longest x3 6.87 us: sent_together(): jnp.split(result, [sum(widths[:k]) for k in range(1, len(widths))], axis=...]
  transfers between devices with their start and end apart: 4 -> 3, of which waited for: 3 -> 3; matrix products, arithmetic and copies ran while one was open for 0% -> 0% of each run, Pallas kernels for 0% -> 6%
where the time goes in v1:
time: 165 us; the launch traced here: 164 us
  blocking collectives  101 us (61%)
  waiting for transfers between devices  23.7 us (14%)
  starting transfers between devices  16.2 us (10%)
  Pallas kernels  15.7 us (10%)
  local copies, waits for them, and re-layouts  5.71 us (3%)
  between operations  1.98 us (1%)
    all_to_all x4, blocking collectives, exchange(): return lax.all_to_all(x, axes, split_axis=0, concat_axis=0, tiled=True)  101 us
    all_to_all x3, waiting for transfers between devices, exchange(): return lax.all_to_all(x, axes, split_axis=0, concat_axis=0, tiled=True)  23.7 us
    all_to_all x3, starting transfers between devices, exchange(): return lax.all_to_all(x, axes, split_axis=0, concat_axis=0, tiled=True)  16.2 us
    pallas_call x5, Pallas kernels, call(): pl.pallas_call(body, out_shape=outs, in_specs=[pl.BlockSpec(memory_space=...  15.7 us
    unnamed x12, local copies, waits for them, and re-layouts  5.71 us
  transfers between devices with their start and end apart: 3, of which 3 were waited for; matrix products, arithmetic and copies ran while one was open for 0% of the time, Pallas kernels for 6%

profile of v1, /device:TPU:1, one launch (start us, length us, event | category | flops | bytes accessed | tf_op | source)
XLA Modules:
  0.0 163.8 jit_solution(12130815250750898295)
XLA Ops:
  0.0 1.4 copy.12
  1.4 1.4 copy.13
  2.8 1.4 copy.14
  4.3 1.4 copy.15
  7.6 2.2 %pack.1 = (bf16[64,24,128]{2,1,0:T(8,128)(2,1)}, f32[8,96,128]{2,1,0:T(8,128)}, f32[64,128]{1,0:T(8,128)}) custom-call(f32[8,512]{1,0:T(8,128)} %bitcast.18, bf16[96,64]{1,0:T(8,128)(2,1)} %bitcast.14, bf16[96,64]{1,0:T(8,128)(2,1)} %bitcast.15, bf16[96,64]{1,0:T(8,128)(2,1)} %bitcast.16, bf16[96,64]{1,0:T(8,128)(2,1)} %bitcast.17, ...), custom_call_target="tpu_custom_call" | custom-call | tf_op jit(solution)/shard_map/pack/pallas_call | solution.py:28
  9.8 24.5 %all_to_all.35.got = f32[8,96,128]{2,1,0:T(8,128)} all-to-all(f32[8,96,128]{2,1,0:T(8,128)} %get-tuple-element.13), channel_id=1, replica_groups=mesh['pair'=4,'side'=2,'row'=8,'col'=8] {'row'}, dimensions={0} | all-to-all | bytes 786432 | tf_op jit(solution)/shard_map/all_to_all | solution.py:285
  34.3 6.9 %all-to-all-start = ((bf16[64,24,128]{2,1,0:T(8,128)(2,1)}), bf16[64,24,128]{2,1,0:T(8,128)(2,1)S(1)}, u32[]{:S(2)}, u32[]{:S(2)}) async-start(bf16[64,24,128]{2,1,0:T(8,128)(2,1)} %get-tuple-element.12), calls=%async_computation | async-start | bytes 786432 | tf_op jit(solution)/shard_map/all_to_all | solution.py:285
  41.3 2.3 %second.1 = (f32[8,320,128]{2,1,0:T(8,128)}, bf16[16,128,128]{2,1,0:T(8,128)(2,1)}) custom-call(f32[8,96,128]{2,1,0:T(8,128)} %all_to_all.35.got, f32[64,128]{1,0:T(8,128)} %get-tuple-element.14.row_v, s32[1,8]{1,0:T(1,128)} %mapping.5), custom_call_target="tpu_custom_call" | custom-call | tf_op jit(solution)/shard_map/second/pallas_call | solution.py:28
  43.6 12.8 %all-to-all-done.got = bf16[64,24,128]{2,1,0:T(8,128)(2,1)S(1)} async-done(((bf16[64,24,128]{2,1,0:T(8,128)(2,1)}), bf16[64,24,128]{2,1,0:T(8,128)(2,1)S(1)}, u32[]{:S(2)}, u32[]{:S(2)}) %all-to-all-start) | async-done | bytes 393248 | tf_op jit(solution)/shard_map/all_to_all | solution.py:285
  56.4 0.0 copy-start
  56.4 22.3 %all_to_all.36.pieces = f32[8,320,128]{2,1,0:T(8,128)} all-to-all(f32[8,320,128]{2,1,0:T(8,128)} %get-tuple-element.15), channel_id=1, replica_groups=mesh['pair'=4,'side'=2,'row'=8,'col'=8] {'col'}, dimensions={0} | all-to-all | bytes 2621440 | tf_op jit(solution)/shard_map/all_to_all | solution.py:285
  78.7 0.0 copy-done
  78.7 4.5 %all-to-all-start.5 = ((bf16[16,128,128]{2,1,0:T(8,128)(2,1)}), bf16[16,128,128]{2,1,0:T(8,128)(2,1)S(1)}, u32[]{:S(2)}, u32[]{:S(2)}) async-start(bf16[16,128,128]{2,1,0:T(8,128)(2,1)} %get-tuple-element.17), calls=%async_computation.5 | async-start | bytes 1048576 | tf_op jit(solution)/shard_map/all_to_all | solution.py:285
  83.2 4.5 %cores.1 = (bf16[128,8,128]{2,1,0:T(8,128)(2,1)}, bf16[16,64,128]{2,1,0:T(8,128)(2,1)}) custom-call(bf16[64,24,128]{2,1,0:T(8,128)(2,1)} %copy-done, f32[8,320,128]{2,1,0:T(8,128)} %all_to_all.36.pieces, s32[1,8]{1,0:T(1,128)} %mapping.5), custom_call_target="tpu_custom_call" | custom-call | tf_op jit(solution)/shard_map/cores/pallas_call | solution.py:28
  87.7 5.1 %all-to-all-done.5.col_in = bf16[16,128,128]{2,1,0:T(8,128)(2,1)S(1)} async-done(((bf16[16,128,128]{2,1,0:T(8,128)(2,1)}), bf16[16,128,128]{2,1,0:T(8,128)(2,1)S(1)}, u32[]{:S(2)}, u32[]{:S(2)}) %all-to-all-start.5) | async-done | bytes 524320 | tf_op jit(solution)/shard_map/all_to_all | solution.py:285
  92.8 0.0 copy-start.1
  92.8 4.7 %all-to-all-start.6 = ((bf16[16,64,128]{2,1,0:T(8,128)(2,1)}), bf16[16,64,128]{2,1,0:T(8,128)(2,1)S(1)}, u32[]{:S(2)}, u32[]{:S(2)}) async-start(bf16[16,64,128]{2,1,0:T(8,128)(2,1)} %get-tuple-element.18), calls=%async_computation.6 | async-start | bytes 524288 | tf_op jit(solution)/shard_map/all_to_all | solution.py:285
  97.6 0.0 copy-start.3
  97.6 2.6 %select.1 = bf16[128,24,128]{2,1,0:T(8,128)(2,1)} custom-call(bf16[64,24,128]{2,1,0:T(8,128)(2,1)} %copy-done, s32[1,8]{1,0:T(1,128)} %mapping.5), custom_call_target="tpu_custom_call" | custom-call | tf_op jit(solution)/shard_map/select/pallas_call | solution.py:28
  100.2 5.7 %all-to-all-done.6.row_in = bf16[16,64,128]{2,1,0:T(8,128)(2,1)S(1)} async-done(((bf16[16,64,128]{2,1,0:T(8,128)(2,1)}), bf16[16,64,128]{2,1,0:T(8,128)(2,1)S(1)}, u32[]{:S(2)}, u32[]{:S(2)}) %all-to-all-start.6) | async-done | bytes 262176 | tf_op jit(solution)/shard_map/all_to_all | solution.py:285
  105.9 0.0 copy-start.2
  105.9 33.7 %all_to_all.37.blocks = bf16[128,24,128]{2,1,0:T(8,128)(2,1)} all-to-all(bf16[128,24,128]{2,1,0:T(8,128)(2,1)} %select.1), channel_id=1, replica_groups=mesh['pair'=4,'side'=2,'row'=8,'col'=8] {'side','row','col'}, dimensions={0} | all-to-all | bytes 1572864 | tf_op jit(solution)/shard_map/all_to_all | solution.py:285
  139.6 0.0 copy-done.1
  139.6 0.0 copy-done.3
  139.6 20.1 %all_to_all.38.core_in = bf16[128,8,128]{2,1,0:T(8,128)(2,1)} all-to-all(bf16[128,8,128]{2,1,0:T(8,128)(2,1)S(1)} %copy-done.3), channel_id=1, replica_groups=mesh['pair'=4,'side'=2,'row'=8,'col'=8] {'side','row','col'}, dimensions={0} | all-to-all | bytes 524288 | tf_op jit(solution)/shard_map/all_to_all | solution.py:285
  159.7 0.0 copy-done.2
  159.7 4.1 %finish.1 = bf16[2,512,512]{2,1,0:T(8,128)(2,1)} custom-call(bf16[128,24,128]{2,1,0:T(8,128)(2,1)} %all_to_all.37.blocks, bf16[128,8,128]{2,1,0:T(8,128)(2,1)} %all_to_all.38.core_in, bf16[16,128,128]{2,1,0:T(8,128)(2,1)} %copy-done.1, bf16[16,64,128]{2,1,0:T(8,128)(2,1)} %copy-done.2), custom_call_target="tpu_custom_call" | custom-call | tf_op jit(solution)/shard_map/finish/pallas_call | solution.py:28
Async XLA Ops:
  34.3 22.1 %all-to-all-start = ((bf16[64,24,128]{2,1,0:T(8,128)(2,1)}), bf16[64,24,128]{2,1,0:T(8,128)(2,1)S(1)}, u32[]{:S(2)}, u32[]{:S(2)}) async-start(bf16[64,24,128]{2,1,0:T(8,128)(2,1)} %get-tuple-element.12), calls=%async_computation | async-start | bytes 786432 | tf_op jit(solution)/shard_map/all_to_all | solution.py:285
  56.4 22.3 %copy-start = (bf16[64,24,128]{2,1,0:T(8,128)(2,1)}, bf16[64,24,128]{2,1,0:T(8,128)(2,1)S(1)}, u32[]{:S(2)}) copy-start(bf16[64,24,128]{2,1,0:T(8,128)(2,1)S(1)} %all-to-all-done.got) | copy-start | bytes 1179652
  78.7 14.2 %all-to-all-start.5 = ((bf16[16,128,128]{2,1,0:T(8,128)(2,1)}), bf16[16,128,128]{2,1,0:T(8,128)(2,1)S(1)}, u32[]{:S(2)}, u32[]{:S(2)}) async-start(bf16[16,128,128]{2,1,0:T(8,128)(2,1)} %get-tuple-element.17), calls=%async_computation.5 | async-start | bytes 1048576 | tf_op jit(solution)/shard_map/all_to_all | solution.py:285
  92.8 46.7 %copy-start.1 = (bf16[16,128,128]{2,1,0:T(8,128)(2,1)}, bf16[16,128,128]{2,1,0:T(8,128)(2,1)S(1)}, u32[]{:S(2)}) copy-start(bf16[16,128,128]{2,1,0:T(8,128)(2,1)S(1)} %all-to-all-done.5.col_in) | copy-start | bytes 1572868
  92.8 13.0 %all-to-all-start.6 = ((bf16[16,64,128]{2,1,0:T(8,128)(2,1)}), bf16[16,64,128]{2,1,0:T(8,128)(2,1)S(1)}, u32[]{:S(2)}, u32[]{:S(2)}) async-start(bf16[16,64,128]{2,1,0:T(8,128)(2,1)} %get-tuple-element.18), calls=%async_computation.6 | async-start | bytes 524288 | tf_op jit(solution)/shard_map/all_to_all | solution.py:285
  97.6 42.0 %copy-start.3 = (bf16[128,8,128]{2,1,0:T(8,128)(2,1)S(1)}, bf16[128,8,128]{2,1,0:T(8,128)(2,1)}, u32[]{:S(2)}) copy-start(bf16[128,8,128]{2,1,0:T(8,128)(2,1)} %get-tuple-element.16) | copy-start | bytes 786436
  105.9 53.8 %copy-start.2 = (bf16[16,64,128]{2,1,0:T(8,128)(2,1)}, bf16[16,64,128]{2,1,0:T(8,128)(2,1)S(1)}, u32[]{:S(2)}) copy-start(bf16[16,64,128]{2,1,0:T(8,128)(2,1)S(1)} %all-to-all-done.6.row_in) | copy-start | bytes 786436

commit v2 on v1

v2 whole, which is shorter than its diff:
```python
import jax
import jax.numpy as jnp
from jax import lax
from jax.experimental import pallas as pl
from jax.experimental.pallas import tpu as pltpu
from jax.sharding import Mesh, PartitionSpec as P


F32 = jnp.float32
BF16 = jnp.bfloat16
RANK = 96
TILE = 512
N = 8
SMEM = pltpu.SMEM
VMEM = pltpu.VMEM


def iota(shape, dim):
    return lax.broadcasted_iota(jnp.int32, shape, dim)


def dot(a, b, contract):
    return lax.dot_general(
        a, b, ((contract[:1], contract[1:]), ((), ())), preferred_element_type=F32
    )


def call(body, outs, args, specs, scratch=()):
    return pl.pallas_call(
        body,
        out_shape=outs,
        in_specs=[pl.BlockSpec(memory_space=s) for s in specs],
        out_specs=[pl.BlockSpec(memory_space=VMEM) for _ in outs],
        scratch_shapes=scratch,
    )(*args)


def fill_inverse(mapping, inverse):
    for k in range(2 * N):
        inverse[k] = N
    for k in range(N):
        inverse[mapping[0, k]] = k


def onehot(offset):
    row = iota((64, RANK), 0)
    level = iota((64, RANK), 1)
    t = row % 8
    return ((t < 6) & (level == 12 * (row // 8) + offset + t)).astype(BF16)


def pack(piv, cu, cv, ru, rv, cbu, cbv, rank_c, rank_r, rank_b, send, col_u):
    level = iota((64, RANK), 1)
    even = onehot(0)
    odd = onehot(6)

    def panel(ref, rank):
        x = jnp.where(level < rank, ref[...].astype(F32), 0.0).astype(BF16)
        return jnp.concatenate([dot(even, x, (1, 1)), dot(odd, x, (1, 1))], axis=1)

    col_u[...] = panel(cu, rank_c[...]).astype(BF16)
    col_v = panel(cv, rank_c[...])
    row_u = panel(ru, rank_r[...])
    row_v = panel(rv, rank_r[...]).astype(BF16)
    r = lax.axis_index("row")
    q = r * N + lax.axis_index("col")
    full = piv[...]
    on_diag = iota((8, TILE), 1) == 8 * q + iota((8, TILE), 0)
    diag = jnp.sum(jnp.where(on_diag, full, 0.0), axis=1, keepdims=True)
    off = jnp.where(on_diag, 0.0, full)
    lane = iota((8, 128), 1)
    sub = iota((8, 128), 0)
    here = 8 * lax.axis_index("col") + sub
    high = diag.astype(BF16).astype(F32)
    rest = diag - high
    mid = rest.astype(BF16).astype(F32)
    low = rest - mid
    zero = jnp.zeros((8, 128), F32)
    first = jnp.where(lane == here, high, jnp.where(lane == 64 + here, mid, zero))
    first = jnp.sum(first, axis=0, keepdims=True)
    last = jnp.sum(jnp.where(lane == here, low, zero), axis=0, keepdims=True)
    parts = jnp.where(sub == 6, first, jnp.where(sub == 7, last, zero))
    pivot = [off[:, 128 * m : 128 * m + 128] for m in range(4)]
    wide = iota((RANK, TILE), 0)
    row = iota((64, RANK), 0)
    lev = iota((64, RANK), 1)
    t = row % 8
    extra = [
        ((t >= 6) & (lev == 64 + 4 * (row // 8) + 2 * e + t - 6)).astype(BF16) for e in range(2)
    ]
    from_lane = iota((128, 128), 0)
    to_lane = iota((128, 128), 1)
    same = (from_lane // 64 == to_lane // 64) & ((to_lane // 8) % 8 == r)
    thin = []
    for g in range(N):
        move = same & (from_lane % 64 == 8 * g + to_lane % 8)
        thin.append(dot(row_v, move.astype(BF16), (1, 0)))
    for side, ref in enumerate((cbu, cbv)):
        x = jnp.where(wide < rank_b[0], ref[...].astype(F32), 0.0)
        narrow = x.astype(BF16)
        x1 = dot(extra[0], narrow, (1, 0))
        x2 = dot(extra[1], narrow, (1, 0))
        for g in range(N):
            rows = slice(8 * g, 8 * g + 8)
            for m in range(4):
                lanes = slice(128 * m, 128 * m + 128)
                c = 2 * m + side
                send[g * N + c] = jnp.concatenate(
                    [
                        x[rows, lanes],
                        col_v[rows] + x1[rows, lanes],
                        row_u[8 * c : 8 * c + 8] + x2[rows, lanes],
                    ]
                    + pivot
                    + [thin[g][8 * c : 8 * c + 8] + parts],
                    axis=0,
                ).astype(BF16)


def slots(got, mapping, send, inverse):
    fill_inverse(mapping, inverse)
    here = lax.axis_index("row")
    for s in range(2):
        at = inverse[2 * here + s]
        x = got[jnp.minimum(at, N - 1)].astype(F32)
        x = jnp.where(at < N, x, jnp.zeros_like(x)).astype(BF16)
        send[64 * s : 64 * s + 64, :] = x


def spread(tiles):
    lane = iota(tiles[0].shape, 1)
    halves = ([], [])
    for m in range(N // 2):
        x, y = tiles[2 * m], tiles[2 * m + 1]
        halves[0].append(jnp.where(lane < 64, x, pltpu.roll(y, 64, 1)))
        halves[1].append(jnp.where(lane < 64, pltpu.roll(x, 64, 1), y))
    return [jnp.concatenate(h, axis=1) for h in halves]


def route(got, mapping, send, inverse, t0, g0, g1, lower_ref, right_ref, tail_ref):
    fill_inverse(mapping, inverse)
    sub = iota((8, 128), 0)
    valid = sub < 6
    zero = jnp.zeros((8, 128), F32)
    t0[64] = zero
    g0[64] = zero
    g1[64] = zero
    left = [[], []]
    diag = []
    right = [[] for _ in range(N)]
    thin = [zero] * N
    for i in range(N):
        row_tiles = []
        total = zero
        for j in range(N):
            k = i * N + j
            x = got[k, 0:24, :].astype(F32)
            a, b = x[8:16], x[16:24]
            t0[k] = x[0:8]
            g0[k] = jnp.where(sub >= 6, a, jnp.where(sub >= 4, pltpu.roll(b, 6, 0), 0.0))
            g1[k] = jnp.where(
                sub >= 4, 0.0, jnp.where(sub >= 2, pltpu.roll(a, 4, 0), pltpu.roll(b, 2, 0))
            )
            row_tiles.append(jnp.where(valid, a, 0.0))
            right[j].append(jnp.where(valid, b, 0.0))
            tail = got[k, 56:64, :].astype(F32)
            thin[j] = thin[j] + jnp.where(valid, tail, 0.0)
            total = total + tail
        parts = spread(row_tiles)
        left[0].append(parts[0])
        left[1].append(parts[1])
        top = total[6:7]
        diag.append(top + pltpu.roll(top, 64, 1) + total[7:8])
    lane = iota((1, 128), 1)
    inv = jnp.concatenate(
        [
            jnp.where(lane < 64, diag[2 * m], pltpu.roll(diag[2 * m + 1], 64, 1))
            for m in range(4)
        ],
        axis=1,
    )
    inv = 1.0 / inv
    off = jnp.concatenate(
        [
            got[:, 24 + 8 * m : 32 + 8 * m, :].astype(F32).reshape(TILE, 128).astype(BF16)
            for m in range(4)
        ],
        axis=1,
    )

    def times(x):
        high = x.astype(BF16)
        low = (x - high.astype(F32)).astype(BF16)
        both = dot(jnp.concatenate([high, low], axis=0), off, (1, 0))
        return (both[:128] + both[128:]) * inv

    v = jnp.concatenate(left[0] + left[1], axis=0) * inv
    y = v - times(v)
    z = y + times(y)
    lower = 2.0 * y - z + times(z)
    for k in range(2 * N):
        lower_ref[k] = lower[8 * k : 8 * k + 8]
    lower_ref[2 * N] = jnp.zeros((8, TILE), F32)
    right_ref[2 * N] = jnp.zeros((8, TILE), F32)
    for j in range(N):
        parts = spread(right[j])
        right_ref[2 * j] = parts[0]
        right_ref[2 * j + 1] = parts[1]
        tail_ref[j] = thin[j]
    tail_ref[N] = zero
    rows = []
    for half in range(2):
        for s in range(2):
            for r in range(N):
                i = inverse[2 * r + s]
                rows.append(lower_ref[jnp.where(i < N, half * N + i, 2 * N)])
    cols = []
    for k in range(2 * N):
        j = inverse[k]
        for half in range(2):
            cols.append(right_ref[jnp.where(j < N, 2 * j + half, 2 * N)])
    core = dot(
        jnp.concatenate(rows, axis=0).astype(BF16), jnp.concatenate(cols, axis=0).astype(BF16), (1, 1)
    )
    core = core.astype(BF16).astype(F32)
    group = iota((64, 128), 1) // 16
    for k in range(2 * N):
        c, h = k // 2, k % 2
        total = jnp.zeros((64, 128), F32)
        for combo in range(4):
            x = core[64 * combo : 64 * combo + 64, 128 * (k // 8) : 128 * (k // 8) + 128]
            shift = (16 * combo - 16 * (k % 8)) % 128
            total = jnp.where(group == combo, pltpu.roll(x, shift, 1) if shift else x, total)
        j = inverse[k]
        tail = tail_ref[j]
        for r in range(N):
            i0 = inverse[2 * r]
            i1 = inverse[2 * r + 1]
            at0 = jnp.where((i0 < N) & (j < N), i0 * N + j, 64)
            at1 = jnp.where((i1 < N) & (j < N), i1 * N + j, 64)
            send[(h * N + r) * N + c] = jnp.concatenate(
                [t0[at0], t0[at1], g0[at0] + g1[at1], tail, total[8 * r : 8 * r + 8]], axis=0
            ).astype(BF16)


def finish(blocks, col_in, out):
    lefts, rights = [], []
    for f in range(2):
        for side, into in ((0, lefts), (1, rights)):
            lanes = []
            for m in range(4):
                c = 2 * m + side
                lanes.append(
                    jnp.concatenate(
                        [blocks[f * 64 + g * N + c, 0:24, :].astype(F32) for g in range(N)], axis=0
                    )
                )
            into.append(jnp.concatenate(lanes, axis=1))
    left = jnp.concatenate(lefts, axis=0)
    row = iota(left.shape, 0) % 24
    of_slot = (
        (row < 8) | (row >= 20),
        (row >= 8) & (row < 20),
    )
    group = iota((64, 128), 1) // 16
    updates = [[], []]
    mixed = []
    for f in range(2):
        parts = [
            jnp.concatenate(
                [blocks[f * 64 + g * N + c, 32:40, :].astype(F32) for g in range(N)], axis=0
            )
            for c in range(N)
        ]
        for s in range(2):
            halves = []
            for half in range(2):
                total = jnp.zeros((64, 128), F32)
                combo = 2 * half + s
                for c in range(N):
                    shift = (16 * c - 16 * combo) % 128
                    x = pltpu.roll(parts[c], shift, 1) if shift else parts[c]
                    total = jnp.where(group == c, x, total)
                halves.append(total)
            core = jnp.concatenate(halves, axis=0).astype(BF16)
            col_u = spread(
                [
                    col_in[(f * N + c) * 128 + 64 * s : (f * N + c) * 128 + 64 * s + 64, :].astype(F32)
                    for c in range(N)
                ]
            )
            col_u = jnp.concatenate(col_u, axis=0).astype(BF16)
            updates[s].append(-dot(core, col_u, (0, 0)))
        for c in range(N):
            mixed += spread([blocks[f * 64 + g * N + c, 24:32, :].astype(F32) for g in range(N)])
    k = iota((TILE, TILE), 0)
    target = 64 * ((k // 8) % 8) + 8 * (k // 64) + k % 8
    order = (target == iota((TILE, TILE), 1)).astype(BF16)
    row_v = dot(jnp.concatenate(mixed, axis=0).astype(BF16), order, (1, 0))
    right = jnp.concatenate(rights + [row_v], axis=0).astype(BF16)
    for s in range(2):
        both = jnp.concatenate([jnp.where(of_slot[s], left, 0.0)] + updates[s], axis=0).astype(BF16)
        out[s] = dot(both, right, (0, 0)).astype(BF16)


def exchange(x, axes):
    return lax.all_to_all(x, axes, split_axis=0, concat_axis=0, tiled=True)


def collect(x, axes):
    return lax.all_gather(x, axes, axis=0, tiled=True)


def shards(
    pivot, col_ut, col_vt, col_rank, row_ut, row_vt, row_rank, cb_ut, cb_vt, cb_rank, parent_map
):
    sds = jax.ShapeDtypeStruct
    send, col_u = call(
        pack,
        (sds((64, 64, 128), BF16), sds((64, 128), BF16)),
        (
            pivot[0],
            col_ut[0, 0].T,
            col_vt[0, 0].T,
            row_ut[0, 0].T,
            row_vt[0, 0].T,
            cb_ut[0, 0, 0],
            cb_vt[0, 0, 0],
            col_rank,
            row_rank,
            cb_rank,
        ),
        (VMEM,) * 10,
    )
    got = exchange(send, ("row", "col"))
    col_rows = collect(col_u, "row")
    (col_slots,) = call(
        slots,
        (sds((128, 128), BF16),),
        (col_rows.reshape(N, 64, 128), parent_map),
        (VMEM, SMEM),
        (SMEM((2 * N,), jnp.int32),),
    )
    (send_f,) = call(
        route,
        (sds((128, 40, 128), BF16),),
        (got, parent_map),
        (VMEM, SMEM),
        (SMEM((2 * N,), jnp.int32),)
        + (VMEM((65, 8, 128), F32),) * 3
        + (VMEM((2 * N + 1, 8, TILE), F32),) * 2
        + (VMEM((N + 1, 8, 128), F32),),
    )
    blocks = exchange(send_f, ("side", "row", "col"))
    col_in = collect(col_slots, ("side", "col"))
    (out,) = call(finish, (sds((2, TILE, TILE), BF16),), (blocks, col_in), (VMEM,) * 2)
    return out[None, :, None]


def solution(mesh):
    front = ("pair", "side")
    split = Mesh(mesh.devices.reshape(4, 2, N, N), ("pair", "side", "row", "col"))
    placed = (
        P(front, ("row", "col"), None),
        P(front, "row", None, "col"),
        P(front, "row", None, "col"),
        P(front, "row"),
        P(front, "col", None, "row"),
        P(front, "col", None, "row"),
        P(front, "col"),
        P(front, "row", "col", None, None),
        P(front, "row", "col", None, None),
        P(front, "row", "col"),
        P(front, None),
    )

    return jax.shard_map(
        shards,
        mesh=split,
        in_specs=placed,
        out_specs=P(front, "row", "col", None, None),
        check_vma=False,
    )
```

time: 165 us -> 143 us (0.87)
  waiting for transfers between devices: 23.7 us -> 0.01 us
  blocking collectives: 101 us -> 118 us
  starting transfers between devices: 16.2 us -> 8.19 us
  local copies, waits for them, and re-layouts: 5.71 us -> 1.08 us
  Pallas kernels: 15.7 us -> 12.6 us
    all_gather x0 -> x2, blocking collectives: none -> 75.1 us  [collect(): return lax.all_gather(x, axes, axis=0, tiled=True)]
    all_to_all x4 -> x1, blocking collectives: 101 us -> 43.1 us  [exchange(): return lax.all_to_all(x, axes, split_axis=0, concat_axis=0, tiled=True)]
    all_to_all x3 -> x1, waiting for transfers between devices: 23.7 us -> 0.01 us  [exchange(): return lax.all_to_all(x, axes, split_axis=0, concat_axis=0, tiled=True)]
    all_to_all x3 -> x1, starting transfers between devices: 16.2 us -> 8.19 us  [exchange(): return lax.all_to_all(x, axes, split_axis=0, concat_axis=0, tiled=True)]
    unnamed x12 -> x4, local copies, waits for them, and re-layouts: 5.71 us -> 1.08 us
    pallas_call x5 -> x4, Pallas kernels: 15.7 us -> 12.6 us  [call(): pl.pallas_call(body, out_shape=outs, in_specs=[pl.BlockSpec(memory_space=...]
  transfers between devices with their start and end apart: 3 -> 1, of which waited for: 3 -> 0; matrix products, arithmetic and copies ran while one was open for 0% -> 0% of each run, Pallas kernels for 6% -> 1%
where the time goes in v2:
time: 143 us; the launch traced here: 142 us
  blocking collectives  118 us (83%)
  Pallas kernels  12.6 us (9%)
  starting transfers between devices  8.19 us (6%)
  between operations  1.96 us (1%)
    all_gather x2, blocking collectives, collect(): return lax.all_gather(x, axes, axis=0, tiled=True)  75.1 us
    all_to_all x1, blocking collectives, exchange(): return lax.all_to_all(x, axes, split_axis=0, concat_axis=0, tiled=True)  43.1 us
    pallas_call x4, Pallas kernels, call(): pl.pallas_call(body, out_shape=outs, in_specs=[pl.BlockSpec(memory_space=...  12.6 us
    all_to_all x1, starting transfers between devices, exchange(): return lax.all_to_all(x, axes, split_axis=0, concat_axis=0, tiled=True)  8.19 us
  transfers between devices with their start and end apart: 1, of which 0 were waited for; matrix products, arithmetic and copies ran while one was open for 0% of the time, Pallas kernels for 1%

profile of v2, /device:TPU:1, one launch (start us, length us, event | category | flops | bytes accessed | tf_op | source)
XLA Modules:
  0.0 142.1 jit_solution(5883169789784425626)
XLA Ops:
  1.9 2.6 %shard_map.109 = (bf16[64,64,128]{2,1,0:T(8,128)(2,1)}, bf16[64,128]{1,0:T(8,128)(2,1)}) custom-call(f32[8,512]{1,0:T(8,128)} %bitcast.22, bf16[64,96]{1,0:T(8,128)(2,1)} %bitcast.23, bf16[64,96]{1,0:T(8,128)(2,1)} %bitcast.24, bf16[64,96]{1,0:T(8,128)(2,1)} %bitcast.25, bf16[64,96]{1,0:T(8,128)(2,1)} %bitcast.26, bf16[96,512]{1,0:T(8,128)(2,1)} %bitcast.20, ...), custom_call_target="tpu_custom_call" | custom-call | tf_op jit(solution)/shard_map/pallas_call | solution.py:29
  4.6 43.1 %all_to_all.10.got = bf16[64,64,128]{2,1,0:T(8,128)(2,1)} all-to-all(bf16[64,64,128]{2,1,0:T(8,128)(2,1)} %get-tuple-element.7), channel_id=1, replica_groups=mesh['pair'=4,'side'=2,'row'=8,'col'=8] {'row','col'}, dimensions={0} | all-to-all | bytes 2097152 | tf_op jit(solution)/shard_map/all_to_all | solution.py:307
  47.7 4.1 %shard_map.110 = bf16[128,40,128]{2,1,0:T(8,128)(2,1)} custom-call(bf16[64,64,128]{2,1,0:T(8,128)(2,1)} %all_to_all.10.got, s32[1,8]{1,0:T(1,128)} %mapping.3), custom_call_target="tpu_custom_call" | custom-call | tf_op jit(solution)/shard_map/pallas_call | solution.py:29
  51.7 0.0 copy-start.1
  51.7 8.2 %all-to-all-start.1 = ((bf16[128,40,128]{2,1,0:T(8,128)(2,1)}), bf16[128,40,128]{2,1,0:T(8,128)(2,1)S(1)}, u32[]{:S(2)}, u32[]{:S(2)}) async-start(bf16[128,40,128]{2,1,0:T(8,128)(2,1)} %shard_map.110), calls=%async_computation.1 | async-start | bytes 2621440 | tf_op jit(solution)/shard_map/all_to_all | solution.py:307
  59.9 0.0 copy-done.1
  60.0 46.3 %all_gather.6 = bf16[512,128]{1,0:T(8,128)(2,1)} all-gather(bf16[64,128]{1,0:T(8,128)(2,1)S(1)} %copy-done.1), channel_id=1, replica_groups=mesh['pair'=4,'side'=2,'row'=8,'col'=8] {'row'}, dimensions={0}, use_global_device_ids=true | all-gather | bytes 147456 | tf_op jit(solution)/shard_map/all_gather | solution.py:311
  106.3 1.6 %shard_map.111 = bf16[128,128]{1,0:T(8,128)(2,1)} custom-call(bf16[8,64,128]{2,1,0:T(8,128)(2,1)} %bitcast.19, s32[1,8]{1,0:T(1,128)} %mapping.3), custom_call_target="tpu_custom_call" | custom-call | tf_op jit(solution)/shard_map/pallas_call | solution.py:29
  107.9 28.8 %all_gather.7.col_in = bf16[2048,128]{1,0:T(8,128)(2,1)} all-gather(bf16[128,128]{1,0:T(8,128)(2,1)} %shard_map.111), channel_id=1, replica_groups=mesh['pair'=4,'side'=2,'row'=8,'col'=8] {'side','col'}, dimensions={0}, use_global_device_ids=true | all-gather | bytes 557056 | tf_op jit(solution)/shard_map/all_gather | solution.py:311
  136.7 0.0 all-to-all-done.1.blocks
  136.7 0.0 copy-start
  136.7 1.1 copy-done
  137.7 4.4 %shard_map.112 = bf16[2,512,512]{2,1,0:T(8,128)(2,1)} custom-call(bf16[128,40,128]{2,1,0:T(8,128)(2,1)} %copy-done, bf16[2048,128]{1,0:T(8,128)(2,1)} %all_gather.7.col_in), custom_call_target="tpu_custom_call" | custom-call | tf_op jit(solution)/shard_map/pallas_call | solution.py:29
Async XLA Ops:
  51.7 8.2 %copy-start.1 = (bf16[64,128]{1,0:T(8,128)(2,1)S(1)}, bf16[64,128]{1,0:T(8,128)(2,1)}, u32[]{:S(2)}) copy-start(bf16[64,128]{1,0:T(8,128)(2,1)} %get-tuple-element.8) | copy-start | bytes 49156
  51.7 84.9 %all-to-all-start.1 = ((bf16[128,40,128]{2,1,0:T(8,128)(2,1)}), bf16[128,40,128]{2,1,0:T(8,128)(2,1)S(1)}, u32[]{:S(2)}, u32[]{:S(2)}) async-start(bf16[128,40,128]{2,1,0:T(8,128)(2,1)} %shard_map.110), calls=%async_computation.1 | async-start | bytes 2621440 | tf_op jit(solution)/shard_map/all_to_all | solution.py:307
  136.7 1.1 copy-start

commit v3 on v2

--- a/solution.py
+++ b/solution.py
@@ -4,7 +4,6 @@
 from jax.experimental import pallas as pl
 from jax.experimental.pallas import tpu as pltpu
 from jax.sharding import Mesh, PartitionSpec as P
-
 
 F32 = jnp.float32
 BF16 = jnp.bfloat16
@@ -25,14 +24,17 @@
     )
 
 
-def call(body, outs, args, specs, scratch=()):
-    return pl.pallas_call(
+def call(body, outs, args, specs, scratch=(), name=None):
+    kernel = pl.pallas_call(
         body,
         out_shape=outs,
         in_specs=[pl.BlockSpec(memory_space=s) for s in specs],
         out_specs=[pl.BlockSpec(memory_space=VMEM) for _ in outs],
         scratch_shapes=scratch,
-    )(*args)
+        name=name,
+    )
+    with jax.named_scope("do_" + name):
+        return kernel(*args)
 
 
 def fill_inverse(mapping, inverse):
@@ -49,7 +51,7 @@
     return ((t < 6) & (level == 12 * (row // 8) + offset + t)).astype(BF16)
 
 
-def pack(piv, cu, cv, ru, rv, cbu, cbv, rank_c, rank_r, rank_b, send, col_u):
+def pack(piv, cu, cv, ru, rv, cbu, cbv, rank_c, rank_r, rank_b, send):
     level = iota((64, RANK), 1)
     even = onehot(0)
     odd = onehot(6)
@@ -58,19 +60,20 @@
         x = jnp.where(level < rank, ref[...].astype(F32), 0.0).astype(BF16)
         return jnp.concatenate([dot(even, x, (1, 1)), dot(odd, x, (1, 1))], axis=1)
 
-    col_u[...] = panel(cu, rank_c[...]).astype(BF16)
-    col_v = panel(cv, rank_c[...])
-    row_u = panel(ru, rank_r[...])
-    row_v = panel(rv, rank_r[...]).astype(BF16)
+    col_u = panel(cu, rank_c[0, 0]).astype(BF16)
+    col_v = panel(cv, rank_c[0, 0])
+    row_u = panel(ru, rank_r[0, 0])
+    row_v = panel(rv, rank_r[0, 0]).astype(BF16)
     r = lax.axis_index("row")
-    q = r * N + lax.axis_index("col")
+    c0 = lax.axis_index("col")
+    q = r * N + c0
     full = piv[...]
     on_diag = iota((8, TILE), 1) == 8 * q + iota((8, TILE), 0)
     diag = jnp.sum(jnp.where(on_diag, full, 0.0), axis=1, keepdims=True)
     off = jnp.where(on_diag, 0.0, full)
     lane = iota((8, 128), 1)
     sub = iota((8, 128), 0)
-    here = 8 * lax.axis_index("col") + sub
+    here = 8 * c0 + sub
     high = diag.astype(BF16).astype(F32)
     rest = diag - high
     mid = rest.astype(BF16).astype(F32)
@@ -90,13 +93,20 @@
     ]
     from_lane = iota((128, 128), 0)
     to_lane = iota((128, 128), 1)
-    same = (from_lane // 64 == to_lane // 64) & ((to_lane // 8) % 8 == r)
+    col_group = (c0 + jnp.where(c0 == r, 1, 0)) % N
+    same = from_lane // 64 == to_lane // 64
+    to_group = (to_lane // 8) % 8
     thin = []
     for g in range(N):
         move = same & (from_lane % 64 == 8 * g + to_lane % 8)
-        thin.append(dot(row_v, move.astype(BF16), (1, 0)))
+        thin.append(
+            (
+                dot(row_v, (move & (to_group == r)).astype(BF16), (1, 0)),
+                dot(col_u, (move & (to_group == col_group)).astype(BF16), (1, 0)),
+            )
+        )
     for side, ref in enumerate((cbu, cbv)):
-        x = jnp.where(wide < rank_b[0], ref[...].astype(F32), 0.0)
+        x = jnp.where(wide < rank_b[0, 0, 0], ref[...].astype(F32), 0.0)
         narrow = x.astype(BF16)
         x1 = dot(extra[0], narrow, (1, 0))
         x2 = dot(extra[1], narrow, (1, 0))
@@ -105,26 +115,17 @@
             for m in range(4):
                 lanes = slice(128 * m, 128 * m + 128)
                 c = 2 * m + side
+                cols = slice(8 * c, 8 * c + 8)
                 send[g * N + c] = jnp.concatenate(
                     [
                         x[rows, lanes],
                         col_v[rows] + x1[rows, lanes],
-                        row_u[8 * c : 8 * c + 8] + x2[rows, lanes],
+                        row_u[cols] + x2[rows, lanes],
                     ]
                     + pivot
-                    + [thin[g][8 * c : 8 * c + 8] + parts],
+                    + [thin[g][0][cols] + thin[c][1][rows] + parts],
                     axis=0,
                 ).astype(BF16)
-
-
-def slots(got, mapping, send, inverse):
-    fill_inverse(mapping, inverse)
-    here = lax.axis_index("row")
-    for s in range(2):
-        at = inverse[2 * here + s]
-        x = got[jnp.minimum(at, N - 1)].astype(F32)
-        x = jnp.where(at < N, x, jnp.zeros_like(x)).astype(BF16)
-        send[64 * s : 64 * s + 64, :] = x
 
 
 def spread(tiles):
@@ -137,7 +138,7 @@
     return [jnp.concatenate(h, axis=1) for h in halves]
 
 
-def route(got, mapping, send, inverse, t0, g0, g1, lower_ref, right_ref, tail_ref):
+def route(got, mapping, send, inverse, t0, g0, g1, lower_ref, right_ref, row_ref, col_ref):
     fill_inverse(mapping, inverse)
     sub = iota((8, 128), 0)
     valid = sub < 6
@@ -149,9 +150,11 @@
     diag = []
     right = [[] for _ in range(N)]
     thin = [zero] * N
+    group = (iota((8, 128), 1) // 8) % 8
     for i in range(N):
         row_tiles = []
         total = zero
+        thick = zero
         for j in range(N):
             k = i * N + j
             x = got[k, 0:24, :].astype(F32)
@@ -164,8 +167,14 @@
             row_tiles.append(jnp.where(valid, a, 0.0))
             right[j].append(jnp.where(valid, b, 0.0))
             tail = got[k, 56:64, :].astype(F32)
-            thin[j] = thin[j] + jnp.where(valid, tail, 0.0)
+            thin[j] = thin[j] + jnp.where(valid & (group == i), tail, 0.0)
+            if i == j:
+                x = jnp.where(valid & (group == (j + 1) % N), tail, 0.0)
+                thick = thick + pltpu.roll(x, 56 if j == N - 1 else 120, 1)
+            else:
+                thick = thick + jnp.where(valid & (group == j), tail, 0.0)
             total = total + tail
+        col_ref[i] = thick
         parts = spread(row_tiles)
         left[0].append(parts[0])
         left[1].append(parts[1])
@@ -206,8 +215,9 @@
         parts = spread(right[j])
         right_ref[2 * j] = parts[0]
         right_ref[2 * j + 1] = parts[1]
-        tail_ref[j] = thin[j]
-    tail_ref[N] = zero
+        row_ref[j] = thin[j]
+    row_ref[N] = zero
+    col_ref[N] = zero
     rows = []
     for half in range(2):
         for s in range(2):
@@ -232,18 +242,30 @@
             shift = (16 * combo - 16 * (k % 8)) % 128
             total = jnp.where(group == combo, pltpu.roll(x, shift, 1) if shift else x, total)
         j = inverse[k]
-        tail = tail_ref[j]
+        tail = row_ref[j]
         for r in range(N):
+            part = total[8 * r : 8 * r + 8]
             i0 = inverse[2 * r]
             i1 = inverse[2 * r + 1]
             at0 = jnp.where((i0 < N) & (j < N), i0 * N + j, 64)
             at1 = jnp.where((i1 < N) & (j < N), i1 * N + j, 64)
             send[(h * N + r) * N + c] = jnp.concatenate(
-                [t0[at0], t0[at1], g0[at0] + g1[at1], tail, total[8 * r : 8 * r + 8]], axis=0
+                [
+                    t0[at0],
+                    t0[at1],
+                    g0[at0] + g1[at1],
+                    jnp.where(valid, tail, pltpu.roll(part, 6, 0)),
+                    jnp.where(valid, col_ref[i0], pltpu.roll(part, 4, 0)),
+                    jnp.where(valid, col_ref[i1], pltpu.roll(part, 2, 0)),
+                ],
+                axis=0,
             ).astype(BF16)
 
 
-def finish(blocks, col_in, out):
+def finish(blocks, out):
+    def tile(f, g, c, at):
+        return blocks[f * 64 + g * N + c, 8 * at : 8 * at + 8, :].astype(F32)
+
     lefts, rights = [], []
     for f in range(2):
         for side, into in ((0, lefts), (1, rights)):
@@ -262,16 +284,19 @@
         (row < 8) | (row >= 20),
         (row >= 8) & (row < 20),
     )
+    sub = iota((8, 128), 0)
     group = iota((64, 128), 1) // 16
     updates = [[], []]
     mixed = []
     for f in range(2):
-        parts = [
-            jnp.concatenate(
-                [blocks[f * 64 + g * N + c, 32:40, :].astype(F32) for g in range(N)], axis=0
-            )
-            for c in range(N)
-        ]
+        parts = []
+        for c in range(N):
+            rows = []
+            for g in range(N):
+                x = jnp.where(sub < 4, pltpu.roll(tile(f, g, c, 4), 4, 0), pltpu.roll(tile(f, g, c, 5), 6, 0))
+                x = jnp.where(sub < 2, pltpu.roll(tile(f, g, c, 3), 2, 0), x)
+                rows.append(jnp.where(sub < 6, x, 0.0))
+            parts.append(jnp.concatenate(rows, axis=0))
         for s in range(2):
             halves = []
             for half in range(2):
@@ -283,41 +308,38 @@
                     total = jnp.where(group == c, x, total)
                 halves.append(total)
             core = jnp.concatenate(halves, axis=0).astype(BF16)
-            col_u = spread(
-                [
-                    col_in[(f * N + c) * 128 + 64 * s : (f * N + c) * 128 + 64 * s + 64, :].astype(F32)
-                    for c in range(N)
-                ]
-            )
-            col_u = jnp.concatenate(col_u, axis=0).astype(BF16)
+            col_u = [[], []]
+            for g in range(N):
+                for half, x in enumerate(spread([tile(f, g, c, 4 + s) for c in range(N)])):
+                    col_u[half].append(x)
+            col_u = jnp.concatenate(col_u[0] + col_u[1], axis=0).astype(BF16)
             updates[s].append(-dot(core, col_u, (0, 0)))
         for c in range(N):
-            mixed += spread([blocks[f * 64 + g * N + c, 24:32, :].astype(F32) for g in range(N)])
+            mixed += spread([tile(f, g, c, 3) for g in range(N)])
     k = iota((TILE, TILE), 0)
     target = 64 * ((k // 8) % 8) + 8 * (k // 64) + k % 8
     order = (target == iota((TILE, TILE), 1)).astype(BF16)
-    row_v = dot(jnp.concatenate(mixed, axis=0).astype(BF16), order, (1, 0))
-    right = jnp.concatenate(rights + [row_v], axis=0).astype(BF16)
+    panels = jnp.concatenate(mixed + updates[0] + updates[1], axis=0).astype(BF16)
+    panels = dot(panels, order, (1, 0))
+    right = jnp.concatenate(rights + [panels[:256]], axis=0).astype(BF16)
     for s in range(2):
-        both = jnp.concatenate([jnp.where(of_slot[s], left, 0.0)] + updates[s], axis=0).astype(BF16)
+        update = panels[256 + 256 * s : 512 + 256 * s]
+        both = jnp.concatenate([jnp.where(of_slot[s], left, 0.0), update], axis=0).astype(BF16)
         out[s] = dot(both, right, (0, 0)).astype(BF16)
 
 
-def exchange(x, axes):
-    return lax.all_to_all(x, axes, split_axis=0, concat_axis=0, tiled=True)
-
-
-def collect(x, axes):
-    return lax.all_gather(x, axes, axis=0, tiled=True)
+def exchange(x, axes, name):
+    with jax.named_scope(name):
+        return lax.all_to_all(x, axes, split_axis=0, concat_axis=0, tiled=True)
 
 
 def shards(
     pivot, col_ut, col_vt, col_rank, row_ut, row_vt, row_rank, cb_ut, cb_vt, cb_rank, parent_map
 ):
     sds = jax.ShapeDtypeStruct
-    send, col_u = call(
+    (send,) = call(
         pack,
-        (sds((64, 64, 128), BF16), sds((64, 128), BF16)),
+        (sds((64, 64, 128), BF16),),
         (
             pivot[0],
             col_ut[0, 0].T,
@@ -330,30 +352,23 @@
             row_rank,
             cb_rank,
         ),
-        (VMEM,) * 10,
-    )
-    got = exchange(send, ("row", "col"))
-    col_rows = collect(col_u, "row")
-    (col_slots,) = call(
-        slots,
-        (sds((128, 128), BF16),),
-        (col_rows.reshape(N, 64, 128), parent_map),
-        (VMEM, SMEM),
-        (SMEM((2 * N,), jnp.int32),),
-    )
-    (send_f,) = call(
+        (VMEM,) * 7 + (SMEM,) * 3,
+        name="pack",
+    )
+    got = exchange(send, ("row", "col"), "scatter")
+    (send,) = call(
         route,
-        (sds((128, 40, 128), BF16),),
+        (sds((128, 48, 128), BF16),),
         (got, parent_map),
         (VMEM, SMEM),
         (SMEM((2 * N,), jnp.int32),)
         + (VMEM((65, 8, 128), F32),) * 3
         + (VMEM((2 * N + 1, 8, TILE), F32),) * 2
-        + (VMEM((N + 1, 8, 128), F32),),
-    )
-    blocks = exchange(send_f, ("side", "row", "col"))
-    col_in = collect(col_slots, ("side", "col"))
-    (out,) = call(finish, (sds((2, TILE, TILE), BF16),), (blocks, col_in), (VMEM,) * 2)
+        + (VMEM((N + 1, 8, 128), F32),) * 2,
+        name="route",
+    )
+    blocks = exchange(send, ("side", "row", "col"), "gather")
+    (out,) = call(finish, (sds((2, TILE, TILE), BF16),), (blocks,), (VMEM,), name="finish")
     return out[None, :, None]
 
 

time: 143 us -> 106 us (0.74)
  blocking collectives: 118 us -> 91.4 us
  starting transfers between devices: 8.19 us -> 0 us
    all_gather x2 -> x0, blocking collectives: 75.1 us -> none  [collect(): return lax.all_gather(x, axes, axis=0, tiled=True)]
    all_to_all x1 -> x2, blocking collectives: 43.1 us -> 91.4 us  [exchange(): return lax.all_to_all(x, axes, split_axis=0, concat_axis=0, tiled=True)]
    all_to_all x1 -> x0, starting transfers between devices: 8.19 us -> none  [exchange(): return lax.all_to_all(x, axes, split_axis=0, concat_axis=0, tiled=True)]
    pallas_call x4 -> x3, Pallas kernels: 12.6 us -> 11.5 us  [call(): return kernel(*args)]
  transfers between devices with their start and end apart: 1 -> 0, of which waited for: 0 -> 0; matrix products, arithmetic and copies ran while one was open for 0% -> 0% of each run, Pallas kernels for 1% -> 0%
where the time goes in v3:
time: 106 us; the launch traced here: 105 us
  blocking collectives  91.4 us (86%)
  Pallas kernels  11.5 us (11%)
  between operations  1.94 us (2%)
    all_to_all x2, blocking collectives, exchange(): return lax.all_to_all(x, axes, split_axis=0, concat_axis=0, tiled=True)  91.4 us
    pallas_call x3, Pallas kernels, call(): return kernel(*args)  11.5 us

profile of v3, /device:TPU:1, one launch (start us, length us, event | category | flops | bytes accessed | tf_op | source)
XLA Modules:
  0.0 104.8 jit_solution(7137627479692393875)
XLA Ops:
  1.9 2.6 %pack.1 = bf16[64,64,128]{2,1,0:T(8,128)(2,1)} custom-call(f32[8,512]{1,0:T(8,128)} %bitcast.20, bf16[64,96]{1,0:T(8,128)(2,1)} %bitcast.21, bf16[64,96]{1,0:T(8,128)(2,1)} %bitcast.22, bf16[64,96]{1,0:T(8,128)(2,1)} %bitcast.23, bf16[64,96]{1,0:T(8,128)(2,1)} %bitcast.24, bf16[96,512]{1,0:T(8,128)(2,1)} %bitcast.18, bf16[96,512]{1,0:T(8,128)(2,1)} %bitcast.19, ...), custom_call_target="tpu_custom_call" | custom-call | tf_op jit(solution)/shard_map/do_pack/pack/pallas_call | solution.py:37
  4.5 43.1 %all_to_all.10.got = bf16[64,64,128]{2,1,0:T(8,128)(2,1)} all-to-all(bf16[64,64,128]{2,1,0:T(8,128)(2,1)} %pack.1), channel_id=1, replica_groups=mesh['pair'=4,'side'=2,'row'=8,'col'=8] {'row','col'}, dimensions={0} | all-to-all | bytes 2097152 | tf_op jit(solution)/shard_map/scatter/all_to_all | solution.py:333
  47.6 4.4 %route.1 = bf16[128,48,128]{2,1,0:T(8,128)(2,1)} custom-call(bf16[64,64,128]{2,1,0:T(8,128)(2,1)} %all_to_all.10.got, s32[1,8]{1,0:T(1,128)} %mapping.1), custom_call_target="tpu_custom_call" | custom-call | tf_op jit(solution)/shard_map/do_route/route/pallas_call | solution.py:37
  52.0 48.3 %all_to_all.11.blocks = bf16[128,48,128]{2,1,0:T(8,128)(2,1)} all-to-all(bf16[128,48,128]{2,1,0:T(8,128)(2,1)} %route.1), channel_id=1, replica_groups=mesh['pair'=4,'side'=2,'row'=8,'col'=8] {'side','row','col'}, dimensions={0} | all-to-all | bytes 3145728 | tf_op jit(solution)/shard_map/gather/all_to_all | solution.py:333
  100.3 4.5 %finish.1 = bf16[2,512,512]{2,1,0:T(8,128)(2,1)} custom-call(bf16[128,48,128]{2,1,0:T(8,128)(2,1)} %all_to_all.11.blocks), custom_call_target="tpu_custom_call" | custom-call | tf_op jit(solution)/shard_map/do_finish/finish/pallas_call | solution.py:37

commit v4 on v3

--- a/solution.py
+++ b/solution.py
@@ -339,7 +339,7 @@
     sds = jax.ShapeDtypeStruct
     (send,) = call(
         pack,
-        (sds((64, 64, 128), BF16),),
+        (VMEM((64, 64, 128), BF16),),
         (
             pivot[0],
             col_ut[0, 0].T,
@@ -358,7 +358,7 @@
     got = exchange(send, ("row", "col"), "scatter")
     (send,) = call(
         route,
-        (sds((128, 48, 128), BF16),),
+        (VMEM((128, 48, 128), BF16),),
         (got, parent_map),
         (VMEM, SMEM),
         (SMEM((2 * N,), jnp.int32),)

time: 106 us -> 103 us (0.972)
  Pallas kernels: 11.5 us -> 9.11 us
    pallas_call x3, Pallas kernels: 11.5 us -> 9.11 us  [call(): return kernel(*args)]
where the time goes in v4:
time: 103 us; the launch traced here: 102 us
  blocking collectives  91 us (88%)
  Pallas kernels  9.11 us (9%)
  between operations  1.96 us (2%)
    all_to_all x2, blocking collectives, exchange(): return lax.all_to_all(x, axes, split_axis=0, concat_axis=0, tiled=True)  91 us
    pallas_call x3, Pallas kernels, call(): return kernel(*args)  9.11 us

profile of v4, /device:TPU:1, one launch (start us, length us, event | category | flops | bytes accessed | tf_op | source)
XLA Modules:
  0.0 102.0 jit_solution(265350662078740083)
XLA Ops:
  1.9 1.6 %pack.1 = bf16[64,64,128]{2,1,0:T(8,128)(2,1)S(1)} custom-call(f32[8,512]{1,0:T(8,128)} %bitcast.20, bf16[64,96]{1,0:T(8,128)(2,1)} %bitcast.21, bf16[64,96]{1,0:T(8,128)(2,1)} %bitcast.22, bf16[64,96]{1,0:T(8,128)(2,1)} %bitcast.23, bf16[64,96]{1,0:T(8,128)(2,1)} %bitcast.24, bf16[96,512]{1,0:T(8,128)(2,1)} %bitcast.18, bf16[96,512]{1,0:T(8,128)(2,1)} %bitcast.19, ...), custom_call_target="tpu_custom_call" | custom-call | tf_op jit(solution)/shard_map/do_pack/pack/pallas_call | solution.py:37
  3.6 42.9 %all_to_all.10.got = bf16[64,64,128]{2,1,0:T(8,128)(2,1)} all-to-all(bf16[64,64,128]{2,1,0:T(8,128)(2,1)S(1)} %pack.1), channel_id=1, replica_groups=mesh['pair'=4,'side'=2,'row'=8,'col'=8] {'row','col'}, dimensions={0} | all-to-all | bytes 2097152 | tf_op jit(solution)/shard_map/scatter/all_to_all | solution.py:333
  46.5 3.0 %route.1 = bf16[128,48,128]{2,1,0:T(8,128)(2,1)S(1)} custom-call(bf16[64,64,128]{2,1,0:T(8,128)(2,1)} %all_to_all.10.got, s32[1,8]{1,0:T(1,128)} %mapping.1), custom_call_target="tpu_custom_call" | custom-call | tf_op jit(solution)/shard_map/do_route/route/pallas_call | solution.py:37
  49.4 48.1 %all_to_all.11.blocks = bf16[128,48,128]{2,1,0:T(8,128)(2,1)} all-to-all(bf16[128,48,128]{2,1,0:T(8,128)(2,1)S(1)} %route.1), channel_id=1, replica_groups=mesh['pair'=4,'side'=2,'row'=8,'col'=8] {'side','row','col'}, dimensions={0} | all-to-all | bytes 3145728 | tf_op jit(solution)/shard_map/gather/all_to_all | solution.py:333
  97.5 4.5 %finish.1 = bf16[2,512,512]{2,1,0:T(8,128)(2,1)} custom-call(bf16[128,48,128]{2,1,0:T(8,128)(2,1)} %all_to_all.11.blocks), custom_call_target="tpu_custom_call" | custom-call | tf_op jit(solution)/shard_map/do_finish/finish/pallas_call | solution.py:37

commit v5 on v4

--- a/solution.py
+++ b/solution.py
@@ -24,12 +24,12 @@
     )
 
 
-def call(body, outs, args, specs, scratch=(), name=None):
+def call(body, outs, args, specs, scratch=(), name=None, into=VMEM):
     kernel = pl.pallas_call(
         body,
         out_shape=outs,
         in_specs=[pl.BlockSpec(memory_space=s) for s in specs],
-        out_specs=[pl.BlockSpec(memory_space=VMEM) for _ in outs],
+        out_specs=[pl.BlockSpec(memory_space=into) for _ in outs],
         scratch_shapes=scratch,
         name=name,
     )
@@ -64,25 +64,25 @@
     col_v = panel(cv, rank_c[0, 0])
     row_u = panel(ru, rank_r[0, 0])
     row_v = panel(rv, rank_r[0, 0]).astype(BF16)
-    r = lax.axis_index("row")
-    c0 = lax.axis_index("col")
-    q = r * N + c0
+    first_half = iota((64, 128), 1) < 64
+    col_v = (
+        jnp.where(first_half, col_v, 0.0),
+        jnp.where(first_half, pltpu.roll(col_v, 64, 1), 0.0),
+    )
+    q = lax.axis_index("row") * N + lax.axis_index("col")
     full = piv[...]
     on_diag = iota((8, TILE), 1) == 8 * q + iota((8, TILE), 0)
     diag = jnp.sum(jnp.where(on_diag, full, 0.0), axis=1, keepdims=True)
     off = jnp.where(on_diag, 0.0, full)
-    lane = iota((8, 128), 1)
-    sub = iota((8, 128), 0)
-    here = 8 * c0 + sub
     high = diag.astype(BF16).astype(F32)
     rest = diag - high
     mid = rest.astype(BF16).astype(F32)
-    low = rest - mid
-    zero = jnp.zeros((8, 128), F32)
-    first = jnp.where(lane == here, high, jnp.where(lane == 64 + here, mid, zero))
-    first = jnp.sum(first, axis=0, keepdims=True)
-    last = jnp.sum(jnp.where(lane == here, low, zero), axis=0, keepdims=True)
-    parts = jnp.where(sub == 6, first, jnp.where(sub == 7, last, zero))
+    lane = iota((8, 128), 1)
+    sub = iota((8, 128), 0)
+    parts = jnp.zeros((8, 128), F32)
+    for k, x in enumerate((high, mid, rest - mid)):
+        parts = jnp.where(lane == 96 + 8 * k + sub, x, parts)
+    parts = jnp.where(sub == 0, jnp.sum(parts, axis=0, keepdims=True), 0.0)
     pivot = [off[:, 128 * m : 128 * m + 128] for m in range(4)]
     wide = iota((RANK, TILE), 0)
     row = iota((64, RANK), 0)
@@ -92,18 +92,15 @@
         ((t >= 6) & (lev == 64 + 4 * (row // 8) + 2 * e + t - 6)).astype(BF16) for e in range(2)
     ]
     from_lane = iota((128, 128), 0)
-    to_lane = iota((128, 128), 1)
-    col_group = (c0 + jnp.where(c0 == r, 1, 0)) % N
-    same = from_lane // 64 == to_lane // 64
-    to_group = (to_lane // 8) % 8
+    place = iota((128, 128), 1) - 8 * (from_lane // 64) - from_lane % 64
+    inside = from_lane % 64 // 8
     thin = []
     for g in range(N):
-        move = same & (from_lane % 64 == 8 * g + to_lane % 8)
         thin.append(
-            (
-                dot(row_v, (move & (to_group == r)).astype(BF16), (1, 0)),
-                dot(col_u, (move & (to_group == col_group)).astype(BF16), (1, 0)),
-            )
+            [
+                dot(x, ((inside == g) & (place == at - 8 * g)).astype(BF16), (1, 0))
+                for x, at in ((row_v, 64), (col_u, 80))
+            ]
         )
     for side, ref in enumerate((cbu, cbv)):
         x = jnp.where(wide < rank_b[0, 0, 0], ref[...].astype(F32), 0.0)
@@ -119,11 +116,11 @@
                 send[g * N + c] = jnp.concatenate(
                     [
                         x[rows, lanes],
-                        col_v[rows] + x1[rows, lanes],
-                        row_u[cols] + x2[rows, lanes],
-                    ]
-                    + pivot
-                    + [thin[g][0][cols] + thin[c][1][rows] + parts],
+                        row_u[cols] + x1[rows, lanes],
+                        col_v[side][rows] + thin[g][0][cols] + thin[c][1][rows] + parts + x2[rows, lanes],
+                        pivot[2 * side],
+                        pivot[2 * side + 1],
+                    ],
                     axis=0,
                 ).astype(BF16)
 
@@ -138,22 +135,42 @@
     return [jnp.concatenate(h, axis=1) for h in halves]
 
 
-def route(got, mapping, send, inverse, t0, g0, g1, lower_ref, right_ref, row_ref, col_ref):
+def route(
+    got, other, mapping, send, inverse, t0, g0, g1, lower_ref, right_ref, row_ref, col_ref, off_ref
+):
     fill_inverse(mapping, inverse)
+    core_id = lax.axis_index("col") % 2
     sub = iota((8, 128), 0)
+    lane = iota((8, 128), 1)
     valid = sub < 6
     zero = jnp.zeros((8, 128), F32)
     t0[64] = zero
     g0[64] = zero
     g1[64] = zero
-    left = [[], []]
-    diag = []
     right = [[] for _ in range(N)]
     thin = [zero] * N
-    group = (iota((8, 128), 1) // 8) % 8
+    diag = [zero] * 4
+    group = lane // 8
+
+    def move(x, start, to):
+        return pltpu.roll(x, (to - start) % 128, 1) if (to - start) % 128 else x
+
+    def halves(ref, i):
+        x = [jnp.where(valid, ref[i * N + j, 16:24, :].astype(F32), 0.0) for j in range(N)]
+        return jnp.concatenate(
+            [jnp.where(lane < 64, x[2 * m], pltpu.roll(x[2 * m + 1], 64, 1)) for m in range(4)], axis=1
+        )
+
+    def columns(ref):
+        return jnp.concatenate(
+            [
+                ref[:, 24 + 8 * m : 32 + 8 * m, :].astype(F32).reshape(TILE, 128).astype(BF16)
+                for m in range(2)
+            ],
+            axis=1,
+        )
+
     for i in range(N):
-        row_tiles = []
-        total = zero
         thick = zero
         for j in range(N):
             k = i * N + j
@@ -164,38 +181,20 @@
             g1[k] = jnp.where(
                 sub >= 4, 0.0, jnp.where(sub >= 2, pltpu.roll(a, 4, 0), pltpu.roll(b, 2, 0))
             )
-            row_tiles.append(jnp.where(valid, a, 0.0))
-            right[j].append(jnp.where(valid, b, 0.0))
-            tail = got[k, 56:64, :].astype(F32)
-            thin[j] = thin[j] + jnp.where(valid & (group == i), tail, 0.0)
-            if i == j:
-                x = jnp.where(valid & (group == (j + 1) % N), tail, 0.0)
-                thick = thick + pltpu.roll(x, 56 if j == N - 1 else 120, 1)
-            else:
-                thick = thick + jnp.where(valid & (group == j), tail, 0.0)
-            total = total + tail
-        col_ref[i] = thick
-        parts = spread(row_tiles)
-        left[0].append(parts[0])
-        left[1].append(parts[1])
-        top = total[6:7]
-        diag.append(top + pltpu.roll(top, 64, 1) + total[7:8])
-    lane = iota((1, 128), 1)
-    inv = jnp.concatenate(
-        [
-            jnp.where(lane < 64, diag[2 * m], pltpu.roll(diag[2 * m + 1], 64, 1))
-            for m in range(4)
-        ],
-        axis=1,
-    )
-    inv = 1.0 / inv
-    off = jnp.concatenate(
-        [
-            got[:, 24 + 8 * m : 32 + 8 * m, :].astype(F32).reshape(TILE, 128).astype(BF16)
-            for m in range(4)
-        ],
-        axis=1,
-    )
+            right[j].append(jnp.where(valid, a, 0.0))
+            for half in range(2):
+                thin[j] = jnp.where(group == 8 * half + i, move(b, 64 + 8 * half, 64 * half + 8 * i), thin[j])
+                thick = jnp.where(group == 8 * half + j, move(b, 80 + 8 * half, 64 * half + 8 * j), thick)
+            total = b + pltpu.roll(b, 120, 1) + pltpu.roll(b, 112, 1)
+            to = 64 * (i % 2) + 8 * j
+            diag[i // 2] = jnp.where(group == to // 8, move(total, 96, to), diag[i // 2])
+        col_ref[i] = jnp.where(valid, thick, 0.0)
+    left = [halves(got, i) for i in range(N)]
+    off_ref[core_id] = columns(got)
+    inv = 1.0 / jnp.concatenate([x[0:1] for x in diag], axis=1)
+    left += [halves(other, i) for i in range(N)]
+    off_ref[1 - core_id] = columns(other)
+    off = jnp.concatenate([off_ref[0], off_ref[1]], axis=1)
 
     def times(x):
         high = x.astype(BF16)
@@ -203,7 +202,7 @@
         both = dot(jnp.concatenate([high, low], axis=0), off, (1, 0))
         return (both[:128] + both[128:]) * inv
 
-    v = jnp.concatenate(left[0] + left[1], axis=0) * inv
+    v = jnp.concatenate(left, axis=0) * inv
     y = v - times(v)
     z = y + times(y)
     lower = 2.0 * y - z + times(z)
@@ -215,7 +214,7 @@
         parts = spread(right[j])
         right_ref[2 * j] = parts[0]
         right_ref[2 * j + 1] = parts[1]
-        row_ref[j] = thin[j]
+        row_ref[j] = jnp.where(valid, thin[j], 0.0)
     row_ref[N] = zero
     col_ref[N] = zero
     rows = []
@@ -223,7 +222,8 @@
         for s in range(2):
             for r in range(N):
                 i = inverse[2 * r + s]
-                rows.append(lower_ref[jnp.where(i < N, half * N + i, 2 * N)])
+                at = jnp.bitwise_xor(half, core_id) * N + i
+                rows.append(lower_ref[jnp.where(i < N, at, 2 * N)])
     cols = []
     for k in range(2 * N):
         j = inverse[k]
@@ -233,14 +233,14 @@
         jnp.concatenate(rows, axis=0).astype(BF16), jnp.concatenate(cols, axis=0).astype(BF16), (1, 1)
     )
     core = core.astype(BF16).astype(F32)
-    group = iota((64, 128), 1) // 16
+    place = iota((64, 128), 1) // 16
     for k in range(2 * N):
         c, h = k // 2, k % 2
         total = jnp.zeros((64, 128), F32)
         for combo in range(4):
             x = core[64 * combo : 64 * combo + 64, 128 * (k // 8) : 128 * (k // 8) + 128]
             shift = (16 * combo - 16 * (k % 8)) % 128
-            total = jnp.where(group == combo, pltpu.roll(x, shift, 1) if shift else x, total)
+            total = jnp.where(place == combo, pltpu.roll(x, shift, 1) if shift else x, total)
         j = inverse[k]
         tail = row_ref[j]
         for r in range(N):
@@ -262,12 +262,27 @@
             ).astype(BF16)
 
 
-def finish(blocks, out):
+def finish(source, out, blocks, made, sems):
+    fetch = [
+        pltpu.make_async_copy(source.at[64 * f : 64 * f + 64], blocks.at[64 * f : 64 * f + 64], sems.at[f])
+        for f in range(2)
+    ]
+    for copy in fetch:
+        copy.start()
+
     def tile(f, g, c, at):
         return blocks[f * 64 + g * N + c, 8 * at : 8 * at + 8, :].astype(F32)
 
     lefts, rights = [], []
+    sub = iota((8, 128), 0)
+    group = iota((64, 128), 1) // 16
+    updates = [[], []]
+    mixed = []
+    k = iota((TILE, TILE), 0)
+    target = 64 * ((k // 8) % 8) + 8 * (k // 64) + k % 8
+    order = (target == iota((TILE, TILE), 1)).astype(BF16)
     for f in range(2):
+        fetch[f].wait()
         for side, into in ((0, lefts), (1, rights)):
             lanes = []
             for m in range(4):
@@ -278,17 +293,6 @@
                     )
                 )
             into.append(jnp.concatenate(lanes, axis=1))
-    left = jnp.concatenate(lefts, axis=0)
-    row = iota(left.shape, 0) % 24
-    of_slot = (
-        (row < 8) | (row >= 20),
-        (row >= 8) & (row < 20),
-    )
-    sub = iota((8, 128), 0)
-    group = iota((64, 128), 1) // 16
-    updates = [[], []]
-    mixed = []
-    for f in range(2):
         parts = []
         for c in range(N):
             rows = []
@@ -316,21 +320,36 @@
             updates[s].append(-dot(core, col_u, (0, 0)))
         for c in range(N):
             mixed += spread([tile(f, g, c, 3) for g in range(N)])
-    k = iota((TILE, TILE), 0)
-    target = 64 * ((k // 8) % 8) + 8 * (k // 64) + k % 8
-    order = (target == iota((TILE, TILE), 1)).astype(BF16)
+    left = jnp.concatenate(lefts, axis=0)
+    row = iota(left.shape, 0) % 24
+    of_slot = (
+        (row < 8) | (row >= 20),
+        (row >= 8) & (row < 20),
+    )
     panels = jnp.concatenate(mixed + updates[0] + updates[1], axis=0).astype(BF16)
     panels = dot(panels, order, (1, 0))
     right = jnp.concatenate(rights + [panels[:256]], axis=0).astype(BF16)
+    stores = []
     for s in range(2):
         update = panels[256 + 256 * s : 512 + 256 * s]
         both = jnp.concatenate([jnp.where(of_slot[s], left, 0.0), update], axis=0).astype(BF16)
-        out[s] = dot(both, right, (0, 0)).astype(BF16)
+        for part in range(2):
+            rows = slice(256 * part, 256 * part + 256)
+            made[s, rows, :] = dot(both[:, rows], right, (0, 0)).astype(BF16)
+            copy = pltpu.make_async_copy(made.at[s, rows], out.at[s, rows], sems.at[2 + 2 * s + part])
+            copy.start()
+            stores.append(copy)
+    for copy in stores:
+        copy.wait()
 
 
 def exchange(x, axes, name):
     with jax.named_scope(name):
         return lax.all_to_all(x, axes, split_axis=0, concat_axis=0, tiled=True)
+
+
+def in_vmem(x):
+    return pltpu.with_memory_space_constraint(x, VMEM)
 
 
 def shards(
@@ -339,7 +358,7 @@
     sds = jax.ShapeDtypeStruct
     (send,) = call(
         pack,
-        (VMEM((64, 64, 128), BF16),),
+        (VMEM((64, 40, 128), BF16),),
         (
             pivot[0],
             col_ut[0, 0].T,
@@ -356,19 +375,33 @@
         name="pack",
     )
     got = exchange(send, ("row", "col"), "scatter")
+    twin = lax.ppermute(got, "col", [(k, k ^ 1) for k in range(N)])
     (send,) = call(
         route,
         (VMEM((128, 48, 128), BF16),),
-        (got, parent_map),
-        (VMEM, SMEM),
+        (in_vmem(got), in_vmem(twin), parent_map),
+        (VMEM, VMEM, SMEM),
         (SMEM((2 * N,), jnp.int32),)
         + (VMEM((65, 8, 128), F32),) * 3
         + (VMEM((2 * N + 1, 8, TILE), F32),) * 2
-        + (VMEM((N + 1, 8, 128), F32),) * 2,
+        + (VMEM((N + 1, 8, 128), F32),) * 2
+        + (VMEM((2, TILE, TILE // 2), BF16),),
         name="route",
     )
     blocks = exchange(send, ("side", "row", "col"), "gather")
-    (out,) = call(finish, (sds((2, TILE, TILE), BF16),), (blocks,), (VMEM,), name="finish")
+    (out,) = call(
+        finish,
+        (sds((2, TILE, TILE), BF16),),
+        (blocks,),
+        (pl.ANY,),
+        (
+            VMEM((128, 48, 128), BF16),
+            VMEM((2, TILE, TILE), BF16),
+            pltpu.SemaphoreType.DMA((6,)),
+        ),
+        name="finish",
+        into=pl.ANY,
+    )
     return out[None, :, None]
 
 

time: 103 us -> 98 us (0.951)
  blocking collectives: 91 us -> 82.4 us
  starting transfers between devices: 0 us -> 2.44 us
  waiting for transfers between devices: 0 us -> 1.7 us
    all_to_all x2, blocking collectives: 91 us -> 82.4 us  [exchange(): return lax.all_to_all(x, axes, split_axis=0, concat_axis=0, tiled=True)]
    ppermute x0 -> x1, starting transfers between devices: none -> 2.44 us  [shards(): twin = lax.ppermute(got, 'col', [(k, k ^ 1) for k in range(N)])]
    ppermute x0 -> x1, waiting for transfers between devices: none -> 1.7 us  [shards(): twin = lax.ppermute(got, 'col', [(k, k ^ 1) for k in range(N)])]
  transfers between devices with their start and end apart: 0 -> 1, of which waited for: 0 -> 1; matrix products, arithmetic and copies ran while one was open for 0% -> 0% of each run, Pallas kernels for 0% -> 0%
where the time goes in v5:
time: 98 us; the launch traced here: 97.3 us
  blocking collectives  82.4 us (84%)
  Pallas kernels  8.74 us (9%)
  starting transfers between devices  2.44 us (2%)
  between operations  1.97 us (2%)
  waiting for transfers between devices  1.7 us (2%)
    all_to_all x2, blocking collectives, exchange(): return lax.all_to_all(x, axes, split_axis=0, concat_axis=0, tiled=True)  82.4 us
    pallas_call x3, Pallas kernels, call(): return kernel(*args)  8.74 us
    ppermute x1, starting transfers between devices, shards(): twin = lax.ppermute(got, 'col', [(k, k ^ 1) for k in range(N)])  2.44 us
  transfers between devices with their start and end apart: 1, of which 1 were waited for; matrix products, arithmetic and copies ran while one was open for 0% of the time, Pallas kernels for 0%

profile of v5, /device:TPU:1, one launch (start us, length us, event | category | flops | bytes accessed | tf_op | source)
XLA Modules:
  0.0 97.3 jit_solution(3102414891799317851)
XLA Ops:
  1.9 1.6 %pack.1 = bf16[64,40,128]{2,1,0:T(8,128)(2,1)S(1)} custom-call(f32[8,512]{1,0:T(8,128)} %bitcast.20, bf16[64,96]{1,0:T(8,128)(2,1)} %bitcast.21, bf16[64,96]{1,0:T(8,128)(2,1)} %bitcast.22, bf16[64,96]{1,0:T(8,128)(2,1)} %bitcast.23, bf16[64,96]{1,0:T(8,128)(2,1)} %bitcast.24, bf16[96,512]{1,0:T(8,128)(2,1)} %bitcast.18, bf16[96,512]{1,0:T(8,128)(2,1)} %bitcast.19, ...), custom_call_target="tpu_custom_call" | custom-call | tf_op jit(solution)/shard_map/do_pack/pack/pallas_call | solution.py:37
  3.6 35.0 %all_to_all.10.got = bf16[64,40,128]{2,1,0:T(8,128)(2,1)S(1)} all-to-all(bf16[64,40,128]{2,1,0:T(8,128)(2,1)S(1)} %pack.1), channel_id=1, replica_groups=mesh['pair'=4,'side'=2,'row'=8,'col'=8] {'row','col'}, dimensions={0} | all-to-all | bytes 1310720 | tf_op jit(solution)/shard_map/scatter/all_to_all | solution.py:348
  38.5 2.4 %collective-permute-start = (bf16[64,40,128]{2,1,0:T(8,128)(2,1)S(1)}, bf16[64,40,128]{2,1,0:T(8,128)(2,1)S(1)}, u32[]{:S(2)}, u32[]{:S(2)}) collective-permute-start(bf16[64,40,128]{2,1,0:T(8,128)(2,1)S(1)} %all_to_all.10.got), channel_id=1, source_target_pairs={{0,1},{1,0},{2,3},{3,2},{4,5},{5,4},{6,7},{7,6},{8,9},{9,8},{10,11... | collective-permute-start | bytes 1966088 | tf_op jit(solution)/shard_map/ppermute | solution.py:378
  41.0 1.7 %collective-permute-done.other = bf16[64,40,128]{2,1,0:T(8,128)(2,1)S(1)} collective-permute-done((bf16[64,40,128]{2,1,0:T(8,128)(2,1)S(1)}, bf16[64,40,128]{2,1,0:T(8,128)(2,1)S(1)}, u32[]{:S(2)}, u32[]{:S(2)}) %collective-permute-start) | collective-permute-done | bytes 655392 | tf_op jit(solution)/shard_map/ppermute | solution.py:378
  42.7 2.8 %route.1 = bf16[128,48,128]{2,1,0:T(8,128)(2,1)S(1)} custom-call(bf16[64,40,128]{2,1,0:T(8,128)(2,1)S(1)} %all_to_all.10.got, bf16[64,40,128]{2,1,0:T(8,128)(2,1)S(1)} %collective-permute-done.other, s32[1,8]{1,0:T(1,128)} %mapping.1), custom_call_target="tpu_custom_call" | custom-call | tf_op jit(solution)/shard_map/do_route/route/pallas_call | solution.py:37
  45.4 47.4 %all_to_all.11.source = bf16[128,48,128]{2,1,0:T(8,128)(2,1)} all-to-all(bf16[128,48,128]{2,1,0:T(8,128)(2,1)S(1)} %route.1), channel_id=1, replica_groups=mesh['pair'=4,'side'=2,'row'=8,'col'=8] {'side','row','col'}, dimensions={0} | all-to-all | bytes 3145728 | tf_op jit(solution)/shard_map/gather/all_to_all | solution.py:348
  92.9 4.4 %finish.1 = bf16[2,512,512]{2,1,0:T(8,128)(2,1)} custom-call(bf16[128,48,128]{2,1,0:T(8,128)(2,1)} %all_to_all.11.source), custom_call_target="tpu_custom_call" | custom-call | tf_op jit(solution)/shard_map/do_finish/finish/pallas_call | solution.py:37
Async XLA Ops:
  38.5 4.2 %collective-permute-start = (bf16[64,40,128]{2,1,0:T(8,128)(2,1)S(1)}, bf16[64,40,128]{2,1,0:T(8,128)(2,1)S(1)}, u32[]{:S(2)}, u32[]{:S(2)}) collective-permute-start(bf16[64,40,128]{2,1,0:T(8,128)(2,1)S(1)} %all_to_all.10.got), channel_id=1, source_target_pairs={{0,1},{1,0},{2,3},{3,2},{4,5},{5,4},{6,7},{7,6},{8,9},{9,8},{10,11... | collective-permute-start | bytes 1966088 | tf_op jit(solution)/shard_map/ppermute | solution.py:378

commit v6 on v5

--- a/solution.py
+++ b/solution.py
@@ -24,13 +24,14 @@
     )
 
 
-def call(body, outs, args, specs, scratch=(), name=None, into=VMEM):
+def call(body, outs, args, specs, scratch=(), name=None, into=VMEM, limit=24 * 2**20):
     kernel = pl.pallas_call(
         body,
         out_shape=outs,
         in_specs=[pl.BlockSpec(memory_space=s) for s in specs],
         out_specs=[pl.BlockSpec(memory_space=into) for _ in outs],
         scratch_shapes=scratch,
+        compiler_params=pltpu.CompilerParams(vmem_limit_bytes=limit),
         name=name,
     )
     with jax.named_scope("do_" + name):
@@ -135,11 +136,31 @@
     return [jnp.concatenate(h, axis=1) for h in halves]
 
 
-def route(
-    got, other, mapping, send, inverse, t0, g0, g1, lower_ref, right_ref, row_ref, col_ref, off_ref
-):
+def move(x, start, to):
+    return pltpu.roll(x, (to - start) % 128, 1) if (to - start) % 128 else x
+
+
+def panel_half(ref, i):
+    sub = iota((8, 128), 0)
+    lane = iota((8, 128), 1)
+    x = [jnp.where(sub < 6, ref[i * N + j, 16:24, :].astype(F32), 0.0) for j in range(N)]
+    return jnp.concatenate(
+        [jnp.where(lane < 64, x[2 * m], pltpu.roll(x[2 * m + 1], 64, 1)) for m in range(4)], axis=1
+    )
+
+
+def pivot_half(ref):
+    return jnp.concatenate(
+        [
+            ref[:, 24 + 8 * m : 32 + 8 * m, :].astype(F32).reshape(TILE, 128).astype(BF16)
+            for m in range(2)
+        ],
+        axis=1,
+    )
+
+
+def sort(got, mapping, t0, g0, g1, left, right_ref, row_ref, pair_ref, off, inv, inverse, col_ref):
     fill_inverse(mapping, inverse)
-    core_id = lax.axis_index("col") % 2
     sub = iota((8, 128), 0)
     lane = iota((8, 128), 1)
     valid = sub < 6
@@ -151,25 +172,6 @@
     thin = [zero] * N
     diag = [zero] * 4
     group = lane // 8
-
-    def move(x, start, to):
-        return pltpu.roll(x, (to - start) % 128, 1) if (to - start) % 128 else x
-
-    def halves(ref, i):
-        x = [jnp.where(valid, ref[i * N + j, 16:24, :].astype(F32), 0.0) for j in range(N)]
-        return jnp.concatenate(
-            [jnp.where(lane < 64, x[2 * m], pltpu.roll(x[2 * m + 1], 64, 1)) for m in range(4)], axis=1
-        )
-
-    def columns(ref):
-        return jnp.concatenate(
-            [
-                ref[:, 24 + 8 * m : 32 + 8 * m, :].astype(F32).reshape(TILE, 128).astype(BF16)
-                for m in range(2)
-            ],
-            axis=1,
-        )
-
     for i in range(N):
         thick = zero
         for j in range(N):
@@ -189,34 +191,50 @@
             to = 64 * (i % 2) + 8 * j
             diag[i // 2] = jnp.where(group == to // 8, move(total, 96, to), diag[i // 2])
         col_ref[i] = jnp.where(valid, thick, 0.0)
-    left = [halves(got, i) for i in range(N)]
-    off_ref[core_id] = columns(got)
-    inv = 1.0 / jnp.concatenate([x[0:1] for x in diag], axis=1)
-    left += [halves(other, i) for i in range(N)]
-    off_ref[1 - core_id] = columns(other)
-    off = jnp.concatenate([off_ref[0], off_ref[1]], axis=1)
+        left[8 * i : 8 * i + 8, :] = panel_half(got, i)
+    col_ref[N] = zero
+    for r in range(N):
+        x = col_ref[inverse[2 * r]]
+        y = col_ref[inverse[2 * r + 1]]
+        pair_ref[2 * r] = jnp.where(lane < 64, x, pltpu.roll(y, 64, 1))
+        pair_ref[2 * r + 1] = jnp.where(lane < 64, pltpu.roll(x, 64, 1), y)
+    off[...] = pivot_half(got)
+    full = 1.0 / jnp.concatenate([x[0:1] for x in diag], axis=1)
+    inv[...] = jnp.broadcast_to(full, (8, TILE))
+    right_ref[2 * N] = jnp.zeros((8, TILE), F32)
+    row_ref[N] = zero
+    for j in range(N):
+        parts = spread(right[j])
+        right_ref[2 * j] = parts[0]
+        right_ref[2 * j + 1] = parts[1]
+        row_ref[j] = jnp.where(valid, thin[j], 0.0)
+
+
+def route(
+    other, t0, g0, g1, left, right_ref, row_ref, pair_ref, off, inv, mapping, send, inverse, lower_ref, off_ref
+):
+    fill_inverse(mapping, inverse)
+    core_id = lax.axis_index("col") % 2
+    sub = iota((8, 128), 0)
+    valid = sub < 6
+    off_ref[core_id] = off[...]
+    off_ref[1 - core_id] = pivot_half(other)
+    whole = jnp.concatenate([off_ref[0], off_ref[1]], axis=1)
+    scale = inv[0:1, :]
 
     def times(x):
         high = x.astype(BF16)
         low = (x - high.astype(F32)).astype(BF16)
-        both = dot(jnp.concatenate([high, low], axis=0), off, (1, 0))
-        return (both[:128] + both[128:]) * inv
-
-    v = jnp.concatenate(left, axis=0) * inv
+        both = dot(jnp.concatenate([high, low], axis=0), whole, (1, 0))
+        return (both[:128] + both[128:]) * scale
+
+    v = jnp.concatenate([left[...]] + [panel_half(other, i) for i in range(N)], axis=0) * scale
     y = v - times(v)
     z = y + times(y)
     lower = 2.0 * y - z + times(z)
     for k in range(2 * N):
         lower_ref[k] = lower[8 * k : 8 * k + 8]
     lower_ref[2 * N] = jnp.zeros((8, TILE), F32)
-    right_ref[2 * N] = jnp.zeros((8, TILE), F32)
-    for j in range(N):
-        parts = spread(right[j])
-        right_ref[2 * j] = parts[0]
-        right_ref[2 * j + 1] = parts[1]
-        row_ref[j] = jnp.where(valid, thin[j], 0.0)
-    row_ref[N] = zero
-    col_ref[N] = zero
     rows = []
     for half in range(2):
         for s in range(2):
@@ -234,56 +252,55 @@
     )
     core = core.astype(BF16).astype(F32)
     place = iota((64, 128), 1) // 16
+    low_lanes = iota((8, 128), 1) < 64
     for k in range(2 * N):
         c, h = k // 2, k % 2
         total = jnp.zeros((64, 128), F32)
         for combo in range(4):
             x = core[64 * combo : 64 * combo + 64, 128 * (k // 8) : 128 * (k // 8) + 128]
-            shift = (16 * combo - 16 * (k % 8)) % 128
-            total = jnp.where(place == combo, pltpu.roll(x, shift, 1) if shift else x, total)
+            total = jnp.where(place == combo, move(x, 16 * (k % 8), 16 * combo), total)
+        beside = pltpu.roll(total, 64, 1)
         j = inverse[k]
         tail = row_ref[j]
         for r in range(N):
             part = total[8 * r : 8 * r + 8]
+            shifted = beside[8 * r : 8 * r + 8]
             i0 = inverse[2 * r]
             i1 = inverse[2 * r + 1]
             at0 = jnp.where((i0 < N) & (j < N), i0 * N + j, 64)
             at1 = jnp.where((i1 < N) & (j < N), i1 * N + j, 64)
+            spare = jnp.where(low_lanes, pltpu.roll(part, 6, 0), pltpu.roll(shifted, 4, 0))
             send[(h * N + r) * N + c] = jnp.concatenate(
                 [
                     t0[at0],
                     t0[at1],
                     g0[at0] + g1[at1],
-                    jnp.where(valid, tail, pltpu.roll(part, 6, 0)),
-                    jnp.where(valid, col_ref[i0], pltpu.roll(part, 4, 0)),
-                    jnp.where(valid, col_ref[i1], pltpu.roll(part, 2, 0)),
+                    jnp.where(valid, tail, spare),
+                    jnp.where(valid, pair_ref[2 * r + c % 2], pltpu.roll(part, 2, 0)),
                 ],
                 axis=0,
             ).astype(BF16)
 
 
-def finish(source, out, blocks, made, sems):
-    fetch = [
-        pltpu.make_async_copy(source.at[64 * f : 64 * f + 64], blocks.at[64 * f : 64 * f + 64], sems.at[f])
-        for f in range(2)
-    ]
-    for copy in fetch:
-        copy.start()
-
+def gather_up(blocks, lefts, rights, cores, order_out):
     def tile(f, g, c, at):
         return blocks[f * 64 + g * N + c, 8 * at : 8 * at + 8, :].astype(F32)
 
-    lefts, rights = [], []
-    sub = iota((8, 128), 0)
-    group = iota((64, 128), 1) // 16
-    updates = [[], []]
-    mixed = []
     k = iota((TILE, TILE), 0)
     target = 64 * ((k // 8) % 8) + 8 * (k // 64) + k % 8
     order = (target == iota((TILE, TILE), 1)).astype(BF16)
+    order_out[...] = order
+    sub = iota((8, 128), 0)
+    group = iota((64, 128), 1) // 16
+    core_id = lax.axis_index("col") % 2
+    row = iota((192, TILE), 0) % 24
+    of_slot = (
+        (row < 8) | (row >= 20),
+        (row >= 8) & (row < 20),
+    )
+    mixed = []
     for f in range(2):
-        fetch[f].wait()
-        for side, into in ((0, lefts), (1, rights)):
+        for side in range(2):
             lanes = []
             for m in range(4):
                 c = 2 * m + side
@@ -292,14 +309,21 @@
                         [blocks[f * 64 + g * N + c, 0:24, :].astype(F32) for g in range(N)], axis=0
                     )
                 )
-            into.append(jnp.concatenate(lanes, axis=1))
+            x = jnp.concatenate(lanes, axis=1)
+            if side == 0:
+                for s in range(2):
+                    lefts[s, 192 * f : 192 * f + 192, :] = jnp.where(of_slot[s], x, 0.0).astype(BF16)
+            else:
+                rights[192 * f : 192 * f + 192, :] = x.astype(BF16)
         parts = []
         for c in range(N):
             rows = []
             for g in range(N):
-                x = jnp.where(sub < 4, pltpu.roll(tile(f, g, c, 4), 4, 0), pltpu.roll(tile(f, g, c, 5), 6, 0))
-                x = jnp.where(sub < 2, pltpu.roll(tile(f, g, c, 3), 2, 0), x)
-                rows.append(jnp.where(sub < 6, x, 0.0))
+                x = tile(f, g, c, 3)
+                y = tile(f, g, c, 4)
+                y = jnp.where(sub < 4, pltpu.roll(pltpu.roll(x, 64, 1), 4, 0), pltpu.roll(y, 6, 0))
+                y = jnp.where(sub < 2, pltpu.roll(x, 2, 0), y)
+                rows.append(jnp.where(sub < 6, y, 0.0))
             parts.append(jnp.concatenate(rows, axis=0))
         for s in range(2):
             halves = []
@@ -307,36 +331,40 @@
                 total = jnp.zeros((64, 128), F32)
                 combo = 2 * half + s
                 for c in range(N):
-                    shift = (16 * c - 16 * combo) % 128
-                    x = pltpu.roll(parts[c], shift, 1) if shift else parts[c]
-                    total = jnp.where(group == c, x, total)
+                    total = jnp.where(group == c, move(parts[c], 16 * combo, 16 * c), total)
                 halves.append(total)
-            core = jnp.concatenate(halves, axis=0).astype(BF16)
-            col_u = [[], []]
-            for g in range(N):
-                for half, x in enumerate(spread([tile(f, g, c, 4 + s) for c in range(N)])):
-                    col_u[half].append(x)
-            col_u = jnp.concatenate(col_u[0] + col_u[1], axis=0).astype(BF16)
-            updates[s].append(-dot(core, col_u, (0, 0)))
+            first = jnp.where(core_id == 0, halves[0], halves[1])
+            second = jnp.where(core_id == 0, halves[1], halves[0])
+            cores[2 * f + s] = jnp.concatenate([first, second], axis=0).astype(BF16)
         for c in range(N):
             mixed += spread([tile(f, g, c, 3) for g in range(N)])
-    left = jnp.concatenate(lefts, axis=0)
-    row = iota(left.shape, 0) % 24
-    of_slot = (
-        (row < 8) | (row >= 20),
-        (row >= 8) & (row < 20),
-    )
-    panels = jnp.concatenate(mixed + updates[0] + updates[1], axis=0).astype(BF16)
-    panels = dot(panels, order, (1, 0))
-    right = jnp.concatenate(rights + [panels[:256]], axis=0).astype(BF16)
+    row_v = jnp.concatenate(mixed, axis=0).astype(BF16)
+    rights[384:640, :] = dot(row_v, order, (1, 0)).astype(BF16)
+
+
+def finish(blocks, twin, lefts, rights, cores, order, out, made, sems):
+    updates = [[], []]
+    for f in range(2):
+        col_u = [[], []]
+        for ref in (blocks, twin):
+            for g in range(N):
+                at = f * 64 + g * N
+                tiles = [ref[at + c, 32:40, :].astype(F32) for c in range(N)]
+                for s, x in enumerate(spread(tiles)):
+                    col_u[s].append(x)
+        for s in range(2):
+            x = jnp.concatenate(col_u[s], axis=0).astype(BF16)
+            updates[s].append(-dot(cores[2 * f + s], x, (0, 0)))
+    update = jnp.concatenate(updates[0] + updates[1], axis=0).astype(BF16)
+    update = dot(update, order[...], (1, 0)).astype(BF16)
+    right = rights[...]
     stores = []
     for s in range(2):
-        update = panels[256 + 256 * s : 512 + 256 * s]
-        both = jnp.concatenate([jnp.where(of_slot[s], left, 0.0), update], axis=0).astype(BF16)
+        both = jnp.concatenate([lefts[s], update[256 * s : 256 * s + 256]], axis=0)
         for part in range(2):
             rows = slice(256 * part, 256 * part + 256)
             made[s, rows, :] = dot(both[:, rows], right, (0, 0)).astype(BF16)
-            copy = pltpu.make_async_copy(made.at[s, rows], out.at[s, rows], sems.at[2 + 2 * s + part])
+            copy = pltpu.make_async_copy(made.at[s, rows], out.at[s, rows], sems.at[2 * s + part])
             copy.start()
             stores.append(copy)
     for copy in stores:
@@ -346,6 +374,10 @@
 def exchange(x, axes, name):
     with jax.named_scope(name):
         return lax.all_to_all(x, axes, split_axis=0, concat_axis=0, tiled=True)
+
+
+def swap(x):
+    return lax.ppermute(x, "col", [(k, k ^ 1) for k in range(N)])
 
 
 def in_vmem(x):
@@ -373,31 +405,61 @@
         ),
         (VMEM,) * 7 + (SMEM,) * 3,
         name="pack",
+        limit=None,
     )
     got = exchange(send, ("row", "col"), "scatter")
-    twin = lax.ppermute(got, "col", [(k, k ^ 1) for k in range(N)])
+    got = in_vmem(got)
+    other = in_vmem(swap(got))
+    sorted_out = call(
+        sort,
+        (VMEM((65, 8, 128), F32),) * 3
+        + (
+            VMEM((64, TILE), F32),
+            VMEM((2 * N + 1, 8, TILE), F32),
+            VMEM((N + 1, 8, 128), F32),
+            VMEM((2 * N, 8, 128), F32),
+            VMEM((TILE, TILE // 2), BF16),
+            VMEM((8, TILE), F32),
+        ),
+        (got, parent_map),
+        (VMEM, SMEM),
+        (SMEM((2 * N,), jnp.int32), VMEM((N + 1, 8, 128), F32)),
+        name="sort",
+    )
     (send,) = call(
         route,
-        (VMEM((128, 48, 128), BF16),),
-        (in_vmem(got), in_vmem(twin), parent_map),
-        (VMEM, VMEM, SMEM),
-        (SMEM((2 * N,), jnp.int32),)
-        + (VMEM((65, 8, 128), F32),) * 3
-        + (VMEM((2 * N + 1, 8, TILE), F32),) * 2
-        + (VMEM((N + 1, 8, 128), F32),) * 2
-        + (VMEM((2, TILE, TILE // 2), BF16),),
+        (VMEM((128, 40, 128), BF16),),
+        (other, *(in_vmem(x) for x in sorted_out), parent_map),
+        (VMEM,) * 10 + (SMEM,),
+        (
+            SMEM((2 * N,), jnp.int32),
+            VMEM((2 * N + 1, 8, TILE), F32),
+            VMEM((2, TILE, TILE // 2), BF16),
+        ),
         name="route",
     )
-    blocks = exchange(send, ("side", "row", "col"), "gather")
+    blocks = in_vmem(exchange(send, ("side", "row", "col"), "gather"))
+    twin = in_vmem(swap(blocks))
+    gathered = call(
+        gather_up,
+        (
+            VMEM((2, 384, TILE), BF16),
+            VMEM((640, TILE), BF16),
+            VMEM((4, 128, 128), BF16),
+            VMEM((TILE, TILE), BF16),
+        ),
+        (blocks,),
+        (VMEM,),
+        name="gather_up",
+    )
     (out,) = call(
         finish,
         (sds((2, TILE, TILE), BF16),),
-        (blocks,),
-        (pl.ANY,),
+        (blocks, twin, *(in_vmem(x) for x in gathered)),
+        (VMEM,) * 6,
         (
-            VMEM((128, 48, 128), BF16),
             VMEM((2, TILE, TILE), BF16),
-            pltpu.SemaphoreType.DMA((6,)),
+            pltpu.SemaphoreType.DMA((4,)),
         ),
         name="finish",
         into=pl.ANY,

time: 98 us -> 96.5 us (0.985)
  blocking collectives: 82.4 us -> 76.5 us
  starting transfers between devices: 2.44 us -> 6.31 us
  Pallas kernels: 8.74 us -> 9.79 us
    all_to_all x2, blocking collectives: 82.4 us -> 76.5 us  [exchange(): return lax.all_to_all(x, axes, split_axis=0, concat_axis=0, tiled=True)]
    ppermute x1 -> x2, starting transfers between devices: 2.44 us -> 6.31 us  [swap(): return lax.ppermute(x, 'col', [(k, k ^ 1) for k in range(N)])]
    pallas_call x3 -> x5, Pallas kernels: 8.74 us -> 9.79 us  [call(): return kernel(*args)]
  transfers between devices with their start and end apart: 1 -> 2, of which waited for: 1 -> 1; matrix products, arithmetic and copies ran while one was open for 0% -> 0% of each run, Pallas kernels for 0% -> 4%
where the time goes in v6:
time: 96.5 us; the launch traced here: 96.2 us
  blocking collectives  76.5 us (79%)
  Pallas kernels  9.79 us (10%)
  starting transfers between devices  6.31 us (7%)
  between operations  2.02 us (2%)
  waiting for transfers between devices  1.59 us (2%)
    all_to_all x2, blocking collectives, exchange(): return lax.all_to_all(x, axes, split_axis=0, concat_axis=0, tiled=True)  76.5 us
    pallas_call x5, Pallas kernels, call(): return kernel(*args)  9.79 us
    ppermute x2, starting transfers between devices, swap(): return lax.ppermute(x, 'col', [(k, k ^ 1) for k in range(N)])  6.31 us
  transfers between devices with their start and end apart: 2, of which 1 were waited for; matrix products, arithmetic and copies ran while one was open for 0% of the time, Pallas kernels for 4%

profile of v6, /device:TPU:1, one launch (start us, length us, event | category | flops | bytes accessed | tf_op | source)
XLA Modules:
  0.0 96.2 jit_solution(14564153337725770280)
XLA Ops:
  0.0 0.0 copy-start
  2.0 1.6 %pack.1 = bf16[64,40,128]{2,1,0:T(8,128)(2,1)S(1)} custom-call(f32[8,512]{1,0:T(8,128)} %bitcast.20, bf16[64,96]{1,0:T(8,128)(2,1)} %bitcast.21, bf16[64,96]{1,0:T(8,128)(2,1)} %bitcast.22, bf16[64,96]{1,0:T(8,128)(2,1)} %bitcast.23, bf16[64,96]{1,0:T(8,128)(2,1)} %bitcast.24, bf16[96,512]{1,0:T(8,128)(2,1)} %bitcast.18, bf16[96,512]{1,0:T(8,128)(2,1)} %bitcast.19, ...), custom_call_target="tpu_custom_call" | custom-call | tf_op jit(solution)/shard_map/do_pack/pack/pallas_call | solution.py:38
  3.6 35.0 %all_to_all.10.got = bf16[64,40,128]{2,1,0:T(8,128)(2,1)S(1)} all-to-all(bf16[64,40,128]{2,1,0:T(8,128)(2,1)S(1)} %pack.1), channel_id=1, replica_groups=mesh['pair'=4,'side'=2,'row'=8,'col'=8] {'row','col'}, dimensions={0} | all-to-all | bytes 1310720 | tf_op jit(solution)/shard_map/scatter/all_to_all | solution.py:376
  38.5 2.4 %collective-permute-start = (bf16[64,40,128]{2,1,0:T(8,128)(2,1)S(1)}, bf16[64,40,128]{2,1,0:T(8,128)(2,1)S(1)}, u32[]{:S(2)}, u32[]{:S(2)}) collective-permute-start(bf16[64,40,128]{2,1,0:T(8,128)(2,1)S(1)} %all_to_all.10.got), channel_id=1, source_target_pairs={{0,1},{1,0},{2,3},{3,2},{4,5},{5,4},{6,7},{7,6},{8,9},{9,8},{10,11... | collective-permute-start | bytes 1966088 | tf_op jit(solution)/shard_map/ppermute | solution.py:380
  41.0 0.0 copy-done
  41.0 2.4 %sort.1 = (f32[65,8,128]{2,1,0:T(8,128)S(1)}, f32[65,8,128]{2,1,0:T(8,128)S(1)}, f32[65,8,128]{2,1,0:T(8,128)S(1)}, f32[64,512]{1,0:T(8,128)S(1)}, f32[17,8,512]...) custom-call(bf16[64,40,128]{2,1,0:T(8,128)(2,1)S(1)} %all_to_all.10., ...), custom_call_target="tpu_custom_call" | custom-call | tf_op jit(solution)/shard_map/do_sort/sort/pallas_call | solution.py:38
  43.4 0.0 collective-permute-done.other
  43.4 2.5 %route.1 = bf16[128,40,128]{2,1,0:T(8,128)(2,1)S(1)} custom-call(bf16[64,40,128]{2,1,0:T(8,128)(2,1)S(1)} %collective-permute-done.other, f32[65,8,128]{2,1,0:T(8,128)S(1)} %get-tuple-element.18.t0, f32[65,8,128]{2,1,0:T(8,128)S(1)} %get-tuple-element.19.g0, f32[65,8,128]{2,1,0:T(8,128)S(1)} %get-tuple-element.20.g1, f32[64,512]{1,0:T(8,128)S(1)} %get-tuple-element.21.left, ...), custom_call_target="tpu_custom_call" | custom-call | tf_op jit(solution)/shard_map/do_route/route/pallas_call | solution.py:38
  45.9 41.5 %all_to_all.11.blocks = bf16[128,40,128]{2,1,0:T(8,128)(2,1)S(1)} all-to-all(bf16[128,40,128]{2,1,0:T(8,128)(2,1)S(1)} %route.1), channel_id=1, replica_groups=mesh['pair'=4,'side'=2,'row'=8,'col'=8] {'side','row','col'}, dimensions={0} | all-to-all | bytes 2621440 | tf_op jit(solution)/shard_map/gather/all_to_all | solution.py:376
  87.4 3.9 %collective-permute-start.1 = (bf16[128,40,128]{2,1,0:T(8,128)(2,1)S(1)}, bf16[128,40,128]{2,1,0:T(8,128)(2,1)S(1)}, u32[]{:S(2)}, u32[]{:S(2)}) collective-permute-start(bf16[128,40,128]{2,1,0:T(8,128)(2,1)S(1)} %all_to_all.11.blocks), channel_id=1, source_target_pairs={{0,1},{1,0},{2,3},{3,2},{4,5},{5,4},{6,7},{7,6},{8,9},{9,8},{10,11... | collective-permute-start | bytes 3932168 | tf_op jit(solution)/shard_map/ppermute | solution.py:380
  91.3 1.0 %gather_up.1 = (bf16[2,384,512]{2,1,0:T(8,128)(2,1)S(1)}, bf16[640,512]{1,0:T(8,128)(2,1)S(1)}, bf16[4,128,128]{2,1,0:T(8,128)(2,1)S(1)}, bf16[512,512]{1,0:T(8,128)(2,1)S(1)}) custom-call(bf16[128,40,128]{2,1,0:T(8,128)(2,1)S(1)} %all_to_all.11.blocks), custom_call_target="tpu_custom_call" | custom-call | tf_op jit(solution)/shard_map/do_gather_up/gather_up/pallas_call | solution.py:38
  92.3 1.6 %collective-permute-done.1.twin = bf16[128,40,128]{2,1,0:T(8,128)(2,1)S(1)} collective-permute-done((bf16[128,40,128]{2,1,0:T(8,128)(2,1)S(1)}, bf16[128,40,128]{2,1,0:T(8,128)(2,1)S(1)}, u32[]{:S(2)}, u32[]{:S(2)}) %collective-permute-start.1) | collective-permute-done | bytes 1310752 | tf_op jit(solution)/shard_map/ppermute | solution.py:380
  93.9 2.3 %finish.1 = bf16[2,512,512]{2,1,0:T(8,128)(2,1)} custom-call(bf16[128,40,128]{2,1,0:T(8,128)(2,1)S(1)} %all_to_all.11.blocks, bf16[128,40,128]{2,1,0:T(8,128)(2,1)S(1)} %collective-permute-done.1.twin, bf16[2,384,512]{2,1,0:T(8,128)(2,1)S(1)} %get-tuple-element.27.lefts, bf16[640,512]{1,0:T(8,128)(2,1)S(1)} %get-tuple-element.28.rights, ...), custom_call_target="tpu_custom_call" | custom-call | tf_op jit(solution)/shard_map/do_finish/finish/pallas_call | solution.py:38
Async XLA Ops:
  0.0 41.0 %copy-start = (s32[1,8]{1,0:T(1,128)S(1)}, s32[1,8]{1,0:T(1,128)}, u32[]{:S(2)}) copy-start(s32[1,8]{1,0:T(1,128)} %mapping.3) | copy-start | bytes 100
  38.5 4.8 %collective-permute-start = (bf16[64,40,128]{2,1,0:T(8,128)(2,1)S(1)}, bf16[64,40,128]{2,1,0:T(8,128)(2,1)S(1)}, u32[]{:S(2)}, u32[]{:S(2)}) collective-permute-start(bf16[64,40,128]{2,1,0:T(8,128)(2,1)S(1)} %all_to_all.10.got), channel_id=1, source_target_pairs={{0,1},{1,0},{2,3},{3,2},{4,5},{5,4},{6,7},{7,6},{8,9},{9,8},{10,11... | collective-permute-start | bytes 1966088 | tf_op jit(solution)/shard_map/ppermute | solution.py:380
  87.4 6.5 %collective-permute-start.1 = (bf16[128,40,128]{2,1,0:T(8,128)(2,1)S(1)}, bf16[128,40,128]{2,1,0:T(8,128)(2,1)S(1)}, u32[]{:S(2)}, u32[]{:S(2)}) collective-permute-start(bf16[128,40,128]{2,1,0:T(8,128)(2,1)S(1)} %all_to_all.11.blocks), channel_id=1, source_target_pairs={{0,1},{1,0},{2,3},{3,2},{4,5},{5,4},{6,7},{7,6},{8,9},{9,8},{10,11... | collective-permute-start | bytes 3932168 | tf_op jit(solution)/shard_map/ppermute | solution.py:380

commit v7 on v6

--- a/solution.py
+++ b/solution.py
@@ -346,10 +346,10 @@
     updates = [[], []]
     for f in range(2):
         col_u = [[], []]
-        for ref in (blocks, twin):
+        for ref, rows in ((blocks, slice(32, 40)), (twin, slice(0, 8))):
             for g in range(N):
                 at = f * 64 + g * N
-                tiles = [ref[at + c, 32:40, :].astype(F32) for c in range(N)]
+                tiles = [ref[at + c, rows, :].astype(F32) for c in range(N)]
                 for s, x in enumerate(spread(tiles)):
                     col_u[s].append(x)
         for s in range(2):
@@ -438,8 +438,9 @@
         ),
         name="route",
     )
-    blocks = in_vmem(exchange(send, ("side", "row", "col"), "gather"))
-    twin = in_vmem(swap(blocks))
+    blocks = exchange(send, ("side", "row", "col"), "gather")
+    twin = in_vmem(swap(blocks[:, 32:40]))
+    blocks = in_vmem(blocks)
     gathered = call(
         gather_up,
         (

time: 96.5 us -> 95 us (0.984)
  waiting for transfers between devices: 1.59 us -> 0.09 us
    ppermute x2, waiting for transfers between devices: 1.59 us -> 0.09 us  [swap(): return lax.ppermute(x, 'col', [(k, k ^ 1) for k in range(N)])]
where the time goes in v7:
time: 95 us; the launch traced here: 94.7 us
  blocking collectives  76.5 us (81%)
  Pallas kernels  9.79 us (10%)
  starting transfers between devices  6.32 us (7%)
  between operations  2.02 us (2%)
    all_to_all x2, blocking collectives, exchange(): return lax.all_to_all(x, axes, split_axis=0, concat_axis=0, tiled=True)  76.5 us
    pallas_call x5, Pallas kernels, call(): return kernel(*args)  9.79 us
    ppermute x2, starting transfers between devices, swap(): return lax.ppermute(x, 'col', [(k, k ^ 1) for k in range(N)])  6.32 us
  transfers between devices with their start and end apart: 2, of which 1 were waited for; matrix products, arithmetic and copies ran while one was open for 0% of the time, Pallas kernels for 4%

profile of v7, /device:TPU:1, one launch (start us, length us, event | category | flops | bytes accessed | tf_op | source)
XLA Modules:
  0.0 94.7 jit_solution(13623204788430914820)
XLA Ops:
  0.0 0.0 copy-start
  2.0 1.6 %pack.1 = bf16[64,40,128]{2,1,0:T(8,128)(2,1)S(1)} custom-call(f32[8,512]{1,0:T(8,128)} %bitcast.20, bf16[64,96]{1,0:T(8,128)(2,1)} %bitcast.21, bf16[64,96]{1,0:T(8,128)(2,1)} %bitcast.22, bf16[64,96]{1,0:T(8,128)(2,1)} %bitcast.23, bf16[64,96]{1,0:T(8,128)(2,1)} %bitcast.24, bf16[96,512]{1,0:T(8,128)(2,1)} %bitcast.18, bf16[96,512]{1,0:T(8,128)(2,1)} %bitcast.19, ...), custom_call_target="tpu_custom_call" | custom-call | tf_op jit(solution)/shard_map/do_pack/pack/pallas_call | solution.py:38
  3.6 35.0 %all_to_all.10.got = bf16[64,40,128]{2,1,0:T(8,128)(2,1)S(1)} all-to-all(bf16[64,40,128]{2,1,0:T(8,128)(2,1)S(1)} %pack.1), channel_id=1, replica_groups=mesh['pair'=4,'side'=2,'row'=8,'col'=8] {'row','col'}, dimensions={0} | all-to-all | bytes 1310720 | tf_op jit(solution)/shard_map/scatter/all_to_all | solution.py:376
  38.5 2.4 %collective-permute-start = (bf16[64,40,128]{2,1,0:T(8,128)(2,1)S(1)}, bf16[64,40,128]{2,1,0:T(8,128)(2,1)S(1)}, u32[]{:S(2)}, u32[]{:S(2)}) collective-permute-start(bf16[64,40,128]{2,1,0:T(8,128)(2,1)S(1)} %all_to_all.10.got), channel_id=1, source_target_pairs={{0,1},{1,0},{2,3},{3,2},{4,5},{5,4},{6,7},{7,6},{8,9},{9,8},{10,11... | collective-permute-start | bytes 1966088 | tf_op jit(solution)/shard_map/ppermute | solution.py:380
  41.0 0.0 copy-done
  41.0 2.4 %sort.1 = (f32[65,8,128]{2,1,0:T(8,128)S(1)}, f32[65,8,128]{2,1,0:T(8,128)S(1)}, f32[65,8,128]{2,1,0:T(8,128)S(1)}, f32[64,512]{1,0:T(8,128)S(1)}, f32[17,8,512]...) custom-call(bf16[64,40,128]{2,1,0:T(8,128)(2,1)S(1)} %all_to_all.10., ...), custom_call_target="tpu_custom_call" | custom-call | tf_op jit(solution)/shard_map/do_sort/sort/pallas_call | solution.py:38
  43.4 0.0 collective-permute-done.other
  43.4 2.5 %route.1 = bf16[128,40,128]{2,1,0:T(8,128)(2,1)S(1)} custom-call(bf16[64,40,128]{2,1,0:T(8,128)(2,1)S(1)} %collective-permute-done.other, f32[65,8,128]{2,1,0:T(8,128)S(1)} %get-tuple-element.18.t0, f32[65,8,128]{2,1,0:T(8,128)S(1)} %get-tuple-element.19.g0, f32[65,8,128]{2,1,0:T(8,128)S(1)} %get-tuple-element.20.g1, f32[64,512]{1,0:T(8,128)S(1)} %get-tuple-element.21.left, ...), custom_call_target="tpu_custom_call" | custom-call | tf_op jit(solution)/shard_map/do_route/route/pallas_call | solution.py:38
  45.9 41.5 %all_to_all.11.blocks = bf16[128,40,128]{2,1,0:T(8,128)(2,1)S(1)} all-to-all(bf16[128,40,128]{2,1,0:T(8,128)(2,1)S(1)} %route.1), channel_id=1, replica_groups=mesh['pair'=4,'side'=2,'row'=8,'col'=8] {'side','row','col'}, dimensions={0} | all-to-all | bytes 2621440 | tf_op jit(solution)/shard_map/gather/all_to_all | solution.py:376
  87.4 3.9 %collective-permute-start.1 = (bf16[128,8,128]{2,1,0:T(8,128)(2,1)S(1)}, bf16[128,8,128]{2,1,0:T(8,128)(2,1)S(1)}, u32[]{:S(2)}, u32[]{:S(2)}) collective-permute-start(bf16[128,8,128]{2,1,0:T(8,128)(2,1)S(1)} %slice.4), channel_id=1, source_target_pairs={{0,1},{1,0},{2,3},{3,2},{4,5},{5,4},{6,7},{7,6},{8,9},{9,8},{10,11... | collective-permute-start | bytes 786440 | tf_op jit(solution)/shard_map/ppermute | solution.py:380
  91.3 1.0 %gather_up.1 = (bf16[2,384,512]{2,1,0:T(8,128)(2,1)S(1)}, bf16[640,512]{1,0:T(8,128)(2,1)S(1)}, bf16[4,128,128]{2,1,0:T(8,128)(2,1)S(1)}, bf16[512,512]{1,0:T(8,128)(2,1)S(1)}) custom-call(bf16[128,40,128]{2,1,0:T(8,128)(2,1)S(1)} %all_to_all.11.blocks), custom_call_target="tpu_custom_call" | custom-call | tf_op jit(solution)/shard_map/do_gather_up/gather_up/pallas_call | solution.py:38
  92.4 0.1 collective-permute-done.1.twin
  92.4 2.3 %finish.1 = bf16[2,512,512]{2,1,0:T(8,128)(2,1)} custom-call(bf16[128,40,128]{2,1,0:T(8,128)(2,1)S(1)} %all_to_all.11.blocks, bf16[128,8,128]{2,1,0:T(8,128)(2,1)S(1)} %collective-permute-done.1.twin, bf16[2,384,512]{2,1,0:T(8,128)(2,1)S(1)} %get-tuple-element.27.lefts, bf16[640,512]{1,0:T(8,128)(2,1)S(1)} %get-tuple-element.28.rights, ...), custom_call_target="tpu_custom_call" | custom-call | tf_op jit(solution)/shard_map/do_finish/finish/pallas_call | solution.py:38
  (1 shorter events, 0.0 us)
Async XLA Ops:
  0.0 41.0 %copy-start = (s32[1,8]{1,0:T(1,128)S(1)}, s32[1,8]{1,0:T(1,128)}, u32[]{:S(2)}) copy-start(s32[1,8]{1,0:T(1,128)} %mapping.3) | copy-start | bytes 100
  38.5 4.8 %collective-permute-start = (bf16[64,40,128]{2,1,0:T(8,128)(2,1)S(1)}, bf16[64,40,128]{2,1,0:T(8,128)(2,1)S(1)}, u32[]{:S(2)}, u32[]{:S(2)}) collective-permute-start(bf16[64,40,128]{2,1,0:T(8,128)(2,1)S(1)} %all_to_all.10.got), channel_id=1, source_target_pairs={{0,1},{1,0},{2,3},{3,2},{4,5},{5,4},{6,7},{7,6},{8,9},{9,8},{10,11... | collective-permute-start | bytes 1966088 | tf_op jit(solution)/shard_map/ppermute | solution.py:380
  87.4 5.0 %collective-permute-start.1 = (bf16[128,8,128]{2,1,0:T(8,128)(2,1)S(1)}, bf16[128,8,128]{2,1,0:T(8,128)(2,1)S(1)}, u32[]{:S(2)}, u32[]{:S(2)}) collective-permute-start(bf16[128,8,128]{2,1,0:T(8,128)(2,1)S(1)} %slice.4), channel_id=1, source_target_pairs={{0,1},{1,0},{2,3},{3,2},{4,5},{5,4},{6,7},{7,6},{8,9},{9,8},{10,11... | collective-permute-start | bytes 786440 | tf_op jit(solution)/shard_map/ppermute | solution.py:380

commit v8 on v7

--- a/solution.py
+++ b/solution.py
@@ -12,6 +12,7 @@
 N = 8
 SMEM = pltpu.SMEM
 VMEM = pltpu.VMEM
+MAP = (SMEM((1, N), jnp.int32), pltpu.SemaphoreType.DMA((1,)), SMEM((2 * N,), jnp.int32))
 
 
 def iota(shape, dim):
@@ -36,6 +37,12 @@
     )
     with jax.named_scope("do_" + name):
         return kernel(*args)
+
+
+def fetch_map(mapping, table, sem):
+    copy = pltpu.make_async_copy(mapping, table, sem.at[0])
+    copy.start()
+    return copy
 
 
 def fill_inverse(mapping, inverse):
@@ -159,8 +166,10 @@
     )
 
 
-def sort(got, mapping, t0, g0, g1, left, right_ref, row_ref, pair_ref, off, inv, inverse, col_ref):
-    fill_inverse(mapping, inverse)
+def sort(
+    got, mapping, t0, g0, g1, left, right_ref, row_ref, pair_ref, off, inv, table, sem, inverse, col_ref
+):
+    fetch = fetch_map(mapping, table, sem)
     sub = iota((8, 128), 0)
     lane = iota((8, 128), 1)
     valid = sub < 6
@@ -193,11 +202,6 @@
         col_ref[i] = jnp.where(valid, thick, 0.0)
         left[8 * i : 8 * i + 8, :] = panel_half(got, i)
     col_ref[N] = zero
-    for r in range(N):
-        x = col_ref[inverse[2 * r]]
-        y = col_ref[inverse[2 * r + 1]]
-        pair_ref[2 * r] = jnp.where(lane < 64, x, pltpu.roll(y, 64, 1))
-        pair_ref[2 * r + 1] = jnp.where(lane < 64, pltpu.roll(x, 64, 1), y)
     off[...] = pivot_half(got)
     full = 1.0 / jnp.concatenate([x[0:1] for x in diag], axis=1)
     inv[...] = jnp.broadcast_to(full, (8, TILE))
@@ -208,12 +212,20 @@
         right_ref[2 * j] = parts[0]
         right_ref[2 * j + 1] = parts[1]
         row_ref[j] = jnp.where(valid, thin[j], 0.0)
+    fetch.wait()
+    fill_inverse(table, inverse)
+    for r in range(N):
+        x = col_ref[inverse[2 * r]]
+        y = col_ref[inverse[2 * r + 1]]
+        pair_ref[2 * r] = jnp.where(lane < 64, x, pltpu.roll(y, 64, 1))
+        pair_ref[2 * r + 1] = jnp.where(lane < 64, pltpu.roll(x, 64, 1), y)
 
 
 def route(
-    other, t0, g0, g1, left, right_ref, row_ref, pair_ref, off, inv, mapping, send, inverse, lower_ref, off_ref
+    other, t0, g0, g1, left, right_ref, row_ref, pair_ref, off, inv, mapping, send, table, sem, inverse,
+    lower_ref, off_ref
 ):
-    fill_inverse(mapping, inverse)
+    fetch = fetch_map(mapping, table, sem)
     core_id = lax.axis_index("col") % 2
     sub = iota((8, 128), 0)
     valid = sub < 6
@@ -235,6 +247,8 @@
     for k in range(2 * N):
         lower_ref[k] = lower[8 * k : 8 * k + 8]
     lower_ref[2 * N] = jnp.zeros((8, TILE), F32)
+    fetch.wait()
+    fill_inverse(table, inverse)
     rows = []
     for half in range(2):
         for s in range(2):
@@ -282,7 +296,7 @@
             ).astype(BF16)
 
 
-def gather_up(blocks, lefts, rights, cores, order_out):
+def gather_up(blocks, lefts, rights, row_v, cores, own_u, order_out):
     def tile(f, g, c, at):
         return blocks[f * 64 + g * N + c, 8 * at : 8 * at + 8, :].astype(F32)
 
@@ -293,28 +307,26 @@
     sub = iota((8, 128), 0)
     group = iota((64, 128), 1) // 16
     core_id = lax.axis_index("col") % 2
-    row = iota((192, TILE), 0) % 24
-    of_slot = (
-        (row < 8) | (row >= 20),
-        (row >= 8) & (row < 20),
-    )
+    of_slot = (sub >= 4, sub < 4)
     mixed = []
+    own = []
     for f in range(2):
-        for side in range(2):
-            lanes = []
+        for side, into in ((0, lefts), (1, rights)):
+            lanes = ([], [])
             for m in range(4):
-                c = 2 * m + side
-                lanes.append(
-                    jnp.concatenate(
-                        [blocks[f * 64 + g * N + c, 0:24, :].astype(F32) for g in range(N)], axis=0
-                    )
-                )
-            x = jnp.concatenate(lanes, axis=1)
-            if side == 0:
+                x = [
+                    blocks[f * 64 + g * N + 2 * m + side, 0:24, :].astype(F32) for g in range(N)
+                ]
                 for s in range(2):
-                    lefts[s, 192 * f : 192 * f + 192, :] = jnp.where(of_slot[s], x, 0.0).astype(BF16)
-            else:
-                rights[192 * f : 192 * f + 192, :] = x.astype(BF16)
+                    rows = []
+                    for y in x:
+                        rest = y[16:24]
+                        if side == 0:
+                            rest = jnp.where(of_slot[s], rest, 0.0)
+                        rows += [y[8 * s : 8 * s + 8], rest]
+                    lanes[s].append(jnp.concatenate(rows, axis=0))
+            for s in range(2):
+                into[s, 128 * f : 128 * f + 128, :] = jnp.concatenate(lanes[s], axis=1).astype(BF16)
         parts = []
         for c in range(N):
             rows = []
@@ -338,29 +350,35 @@
             cores[2 * f + s] = jnp.concatenate([first, second], axis=0).astype(BF16)
         for c in range(N):
             mixed += spread([tile(f, g, c, 3) for g in range(N)])
-    row_v = jnp.concatenate(mixed, axis=0).astype(BF16)
-    rights[384:640, :] = dot(row_v, order, (1, 0)).astype(BF16)
-
-
-def finish(blocks, twin, lefts, rights, cores, order, out, made, sems):
+        own += half_panels([[tile(f, g, c, 4) for c in range(N)] for g in range(N)])
+    panels = jnp.concatenate(mixed + own, axis=0).astype(BF16)
+    panels = dot(panels, order, (1, 0)).astype(BF16)
+    row_v[...] = panels[:256]
+    own_u[...] = panels[256:]
+
+
+def half_panels(tiles):
+    both = [spread(x) for x in tiles]
+    return [jnp.concatenate([x[s] for x in both], axis=0) for s in range(2)]
+
+
+def finish(twin, lefts, rights, row_v, cores, own_u, order, out, made, sems):
+    other = []
+    for f in range(2):
+        other += half_panels(
+            [[twin[f * 64 + g * N + c].astype(F32) for c in range(N)] for g in range(N)]
+        )
+    other = dot(jnp.concatenate(other, axis=0).astype(BF16), order[...], (1, 0)).astype(BF16)
     updates = [[], []]
     for f in range(2):
-        col_u = [[], []]
-        for ref, rows in ((blocks, slice(32, 40)), (twin, slice(0, 8))):
-            for g in range(N):
-                at = f * 64 + g * N
-                tiles = [ref[at + c, rows, :].astype(F32) for c in range(N)]
-                for s, x in enumerate(spread(tiles)):
-                    col_u[s].append(x)
         for s in range(2):
-            x = jnp.concatenate(col_u[s], axis=0).astype(BF16)
-            updates[s].append(-dot(cores[2 * f + s], x, (0, 0)))
-    update = jnp.concatenate(updates[0] + updates[1], axis=0).astype(BF16)
-    update = dot(update, order[...], (1, 0)).astype(BF16)
-    right = rights[...]
+            at = slice(64 * (2 * f + s), 64 * (2 * f + s) + 64)
+            col_u = jnp.concatenate([own_u[at, :], other[at]], axis=0)
+            updates[s].append((-dot(cores[2 * f + s], col_u, (0, 0))).astype(BF16))
     stores = []
     for s in range(2):
-        both = jnp.concatenate([lefts[s], update[256 * s : 256 * s + 256]], axis=0)
+        both = jnp.concatenate([lefts[s]] + updates[s], axis=0)
+        right = jnp.concatenate([rights[s], row_v[...]], axis=0)
         for part in range(2):
             rows = slice(256 * part, 256 * part + 256)
             made[s, rows, :] = dot(both[:, rows], right, (0, 0)).astype(BF16)
@@ -422,17 +440,17 @@
             VMEM((8, TILE), F32),
         ),
         (got, parent_map),
-        (VMEM, SMEM),
-        (SMEM((2 * N,), jnp.int32), VMEM((N + 1, 8, 128), F32)),
+        (VMEM, pl.ANY),
+        MAP + (VMEM((N + 1, 8, 128), F32),),
         name="sort",
     )
     (send,) = call(
         route,
         (VMEM((128, 40, 128), BF16),),
         (other, *(in_vmem(x) for x in sorted_out), parent_map),
-        (VMEM,) * 10 + (SMEM,),
-        (
-            SMEM((2 * N,), jnp.int32),
+        (VMEM,) * 10 + (pl.ANY,),
+        MAP
+        + (
             VMEM((2 * N + 1, 8, TILE), F32),
             VMEM((2, TILE, TILE // 2), BF16),
         ),
@@ -444,9 +462,11 @@
     gathered = call(
         gather_up,
         (
-            VMEM((2, 384, TILE), BF16),
-            VMEM((640, TILE), BF16),
+            VMEM((2, 256, TILE), BF16),
+            VMEM((2, 256, TILE), BF16),
+            VMEM((256, TILE), BF16),
             VMEM((4, 128, 128), BF16),
+            VMEM((256, TILE), BF16),
             VMEM((TILE, TILE), BF16),
         ),
         (blocks,),
@@ -456,8 +476,8 @@
     (out,) = call(
         finish,
         (sds((2, TILE, TILE), BF16),),
-        (blocks, twin, *(in_vmem(x) for x in gathered)),
-        (VMEM,) * 6,
+        (twin, *(in_vmem(x) for x in gathered)),
+        (VMEM,) * 7,
         (
             VMEM((2, TILE, TILE), BF16),
             pltpu.SemaphoreType.DMA((4,)),

time: 95 us -> 94 us (0.989)
  Pallas kernels: 9.79 us -> 8.77 us
    pallas_call x5, Pallas kernels: 9.79 us -> 8.77 us  [call(): return kernel(*args)]
  transfers between devices with their start and end apart: 2 -> 2, of which waited for: 1 -> 1; matrix products, arithmetic and copies ran while one was open for 0% -> 0% of each run, Pallas kernels for 4% -> 3%
where the time goes in v8:
time: 94 us; the launch traced here: 93.8 us
  blocking collectives  76.5 us (81%)
  Pallas kernels  8.77 us (9%)
  starting transfers between devices  6.32 us (7%)
  between operations  2.02 us (2%)
    all_to_all x2, blocking collectives, exchange(): return lax.all_to_all(x, axes, split_axis=0, concat_axis=0, tiled=True)  76.5 us
    pallas_call x5, Pallas kernels, call(): return kernel(*args)  8.77 us
    ppermute x2, starting transfers between devices, swap(): return lax.ppermute(x, 'col', [(k, k ^ 1) for k in range(N)])  6.32 us
  transfers between devices with their start and end apart: 2, of which 1 were waited for; matrix products, arithmetic and copies ran while one was open for 0% of the time, Pallas kernels for 3%

profile of v8, /device:TPU:1, one launch (start us, length us, event | category | flops | bytes accessed | tf_op | source)
XLA Modules:
  0.0 93.8 jit_solution(3880310046229588944)
XLA Ops:
  0.0 0.0 copy-start
  2.0 1.6 %pack.1 = bf16[64,40,128]{2,1,0:T(8,128)(2,1)S(1)} custom-call(f32[8,512]{1,0:T(8,128)} %bitcast.20, bf16[64,96]{1,0:T(8,128)(2,1)} %bitcast.21, bf16[64,96]{1,0:T(8,128)(2,1)} %bitcast.22, bf16[64,96]{1,0:T(8,128)(2,1)} %bitcast.23, bf16[64,96]{1,0:T(8,128)(2,1)} %bitcast.24, bf16[96,512]{1,0:T(8,128)(2,1)} %bitcast.18, bf16[96,512]{1,0:T(8,128)(2,1)} %bitcast.19, ...), custom_call_target="tpu_custom_call" | custom-call | tf_op jit(solution)/shard_map/do_pack/pack/pallas_call | solution.py:39
  3.6 35.0 %all_to_all.10.got = bf16[64,40,128]{2,1,0:T(8,128)(2,1)S(1)} all-to-all(bf16[64,40,128]{2,1,0:T(8,128)(2,1)S(1)} %pack.1), channel_id=1, replica_groups=mesh['pair'=4,'side'=2,'row'=8,'col'=8] {'row','col'}, dimensions={0} | all-to-all | bytes 1310720 | tf_op jit(solution)/shard_map/scatter/all_to_all | solution.py:394
  38.5 2.4 %collective-permute-start = (bf16[64,40,128]{2,1,0:T(8,128)(2,1)S(1)}, bf16[64,40,128]{2,1,0:T(8,128)(2,1)S(1)}, u32[]{:S(2)}, u32[]{:S(2)}) collective-permute-start(bf16[64,40,128]{2,1,0:T(8,128)(2,1)S(1)} %all_to_all.10.got), channel_id=1, source_target_pairs={{0,1},{1,0},{2,3},{3,2},{4,5},{5,4},{6,7},{7,6},{8,9},{9,8},{10,11... | collective-permute-start | bytes 1966088 | tf_op jit(solution)/shard_map/ppermute | solution.py:398
  41.0 0.0 copy-done
  41.0 2.2 %sort.1 = (f32[65,8,128]{2,1,0:T(8,128)S(1)}, f32[65,8,128]{2,1,0:T(8,128)S(1)}, f32[65,8,128]{2,1,0:T(8,128)S(1)}, f32[64,512]{1,0:T(8,128)S(1)}, f32[17,8,512]...) custom-call(bf16[64,40,128]{2,1,0:T(8,128)(2,1)S(1)} %all_to_all.10., ...), custom_call_target="tpu_custom_call" | custom-call | tf_op jit(solution)/shard_map/do_sort/sort/pallas_call | solution.py:39
  43.2 0.0 collective-permute-done.other
  43.2 2.0 %route.1 = bf16[128,40,128]{2,1,0:T(8,128)(2,1)S(1)} custom-call(bf16[64,40,128]{2,1,0:T(8,128)(2,1)S(1)} %collective-permute-done.other, f32[65,8,128]{2,1,0:T(8,128)S(1)} %get-tuple-element.20.t0, f32[65,8,128]{2,1,0:T(8,128)S(1)} %get-tuple-element.21.g0, f32[65,8,128]{2,1,0:T(8,128)S(1)} %get-tuple-element.22.g1, f32[64,512]{1,0:T(8,128)S(1)} %get-tuple-element.23.left, ...), custom_call_target="tpu_custom_call" | custom-call | tf_op jit(solution)/shard_map/do_route/route/pallas_call | solution.py:39
  45.3 41.5 %all_to_all.11.blocks = bf16[128,40,128]{2,1,0:T(8,128)(2,1)S(1)} all-to-all(bf16[128,40,128]{2,1,0:T(8,128)(2,1)S(1)} %route.1), channel_id=1, replica_groups=mesh['pair'=4,'side'=2,'row'=8,'col'=8] {'side','row','col'}, dimensions={0} | all-to-all | bytes 2621440 | tf_op jit(solution)/shard_map/gather/all_to_all | solution.py:394
  86.8 3.9 %collective-permute-start.1 = (bf16[128,8,128]{2,1,0:T(8,128)(2,1)S(1)}, bf16[128,8,128]{2,1,0:T(8,128)(2,1)S(1)}, u32[]{:S(2)}, u32[]{:S(2)}) collective-permute-start(bf16[128,8,128]{2,1,0:T(8,128)(2,1)S(1)} %slice.4), channel_id=1, source_target_pairs={{0,1},{1,0},{2,3},{3,2},{4,5},{5,4},{6,7},{7,6},{8,9},{9,8},{10,11... | collective-permute-start | bytes 786440 | tf_op jit(solution)/shard_map/ppermute | solution.py:398
  90.7 1.0 %gather_up.1 = (bf16[2,256,512]{2,1,0:T(8,128)(2,1)S(1)}, bf16[2,256,512]{2,1,0:T(8,128)(2,1)S(1)}, bf16[256,512]{1,0:T(8,128)(2,1)S(1)}, bf16[4,128,128]{2,1,0:...) custom-call(bf16[128,40,128]{2,1,0:T(8,128)(2,1)S(1)} %all_to_all.11.blocks), custom_call_target="tpu_custom_call" | custom-call | tf_op jit(solution)/shard_map/do_gather_up/gather_up/pallas_call | solution.py:39
  91.7 0.1 collective-permute-done.1.twin
  91.8 1.9 %finish.1 = bf16[2,512,512]{2,1,0:T(8,128)(2,1)} custom-call(bf16[128,8,128]{2,1,0:T(8,128)(2,1)S(1)} %collective-permute-done.1.twin, bf16[2,256,512]{2,1,0:T(8,128)(2,1)S(1)} %get-tuple-element.29.lefts, bf16[2,256,512]{2,1,0:T(8,128)(2,1)S(1)} %get-tuple-element.30.rights, bf16[256,512]{1,0:T(8,128)(2,1)S(1)} %get-tuple-element.31.row_v, ...), custom_call_target="tpu_custom_call" | custom-call | tf_op jit(solution)/shard_map/do_finish/finish/pallas_call | solution.py:39
  (1 shorter events, 0.0 us)
Async XLA Ops:
  0.0 41.0 %copy-start = (s32[1,8]{1,0:T(1,128)S(1)}, s32[1,8]{1,0:T(1,128)}, u32[]{:S(2)}) copy-start(s32[1,8]{1,0:T(1,128)} %mapping.3) | copy-start | bytes 100
  38.5 4.7 %collective-permute-start = (bf16[64,40,128]{2,1,0:T(8,128)(2,1)S(1)}, bf16[64,40,128]{2,1,0:T(8,128)(2,1)S(1)}, u32[]{:S(2)}, u32[]{:S(2)}) collective-permute-start(bf16[64,40,128]{2,1,0:T(8,128)(2,1)S(1)} %all_to_all.10.got), channel_id=1, source_target_pairs={{0,1},{1,0},{2,3},{3,2},{4,5},{5,4},{6,7},{7,6},{8,9},{9,8},{10,11... | collective-permute-start | bytes 1966088 | tf_op jit(solution)/shard_map/ppermute | solution.py:398
  86.8 5.0 %collective-permute-start.1 = (bf16[128,8,128]{2,1,0:T(8,128)(2,1)S(1)}, bf16[128,8,128]{2,1,0:T(8,128)(2,1)S(1)}, u32[]{:S(2)}, u32[]{:S(2)}) collective-permute-start(bf16[128,8,128]{2,1,0:T(8,128)(2,1)S(1)} %slice.4), channel_id=1, source_target_pairs={{0,1},{1,0},{2,3},{3,2},{4,5},{5,4},{6,7},{7,6},{8,9},{9,8},{10,11... | collective-permute-start | bytes 786440 | tf_op jit(solution)/shard_map/ppermute | solution.py:398

commit v9 on v8

--- a/solution.py
+++ b/solution.py
@@ -12,7 +12,6 @@
 N = 8
 SMEM = pltpu.SMEM
 VMEM = pltpu.VMEM
-MAP = (SMEM((1, N), jnp.int32), pltpu.SemaphoreType.DMA((1,)), SMEM((2 * N,), jnp.int32))
 
 
 def iota(shape, dim):
@@ -39,17 +38,17 @@
         return kernel(*args)
 
 
-def fetch_map(mapping, table, sem):
-    copy = pltpu.make_async_copy(mapping, table, sem.at[0])
-    copy.start()
-    return copy
-
-
 def fill_inverse(mapping, inverse):
+    lane = iota((1, N), 1)
+    x = mapping[...].astype(F32)
+    scale = jnp.where(lane % 4 == 0, 1.0, jnp.where(lane % 4 == 1, 16.0, jnp.where(lane % 4 == 2, 256.0, 4096.0)))
+    digits = [
+        jnp.sum(jnp.where(lane // 4 == k, x * scale, 0.0)).astype(jnp.int32) for k in range(2)
+    ]
     for k in range(2 * N):
         inverse[k] = N
     for k in range(N):
-        inverse[mapping[0, k]] = k
+        inverse[(digits[k // 4] >> (4 * (k % 4))) & 15] = k
 
 
 def onehot(offset):
@@ -147,19 +146,19 @@
     return pltpu.roll(x, (to - start) % 128, 1) if (to - start) % 128 else x
 
 
-def panel_half(ref, i):
+def panel_half(ref, i, at):
     sub = iota((8, 128), 0)
     lane = iota((8, 128), 1)
-    x = [jnp.where(sub < 6, ref[i * N + j, 16:24, :].astype(F32), 0.0) for j in range(N)]
+    x = [jnp.where(sub < 6, ref[i * N + j, at : at + 8, :].astype(F32), 0.0) for j in range(N)]
     return jnp.concatenate(
         [jnp.where(lane < 64, x[2 * m], pltpu.roll(x[2 * m + 1], 64, 1)) for m in range(4)], axis=1
     )
 
 
-def pivot_half(ref):
+def pivot_half(ref, at):
     return jnp.concatenate(
         [
-            ref[:, 24 + 8 * m : 32 + 8 * m, :].astype(F32).reshape(TILE, 128).astype(BF16)
+            ref[:, at + 8 * m : at + 8 * m + 8, :].astype(F32).reshape(TILE, 128).astype(BF16)
             for m in range(2)
         ],
         axis=1,
@@ -167,9 +166,9 @@
 
 
 def sort(
-    got, mapping, t0, g0, g1, left, right_ref, row_ref, pair_ref, off, inv, table, sem, inverse, col_ref
+    got, mapping, t0, g0, g1, left, right_ref, row_ref, pair_ref, off, inv, inverse, col_ref
 ):
-    fetch = fetch_map(mapping, table, sem)
+    fill_inverse(mapping, inverse)
     sub = iota((8, 128), 0)
     lane = iota((8, 128), 1)
     valid = sub < 6
@@ -200,9 +199,9 @@
             to = 64 * (i % 2) + 8 * j
             diag[i // 2] = jnp.where(group == to // 8, move(total, 96, to), diag[i // 2])
         col_ref[i] = jnp.where(valid, thick, 0.0)
-        left[8 * i : 8 * i + 8, :] = panel_half(got, i)
+        left[8 * i : 8 * i + 8, :] = panel_half(got, i, 16)
     col_ref[N] = zero
-    off[...] = pivot_half(got)
+    off[...] = pivot_half(got, 24)
     full = 1.0 / jnp.concatenate([x[0:1] for x in diag], axis=1)
     inv[...] = jnp.broadcast_to(full, (8, TILE))
     right_ref[2 * N] = jnp.zeros((8, TILE), F32)
@@ -212,8 +211,6 @@
         right_ref[2 * j] = parts[0]
         right_ref[2 * j + 1] = parts[1]
         row_ref[j] = jnp.where(valid, thin[j], 0.0)
-    fetch.wait()
-    fill_inverse(table, inverse)
     for r in range(N):
         x = col_ref[inverse[2 * r]]
         y = col_ref[inverse[2 * r + 1]]
@@ -222,15 +219,14 @@
 
 
 def route(
-    other, t0, g0, g1, left, right_ref, row_ref, pair_ref, off, inv, mapping, send, table, sem, inverse,
-    lower_ref, off_ref
+    other, t0, g0, g1, left, right_ref, row_ref, pair_ref, off, inv, mapping, send, inverse, lower_ref, off_ref
 ):
-    fetch = fetch_map(mapping, table, sem)
+    fill_inverse(mapping, inverse)
     core_id = lax.axis_index("col") % 2
     sub = iota((8, 128), 0)
     valid = sub < 6
     off_ref[core_id] = off[...]
-    off_ref[1 - core_id] = pivot_half(other)
+    off_ref[1 - core_id] = pivot_half(other, 8)
     whole = jnp.concatenate([off_ref[0], off_ref[1]], axis=1)
     scale = inv[0:1, :]
 
@@ -240,15 +236,13 @@
         both = dot(jnp.concatenate([high, low], axis=0), whole, (1, 0))
         return (both[:128] + both[128:]) * scale
 
-    v = jnp.concatenate([left[...]] + [panel_half(other, i) for i in range(N)], axis=0) * scale
+    v = jnp.concatenate([left[...]] + [panel_half(other, i, 0) for i in range(N)], axis=0) * scale
     y = v - times(v)
     z = y + times(y)
     lower = 2.0 * y - z + times(z)
     for k in range(2 * N):
         lower_ref[k] = lower[8 * k : 8 * k + 8]
     lower_ref[2 * N] = jnp.zeros((8, TILE), F32)
-    fetch.wait()
-    fill_inverse(table, inverse)
     rows = []
     for half in range(2):
         for s in range(2):
@@ -426,8 +420,8 @@
         limit=None,
     )
     got = exchange(send, ("row", "col"), "scatter")
+    other = in_vmem(swap(got[:, 16:40]))
     got = in_vmem(got)
-    other = in_vmem(swap(got))
     sorted_out = call(
         sort,
         (VMEM((65, 8, 128), F32),) * 3
@@ -440,17 +434,17 @@
             VMEM((8, TILE), F32),
         ),
         (got, parent_map),
-        (VMEM, pl.ANY),
-        MAP + (VMEM((N + 1, 8, 128), F32),),
+        (VMEM, VMEM),
+        (SMEM((2 * N,), jnp.int32), VMEM((N + 1, 8, 128), F32)),
         name="sort",
     )
     (send,) = call(
         route,
         (VMEM((128, 40, 128), BF16),),
         (other, *(in_vmem(x) for x in sorted_out), parent_map),
-        (VMEM,) * 10 + (pl.ANY,),
-        MAP
-        + (
+        (VMEM,) * 11,
+        (
+            SMEM((2 * N,), jnp.int32),
             VMEM((2 * N + 1, 8, TILE), F32),
             VMEM((2, TILE, TILE // 2), BF16),
         ),

time: 94 us -> 93.6 us (level)
  no operation moved by 1% of the time
where the time goes in v9:
time: 93.6 us; the launch traced here: 93.3 us
  blocking collectives  76.5 us (82%)
  Pallas kernels  8.32 us (9%)
  starting transfers between devices  6.33 us (7%)
  between operations  2.02 us (2%)
    all_to_all x2, blocking collectives, exchange(): return lax.all_to_all(x, axes, split_axis=0, concat_axis=0, tiled=True)  76.5 us
    pallas_call x5, Pallas kernels, call(): return kernel(*args)  8.32 us
    ppermute x2, starting transfers between devices, swap(): return lax.ppermute(x, 'col', [(k, k ^ 1) for k in range(N)])  6.33 us
  transfers between devices with their start and end apart: 2, of which 1 were waited for; matrix products, arithmetic and copies ran while one was open for 0% of the time, Pallas kernels for 3%

profile of v9, /device:TPU:1, one launch (start us, length us, event | category | flops | bytes accessed | tf_op | source)
XLA Modules:
  0.0 93.3 jit_solution(14437309040495559717)
XLA Ops:
  1.9 0.0 copy-start
  2.0 1.6 %pack.1 = bf16[64,40,128]{2,1,0:T(8,128)(2,1)S(1)} custom-call(f32[8,512]{1,0:T(8,128)} %bitcast.20, bf16[64,96]{1,0:T(8,128)(2,1)} %bitcast.21, bf16[64,96]{1,0:T(8,128)(2,1)} %bitcast.22, bf16[64,96]{1,0:T(8,128)(2,1)} %bitcast.23, bf16[64,96]{1,0:T(8,128)(2,1)} %bitcast.24, bf16[96,512]{1,0:T(8,128)(2,1)} %bitcast.18, bf16[96,512]{1,0:T(8,128)(2,1)} %bitcast.19, ...), custom_call_target="tpu_custom_call" | custom-call | tf_op jit(solution)/shard_map/do_pack/pack/pallas_call | solution.py:38
  3.6 35.0 %all_to_all.10.got = bf16[64,40,128]{2,1,0:T(8,128)(2,1)S(1)} all-to-all(bf16[64,40,128]{2,1,0:T(8,128)(2,1)S(1)} %pack.1), channel_id=1, replica_groups=mesh['pair'=4,'side'=2,'row'=8,'col'=8] {'row','col'}, dimensions={0} | all-to-all | bytes 1310720 | tf_op jit(solution)/shard_map/scatter/all_to_all | solution.py:388
  38.6 2.5 %collective-permute-start = (bf16[64,24,128]{2,1,0:T(8,128)(2,1)S(1)}, bf16[64,24,128]{2,1,0:T(8,128)(2,1)S(1)}, u32[]{:S(2)}, u32[]{:S(2)}) collective-permute-start(bf16[64,24,128]{2,1,0:T(8,128)(2,1)S(1)} %slice.8), channel_id=1, source_target_pairs={{0,1},{1,0},{2,3},{3,2},{4,5},{5,4},{6,7},{7,6},{8,9},{9,8},{10,11... | collective-permute-start | bytes 1179656 | tf_op jit(solution)/shard_map/ppermute | solution.py:392
  41.0 0.0 copy-done
  41.1 1.8 %sort.1 = (f32[65,8,128]{2,1,0:T(8,128)S(1)}, f32[65,8,128]{2,1,0:T(8,128)S(1)}, f32[65,8,128]{2,1,0:T(8,128)S(1)}, f32[64,512]{1,0:T(8,128)S(1)}, f32[17,8,512]...) custom-call(bf16[64,40,128]{2,1,0:T(8,128)(2,1)S(1)} %all_to_all.10., ...), custom_call_target="tpu_custom_call" | custom-call | tf_op jit(solution)/shard_map/do_sort/sort/pallas_call | solution.py:38
  42.9 0.0 collective-permute-done.other
  42.9 2.0 %route.1 = bf16[128,40,128]{2,1,0:T(8,128)(2,1)S(1)} custom-call(bf16[64,24,128]{2,1,0:T(8,128)(2,1)S(1)} %collective-permute-done.other, f32[65,8,128]{2,1,0:T(8,128)S(1)} %get-tuple-element.20.t0, f32[65,8,128]{2,1,0:T(8,128)S(1)} %get-tuple-element.21.g0, f32[65,8,128]{2,1,0:T(8,128)S(1)} %get-tuple-element.22.g1, f32[64,512]{1,0:T(8,128)S(1)} %get-tuple-element.23.left, ...), custom_call_target="tpu_custom_call" | custom-call | tf_op jit(solution)/shard_map/do_route/route/pallas_call | solution.py:38
  44.9 41.5 %all_to_all.11.blocks = bf16[128,40,128]{2,1,0:T(8,128)(2,1)S(1)} all-to-all(bf16[128,40,128]{2,1,0:T(8,128)(2,1)S(1)} %route.1), channel_id=1, replica_groups=mesh['pair'=4,'side'=2,'row'=8,'col'=8] {'side','row','col'}, dimensions={0} | all-to-all | bytes 2621440 | tf_op jit(solution)/shard_map/gather/all_to_all | solution.py:388
  86.4 3.9 %collective-permute-start.1 = (bf16[128,8,128]{2,1,0:T(8,128)(2,1)S(1)}, bf16[128,8,128]{2,1,0:T(8,128)(2,1)S(1)}, u32[]{:S(2)}, u32[]{:S(2)}) collective-permute-start(bf16[128,8,128]{2,1,0:T(8,128)(2,1)S(1)} %slice.9), channel_id=1, source_target_pairs={{0,1},{1,0},{2,3},{3,2},{4,5},{5,4},{6,7},{7,6},{8,9},{9,8},{10,11... | collective-permute-start | bytes 786440 | tf_op jit(solution)/shard_map/ppermute | solution.py:392
  90.3 1.0 %gather_up.1 = (bf16[2,256,512]{2,1,0:T(8,128)(2,1)S(1)}, bf16[2,256,512]{2,1,0:T(8,128)(2,1)S(1)}, bf16[256,512]{1,0:T(8,128)(2,1)S(1)}, bf16[4,128,128]{2,1,0:...) custom-call(bf16[128,40,128]{2,1,0:T(8,128)(2,1)S(1)} %all_to_all.11.blocks), custom_call_target="tpu_custom_call" | custom-call | tf_op jit(solution)/shard_map/do_gather_up/gather_up/pallas_call | solution.py:38
  91.3 0.1 collective-permute-done.1.twin
  91.4 1.9 %finish.1 = bf16[2,512,512]{2,1,0:T(8,128)(2,1)} custom-call(bf16[128,8,128]{2,1,0:T(8,128)(2,1)S(1)} %collective-permute-done.1.twin, bf16[2,256,512]{2,1,0:T(8,128)(2,1)S(1)} %get-tuple-element.29.lefts, bf16[2,256,512]{2,1,0:T(8,128)(2,1)S(1)} %get-tuple-element.30.rights, bf16[256,512]{1,0:T(8,128)(2,1)S(1)} %get-tuple-element.31.row_v, ...), custom_call_target="tpu_custom_call" | custom-call | tf_op jit(solution)/shard_map/do_finish/finish/pallas_call | solution.py:38
  (2 shorter events, 0.1 us)
Async XLA Ops:
  1.9 39.1 %copy-start = (s32[1,8]{1,0:T(1,128)S(1)}, s32[1,8]{1,0:T(1,128)}, u32[]{:S(2)}) copy-start(s32[1,8]{1,0:T(1,128)} %mapping.3) | copy-start | bytes 100
  38.6 4.3 %collective-permute-start = (bf16[64,24,128]{2,1,0:T(8,128)(2,1)S(1)}, bf16[64,24,128]{2,1,0:T(8,128)(2,1)S(1)}, u32[]{:S(2)}, u32[]{:S(2)}) collective-permute-start(bf16[64,24,128]{2,1,0:T(8,128)(2,1)S(1)} %slice.8), channel_id=1, source_target_pairs={{0,1},{1,0},{2,3},{3,2},{4,5},{5,4},{6,7},{7,6},{8,9},{9,8},{10,11... | collective-permute-start | bytes 1179656 | tf_op jit(solution)/shard_map/ppermute | solution.py:392
  86.4 5.0 %collective-permute-start.1 = (bf16[128,8,128]{2,1,0:T(8,128)(2,1)S(1)}, bf16[128,8,128]{2,1,0:T(8,128)(2,1)S(1)}, u32[]{:S(2)}, u32[]{:S(2)}) collective-permute-start(bf16[128,8,128]{2,1,0:T(8,128)(2,1)S(1)} %slice.9), channel_id=1, source_target_pairs={{0,1},{1,0},{2,3},{3,2},{4,5},{5,4},{6,7},{7,6},{8,9},{9,8},{10,11... | collective-permute-start | bytes 786440 | tf_op jit(solution)/shard_map/ppermute | solution.py:392

commit v10 on v9

--- a/solution.py
+++ b/solution.py
@@ -166,9 +166,8 @@
 
 
 def sort(
-    got, mapping, t0, g0, g1, left, right_ref, row_ref, pair_ref, off, inv, inverse, col_ref
+    got, t0, g0, g1, left, right_ref, row_ref, col_ref, off, inv
 ):
-    fill_inverse(mapping, inverse)
     sub = iota((8, 128), 0)
     lane = iota((8, 128), 1)
     valid = sub < 6
@@ -211,15 +210,11 @@
         right_ref[2 * j] = parts[0]
         right_ref[2 * j + 1] = parts[1]
         row_ref[j] = jnp.where(valid, thin[j], 0.0)
-    for r in range(N):
-        x = col_ref[inverse[2 * r]]
-        y = col_ref[inverse[2 * r + 1]]
-        pair_ref[2 * r] = jnp.where(lane < 64, x, pltpu.roll(y, 64, 1))
-        pair_ref[2 * r + 1] = jnp.where(lane < 64, pltpu.roll(x, 64, 1), y)
 
 
 def route(
-    other, t0, g0, g1, left, right_ref, row_ref, pair_ref, off, inv, mapping, send, inverse, lower_ref, off_ref
+    other, t0, g0, g1, left, right_ref, row_ref, col_ref, off, inv, mapping, send, inverse, lower_ref, off_ref,
+    pair_ref
 ):
     fill_inverse(mapping, inverse)
     core_id = lax.axis_index("col") % 2
@@ -260,7 +255,13 @@
     )
     core = core.astype(BF16).astype(F32)
     place = iota((64, 128), 1) // 16
-    low_lanes = iota((8, 128), 1) < 64
+    lane = iota((8, 128), 1)
+    low_lanes = lane < 64
+    for r in range(N):
+        x = col_ref[inverse[2 * r]]
+        y = col_ref[inverse[2 * r + 1]]
+        pair_ref[2 * r] = jnp.where(lane < 64, x, pltpu.roll(y, 64, 1))
+        pair_ref[2 * r + 1] = jnp.where(lane < 64, pltpu.roll(x, 64, 1), y)
     for k in range(2 * N):
         c, h = k // 2, k % 2
         total = jnp.zeros((64, 128), F32)
@@ -373,10 +374,10 @@
     for s in range(2):
         both = jnp.concatenate([lefts[s]] + updates[s], axis=0)
         right = jnp.concatenate([rights[s], row_v[...]], axis=0)
-        for part in range(2):
-            rows = slice(256 * part, 256 * part + 256)
+        for part in range(4):
+            rows = slice(128 * part, 128 * part + 128)
             made[s, rows, :] = dot(both[:, rows], right, (0, 0)).astype(BF16)
-            copy = pltpu.make_async_copy(made.at[s, rows], out.at[s, rows], sems.at[2 * s + part])
+            copy = pltpu.make_async_copy(made.at[s, rows], out.at[s, rows], sems.at[4 * s + part])
             copy.start()
             stores.append(copy)
     for copy in stores:
@@ -429,13 +430,12 @@
             VMEM((64, TILE), F32),
             VMEM((2 * N + 1, 8, TILE), F32),
             VMEM((N + 1, 8, 128), F32),
-            VMEM((2 * N, 8, 128), F32),
+            VMEM((N + 1, 8, 128), F32),
             VMEM((TILE, TILE // 2), BF16),
             VMEM((8, TILE), F32),
         ),
-        (got, parent_map),
-        (VMEM, VMEM),
-        (SMEM((2 * N,), jnp.int32), VMEM((N + 1, 8, 128), F32)),
+        (got,),
+        (VMEM,),
         name="sort",
     )
     (send,) = call(
@@ -447,6 +447,7 @@
             SMEM((2 * N,), jnp.int32),
             VMEM((2 * N + 1, 8, TILE), F32),
             VMEM((2, TILE, TILE // 2), BF16),
+            VMEM((2 * N, 8, 128), F32),
         ),
         name="route",
     )
@@ -474,7 +475,7 @@
         (VMEM,) * 7,
         (
             VMEM((2, TILE, TILE), BF16),
-            pltpu.SemaphoreType.DMA((4,)),
+            pltpu.SemaphoreType.DMA((8,)),
         ),
         name="finish",
         into=pl.ANY,

time: 93.6 us -> 93.5 us (level)
  no operation moved by 1% of the time
where the time goes in v10:
time: 93.5 us; the launch traced here: 93.2 us
  blocking collectives  76.5 us (82%)
  Pallas kernels  8.15 us (9%)
  starting transfers between devices  6.33 us (7%)
  between operations  2.02 us (2%)
    all_to_all x2, blocking collectives, exchange(): return lax.all_to_all(x, axes, split_axis=0, concat_axis=0, tiled=True)  76.5 us
    pallas_call x5, Pallas kernels, call(): return kernel(*args)  8.15 us
    ppermute x2, starting transfers between devices, swap(): return lax.ppermute(x, 'col', [(k, k ^ 1) for k in range(N)])  6.33 us
  transfers between devices with their start and end apart: 2, of which 1 were waited for; matrix products, arithmetic and copies ran while one was open for 0% of the time, Pallas kernels for 3%

profile of v10, /device:TPU:1, one launch (start us, length us, event | category | flops | bytes accessed | tf_op | source)
XLA Modules:
  0.0 93.2 jit_solution(3913912309687955398)
XLA Ops:
  1.9 1.6 %pack.1 = bf16[64,40,128]{2,1,0:T(8,128)(2,1)S(1)} custom-call(f32[8,512]{1,0:T(8,128)} %bitcast.20, bf16[64,96]{1,0:T(8,128)(2,1)} %bitcast.21, bf16[64,96]{1,0:T(8,128)(2,1)} %bitcast.22, bf16[64,96]{1,0:T(8,128)(2,1)} %bitcast.23, bf16[64,96]{1,0:T(8,128)(2,1)} %bitcast.24, bf16[96,512]{1,0:T(8,128)(2,1)} %bitcast.18, bf16[96,512]{1,0:T(8,128)(2,1)} %bitcast.19, ...), custom_call_target="tpu_custom_call" | custom-call | tf_op jit(solution)/shard_map/do_pack/pack/pallas_call | solution.py:38
  3.6 0.0 copy-start
  3.6 35.0 %all_to_all.10.got = bf16[64,40,128]{2,1,0:T(8,128)(2,1)S(1)} all-to-all(bf16[64,40,128]{2,1,0:T(8,128)(2,1)S(1)} %pack.1), channel_id=1, replica_groups=mesh['pair'=4,'side'=2,'row'=8,'col'=8] {'row','col'}, dimensions={0} | all-to-all | bytes 1310720 | tf_op jit(solution)/shard_map/scatter/all_to_all | solution.py:389
  38.6 2.5 %collective-permute-start = (bf16[64,24,128]{2,1,0:T(8,128)(2,1)S(1)}, bf16[64,24,128]{2,1,0:T(8,128)(2,1)S(1)}, u32[]{:S(2)}, u32[]{:S(2)}) collective-permute-start(bf16[64,24,128]{2,1,0:T(8,128)(2,1)S(1)} %slice.8), channel_id=1, source_target_pairs={{0,1},{1,0},{2,3},{3,2},{4,5},{5,4},{6,7},{7,6},{8,9},{9,8},{10,11... | collective-permute-start | bytes 1179656 | tf_op jit(solution)/shard_map/ppermute | solution.py:393
  41.0 1.7 %sort.1 = (f32[65,8,128]{2,1,0:T(8,128)S(1)}, f32[65,8,128]{2,1,0:T(8,128)S(1)}, f32[65,8,128]{2,1,0:T(8,128)S(1)}, f32[64,512]{1,0:T(8,128)S(1)}, f32[17,8,512]...) custom-call(bf16[64,40,128]{2,1,0:T(8,128)(2,1)S(1)} %all_to_all.10.got), custom_call_target="tpu_custom_call" | custom-call | tf_op jit(solution)/shard_map/do_sort/sort/pallas_call | solution.py:38
  42.7 0.0 collective-permute-done.other
  42.7 0.0 copy-done
  42.8 1.9 %route.1 = bf16[128,40,128]{2,1,0:T(8,128)(2,1)S(1)} custom-call(bf16[64,24,128]{2,1,0:T(8,128)(2,1)S(1)} %collective-permute-done.other, f32[65,8,128]{2,1,0:T(8,128)S(1)} %get-tuple-element.20.t0, f32[65,8,128]{2,1,0:T(8,128)S(1)} %get-tuple-element.21.g0, f32[65,8,128]{2,1,0:T(8,128)S(1)} %get-tuple-element.22.g1, f32[64,512]{1,0:T(8,128)S(1)} %get-tuple-element.23.left, ...), custom_call_target="tpu_custom_call" | custom-call | tf_op jit(solution)/shard_map/do_route/route/pallas_call | solution.py:38
  44.7 41.5 %all_to_all.11.blocks = bf16[128,40,128]{2,1,0:T(8,128)(2,1)S(1)} all-to-all(bf16[128,40,128]{2,1,0:T(8,128)(2,1)S(1)} %route.1), channel_id=1, replica_groups=mesh['pair'=4,'side'=2,'row'=8,'col'=8] {'side','row','col'}, dimensions={0} | all-to-all | bytes 2621440 | tf_op jit(solution)/shard_map/gather/all_to_all | solution.py:389
  86.2 3.9 %collective-permute-start.1 = (bf16[128,8,128]{2,1,0:T(8,128)(2,1)S(1)}, bf16[128,8,128]{2,1,0:T(8,128)(2,1)S(1)}, u32[]{:S(2)}, u32[]{:S(2)}) collective-permute-start(bf16[128,8,128]{2,1,0:T(8,128)(2,1)S(1)} %slice.9), channel_id=1, source_target_pairs={{0,1},{1,0},{2,3},{3,2},{4,5},{5,4},{6,7},{7,6},{8,9},{9,8},{10,11... | collective-permute-start | bytes 786440 | tf_op jit(solution)/shard_map/ppermute | solution.py:393
  90.1 1.0 %gather_up.1 = (bf16[2,256,512]{2,1,0:T(8,128)(2,1)S(1)}, bf16[2,256,512]{2,1,0:T(8,128)(2,1)S(1)}, bf16[256,512]{1,0:T(8,128)(2,1)S(1)}, bf16[4,128,128]{2,1,0:...) custom-call(bf16[128,40,128]{2,1,0:T(8,128)(2,1)S(1)} %all_to_all.11.blocks), custom_call_target="tpu_custom_call" | custom-call | tf_op jit(solution)/shard_map/do_gather_up/gather_up/pallas_call | solution.py:38
  91.1 0.1 collective-permute-done.1.twin
  91.2 2.0 %finish.1 = bf16[2,512,512]{2,1,0:T(8,128)(2,1)} custom-call(bf16[128,8,128]{2,1,0:T(8,128)(2,1)S(1)} %collective-permute-done.1.twin, bf16[2,256,512]{2,1,0:T(8,128)(2,1)S(1)} %get-tuple-element.29.lefts, bf16[2,256,512]{2,1,0:T(8,128)(2,1)S(1)} %get-tuple-element.30.rights, bf16[256,512]{1,0:T(8,128)(2,1)S(1)} %get-tuple-element.31.row_v, ...), custom_call_target="tpu_custom_call" | custom-call | tf_op jit(solution)/shard_map/do_finish/finish/pallas_call | solution.py:38
  (2 shorter events, 0.1 us)
Async XLA Ops:
  3.6 39.2 %copy-start = (s32[1,8]{1,0:T(1,128)S(1)}, s32[1,8]{1,0:T(1,128)}, u32[]{:S(2)}) copy-start(s32[1,8]{1,0:T(1,128)} %mapping.1) | copy-start | bytes 100
  38.6 4.2 %collective-permute-start = (bf16[64,24,128]{2,1,0:T(8,128)(2,1)S(1)}, bf16[64,24,128]{2,1,0:T(8,128)(2,1)S(1)}, u32[]{:S(2)}, u32[]{:S(2)}) collective-permute-start(bf16[64,24,128]{2,1,0:T(8,128)(2,1)S(1)} %slice.8), channel_id=1, source_target_pairs={{0,1},{1,0},{2,3},{3,2},{4,5},{5,4},{6,7},{7,6},{8,9},{9,8},{10,11... | collective-permute-start | bytes 1179656 | tf_op jit(solution)/shard_map/ppermute | solution.py:393
  86.2 5.0 %collective-permute-start.1 = (bf16[128,8,128]{2,1,0:T(8,128)(2,1)S(1)}, bf16[128,8,128]{2,1,0:T(8,128)(2,1)S(1)}, u32[]{:S(2)}, u32[]{:S(2)}) collective-permute-start(bf16[128,8,128]{2,1,0:T(8,128)(2,1)S(1)} %slice.9), channel_id=1, source_target_pairs={{0,1},{1,0},{2,3},{3,2},{4,5},{5,4},{6,7},{7,6},{8,9},{9,8},{10,11... | collective-permute-start | bytes 786440 | tf_op jit(solution)/shard_map/ppermute | solution.py:393

commit v11 on v10

--- a/solution.py
+++ b/solution.py
@@ -172,9 +172,11 @@
     lane = iota((8, 128), 1)
     valid = sub < 6
     zero = jnp.zeros((8, 128), F32)
-    t0[64] = zero
-    g0[64] = zero
-    g1[64] = zero
+    for k in range(N + 1):
+        for at in sorted({N * (N + 1) + k, k * (N + 1) + N}):
+            t0[at] = zero
+            g0[at] = zero
+            g1[at] = zero
     right = [[] for _ in range(N)]
     thin = [zero] * N
     diag = [zero] * 4
@@ -185,9 +187,10 @@
             k = i * N + j
             x = got[k, 0:24, :].astype(F32)
             a, b = x[8:16], x[16:24]
-            t0[k] = x[0:8]
-            g0[k] = jnp.where(sub >= 6, a, jnp.where(sub >= 4, pltpu.roll(b, 6, 0), 0.0))
-            g1[k] = jnp.where(
+            at = i * (N + 1) + j
+            t0[at] = x[0:8]
+            g0[at] = jnp.where(sub >= 6, a, jnp.where(sub >= 4, pltpu.roll(b, 6, 0), 0.0))
+            g1[at] = jnp.where(
                 sub >= 4, 0.0, jnp.where(sub >= 2, pltpu.roll(a, 4, 0), pltpu.roll(b, 2, 0))
             )
             right[j].append(jnp.where(valid, a, 0.0))
@@ -204,6 +207,7 @@
     full = 1.0 / jnp.concatenate([x[0:1] for x in diag], axis=1)
     inv[...] = jnp.broadcast_to(full, (8, TILE))
     right_ref[2 * N] = jnp.zeros((8, TILE), F32)
+    right_ref[2 * N + 1] = jnp.zeros((8, TILE), F32)
     row_ref[N] = zero
     for j in range(N):
         parts = spread(right[j])
@@ -235,31 +239,32 @@
     y = v - times(v)
     z = y + times(y)
     lower = 2.0 * y - z + times(z)
-    for k in range(2 * N):
-        lower_ref[k] = lower[8 * k : 8 * k + 8]
-    lower_ref[2 * N] = jnp.zeros((8, TILE), F32)
+    for half in range(2):
+        for i in range(N):
+            at = 8 * (half * N + i)
+            lower_ref[half * (N + 1) + i] = lower[at : at + 8]
+        lower_ref[half * (N + 1) + N] = jnp.zeros((8, TILE), F32)
+    index = [inverse[k] for k in range(2 * N)]
     rows = []
     for half in range(2):
         for s in range(2):
             for r in range(N):
-                i = inverse[2 * r + s]
-                at = jnp.bitwise_xor(half, core_id) * N + i
-                rows.append(lower_ref[jnp.where(i < N, at, 2 * N)])
+                rows.append(lower_ref[jnp.bitwise_xor(half, core_id) * (N + 1) + index[2 * r + s]])
     cols = []
     for k in range(2 * N):
-        j = inverse[k]
         for half in range(2):
-            cols.append(right_ref[jnp.where(j < N, 2 * j + half, 2 * N)])
+            cols.append(right_ref[2 * index[k] + half])
     core = dot(
         jnp.concatenate(rows, axis=0).astype(BF16), jnp.concatenate(cols, axis=0).astype(BF16), (1, 1)
     )
     core = core.astype(BF16).astype(F32)
+    first = [(N + 1) * x for x in index]
     place = iota((64, 128), 1) // 16
     lane = iota((8, 128), 1)
     low_lanes = lane < 64
     for r in range(N):
-        x = col_ref[inverse[2 * r]]
-        y = col_ref[inverse[2 * r + 1]]
+        x = col_ref[index[2 * r]]
+        y = col_ref[index[2 * r + 1]]
         pair_ref[2 * r] = jnp.where(lane < 64, x, pltpu.roll(y, 64, 1))
         pair_ref[2 * r + 1] = jnp.where(lane < 64, pltpu.roll(x, 64, 1), y)
     for k in range(2 * N):
@@ -269,15 +274,13 @@
             x = core[64 * combo : 64 * combo + 64, 128 * (k // 8) : 128 * (k // 8) + 128]
             total = jnp.where(place == combo, move(x, 16 * (k % 8), 16 * combo), total)
         beside = pltpu.roll(total, 64, 1)
-        j = inverse[k]
+        j = index[k]
         tail = row_ref[j]
         for r in range(N):
             part = total[8 * r : 8 * r + 8]
             shifted = beside[8 * r : 8 * r + 8]
-            i0 = inverse[2 * r]
-            i1 = inverse[2 * r + 1]
-            at0 = jnp.where((i0 < N) & (j < N), i0 * N + j, 64)
-            at1 = jnp.where((i1 < N) & (j < N), i1 * N + j, 64)
+            at0 = first[2 * r] + j
+            at1 = first[2 * r + 1] + j
             spare = jnp.where(low_lanes, pltpu.roll(part, 6, 0), pltpu.roll(shifted, 4, 0))
             send[(h * N + r) * N + c] = jnp.concatenate(
                 [
@@ -425,10 +428,10 @@
     got = in_vmem(got)
     sorted_out = call(
         sort,
-        (VMEM((65, 8, 128), F32),) * 3
+        (VMEM(((N + 1) ** 2, 8, 128), F32),) * 3
         + (
             VMEM((64, TILE), F32),
-            VMEM((2 * N + 1, 8, TILE), F32),
+            VMEM((2 * N + 2, 8, TILE), F32),
             VMEM((N + 1, 8, 128), F32),
             VMEM((N + 1, 8, 128), F32),
             VMEM((TILE, TILE // 2), BF16),
@@ -445,7 +448,7 @@
         (VMEM,) * 11,
         (
             SMEM((2 * N,), jnp.int32),
-            VMEM((2 * N + 1, 8, TILE), F32),
+            VMEM((2 * N + 2, 8, TILE), F32),
             VMEM((2, TILE, TILE // 2), BF16),
             VMEM((2 * N, 8, 128), F32),
         ),

time: 93.5 us -> 93.3 us (level)
  no operation moved by 1% of the time
where the time goes in v11:
time: 93.3 us; the launch traced here: 93 us
  blocking collectives  76.5 us (82%)
  Pallas kernels  7.99 us (9%)
  starting transfers between devices  6.33 us (7%)
  between operations  2.02 us (2%)
    all_to_all x2, blocking collectives, exchange(): return lax.all_to_all(x, axes, split_axis=0, concat_axis=0, tiled=True)  76.5 us
    pallas_call x5, Pallas kernels, call(): return kernel(*args)  7.99 us
    ppermute x2, starting transfers between devices, swap(): return lax.ppermute(x, 'col', [(k, k ^ 1) for k in range(N)])  6.33 us
  transfers between devices with their start and end apart: 2, of which 1 were waited for; matrix products, arithmetic and copies ran while one was open for 0% of the time, Pallas kernels for 3%

profile of v11, /device:TPU:1, one launch (start us, length us, event | category | flops | bytes accessed | tf_op | source)
XLA Modules:
  0.0 93.0 jit_solution(6132796350999174151)
XLA Ops:
  1.9 1.6 %pack.1 = bf16[64,40,128]{2,1,0:T(8,128)(2,1)S(1)} custom-call(f32[8,512]{1,0:T(8,128)} %bitcast.20, bf16[64,96]{1,0:T(8,128)(2,1)} %bitcast.21, bf16[64,96]{1,0:T(8,128)(2,1)} %bitcast.22, bf16[64,96]{1,0:T(8,128)(2,1)} %bitcast.23, bf16[64,96]{1,0:T(8,128)(2,1)} %bitcast.24, bf16[96,512]{1,0:T(8,128)(2,1)} %bitcast.18, bf16[96,512]{1,0:T(8,128)(2,1)} %bitcast.19, ...), custom_call_target="tpu_custom_call" | custom-call | tf_op jit(solution)/shard_map/do_pack/pack/pallas_call | solution.py:38
  3.6 0.0 copy-start
  3.6 35.0 %all_to_all.10.got = bf16[64,40,128]{2,1,0:T(8,128)(2,1)S(1)} all-to-all(bf16[64,40,128]{2,1,0:T(8,128)(2,1)S(1)} %pack.1), channel_id=1, replica_groups=mesh['pair'=4,'side'=2,'row'=8,'col'=8] {'row','col'}, dimensions={0} | all-to-all | bytes 1310720 | tf_op jit(solution)/shard_map/scatter/all_to_all | solution.py:392
  38.6 2.5 %collective-permute-start = (bf16[64,24,128]{2,1,0:T(8,128)(2,1)S(1)}, bf16[64,24,128]{2,1,0:T(8,128)(2,1)S(1)}, u32[]{:S(2)}, u32[]{:S(2)}) collective-permute-start(bf16[64,24,128]{2,1,0:T(8,128)(2,1)S(1)} %slice.8), channel_id=1, source_target_pairs={{0,1},{1,0},{2,3},{3,2},{4,5},{5,4},{6,7},{7,6},{8,9},{9,8},{10,11... | collective-permute-start | bytes 1179656 | tf_op jit(solution)/shard_map/ppermute | solution.py:396
  41.0 1.7 %sort.1 = (f32[81,8,128]{2,1,0:T(8,128)S(1)}, f32[81,8,128]{2,1,0:T(8,128)S(1)}, f32[81,8,128]{2,1,0:T(8,128)S(1)}, f32[64,512]{1,0:T(8,128)S(1)}, f32[18,8,512]...) custom-call(bf16[64,40,128]{2,1,0:T(8,128)(2,1)S(1)} %all_to_all.10.got), custom_call_target="tpu_custom_call" | custom-call | tf_op jit(solution)/shard_map/do_sort/sort/pallas_call | solution.py:38
  42.7 0.0 collective-permute-done.other
  42.7 0.0 copy-done
  42.8 1.7 %route.1 = bf16[128,40,128]{2,1,0:T(8,128)(2,1)S(1)} custom-call(bf16[64,24,128]{2,1,0:T(8,128)(2,1)S(1)} %collective-permute-done.other, f32[81,8,128]{2,1,0:T(8,128)S(1)} %get-tuple-element.20.t0, f32[81,8,128]{2,1,0:T(8,128)S(1)} %get-tuple-element.21.g0, f32[81,8,128]{2,1,0:T(8,128)S(1)} %get-tuple-element.22.g1, f32[64,512]{1,0:T(8,128)S(1)} %get-tuple-element.23.left, ...), custom_call_target="tpu_custom_call" | custom-call | tf_op jit(solution)/shard_map/do_route/route/pallas_call | solution.py:38
  44.5 41.5 %all_to_all.11.blocks = bf16[128,40,128]{2,1,0:T(8,128)(2,1)S(1)} all-to-all(bf16[128,40,128]{2,1,0:T(8,128)(2,1)S(1)} %route.1), channel_id=1, replica_groups=mesh['pair'=4,'side'=2,'row'=8,'col'=8] {'side','row','col'}, dimensions={0} | all-to-all | bytes 2621440 | tf_op jit(solution)/shard_map/gather/all_to_all | solution.py:392
  86.0 3.9 %collective-permute-start.1 = (bf16[128,8,128]{2,1,0:T(8,128)(2,1)S(1)}, bf16[128,8,128]{2,1,0:T(8,128)(2,1)S(1)}, u32[]{:S(2)}, u32[]{:S(2)}) collective-permute-start(bf16[128,8,128]{2,1,0:T(8,128)(2,1)S(1)} %slice.9), channel_id=1, source_target_pairs={{0,1},{1,0},{2,3},{3,2},{4,5},{5,4},{6,7},{7,6},{8,9},{9,8},{10,11... | collective-permute-start | bytes 786440 | tf_op jit(solution)/shard_map/ppermute | solution.py:396
  89.9 1.0 %gather_up.1 = (bf16[2,256,512]{2,1,0:T(8,128)(2,1)S(1)}, bf16[2,256,512]{2,1,0:T(8,128)(2,1)S(1)}, bf16[256,512]{1,0:T(8,128)(2,1)S(1)}, bf16[4,128,128]{2,1,0:...) custom-call(bf16[128,40,128]{2,1,0:T(8,128)(2,1)S(1)} %all_to_all.11.blocks), custom_call_target="tpu_custom_call" | custom-call | tf_op jit(solution)/shard_map/do_gather_up/gather_up/pallas_call | solution.py:38
  90.9 0.1 collective-permute-done.1.twin
  91.1 2.0 %finish.1 = bf16[2,512,512]{2,1,0:T(8,128)(2,1)} custom-call(bf16[128,8,128]{2,1,0:T(8,128)(2,1)S(1)} %collective-permute-done.1.twin, bf16[2,256,512]{2,1,0:T(8,128)(2,1)S(1)} %get-tuple-element.29.lefts, bf16[2,256,512]{2,1,0:T(8,128)(2,1)S(1)} %get-tuple-element.30.rights, bf16[256,512]{1,0:T(8,128)(2,1)S(1)} %get-tuple-element.31.row_v, ...), custom_call_target="tpu_custom_call" | custom-call | tf_op jit(solution)/shard_map/do_finish/finish/pallas_call | solution.py:38
  (2 shorter events, 0.1 us)
Async XLA Ops:
  3.6 39.2 %copy-start = (s32[1,8]{1,0:T(1,128)S(1)}, s32[1,8]{1,0:T(1,128)}, u32[]{:S(2)}) copy-start(s32[1,8]{1,0:T(1,128)} %mapping.1) | copy-start | bytes 100
  38.6 4.2 %collective-permute-start = (bf16[64,24,128]{2,1,0:T(8,128)(2,1)S(1)}, bf16[64,24,128]{2,1,0:T(8,128)(2,1)S(1)}, u32[]{:S(2)}, u32[]{:S(2)}) collective-permute-start(bf16[64,24,128]{2,1,0:T(8,128)(2,1)S(1)} %slice.8), channel_id=1, source_target_pairs={{0,1},{1,0},{2,3},{3,2},{4,5},{5,4},{6,7},{7,6},{8,9},{9,8},{10,11... | collective-permute-start | bytes 1179656 | tf_op jit(solution)/shard_map/ppermute | solution.py:396
  86.0 5.0 %collective-permute-start.1 = (bf16[128,8,128]{2,1,0:T(8,128)(2,1)S(1)}, bf16[128,8,128]{2,1,0:T(8,128)(2,1)S(1)}, u32[]{:S(2)}, u32[]{:S(2)}) collective-permute-start(bf16[128,8,128]{2,1,0:T(8,128)(2,1)S(1)} %slice.9), channel_id=1, source_target_pairs={{0,1},{1,0},{2,3},{3,2},{4,5},{5,4},{6,7},{7,6},{8,9},{9,8},{10,11... | collective-permute-start | bytes 786440 | tf_op jit(solution)/shard_map/ppermute | solution.py:396

commit v12 on v11

--- a/solution.py
+++ b/solution.py
@@ -366,16 +366,16 @@
         other += half_panels(
             [[twin[f * 64 + g * N + c].astype(F32) for c in range(N)] for g in range(N)]
         )
-    other = dot(jnp.concatenate(other, axis=0).astype(BF16), order[...], (1, 0)).astype(BF16)
-    updates = [[], []]
-    for f in range(2):
-        for s in range(2):
-            at = slice(64 * (2 * f + s), 64 * (2 * f + s) + 64)
-            col_u = jnp.concatenate([own_u[at, :], other[at]], axis=0)
-            updates[s].append((-dot(cores[2 * f + s], col_u, (0, 0))).astype(BF16))
     stores = []
     for s in range(2):
-        both = jnp.concatenate([lefts[s]] + updates[s], axis=0)
+        half = jnp.concatenate([other[s], other[2 + s]], axis=0).astype(BF16)
+        half = dot(half, order[...], (1, 0)).astype(BF16)
+        updates = []
+        for f in range(2):
+            at = slice(64 * (2 * f + s), 64 * (2 * f + s) + 64)
+            col_u = jnp.concatenate([own_u[at, :], half[64 * f : 64 * f + 64]], axis=0)
+            updates.append((-dot(cores[2 * f + s], col_u, (0, 0))).astype(BF16))
+        both = jnp.concatenate([lefts[s]] + updates, axis=0)
         right = jnp.concatenate([rights[s], row_v[...]], axis=0)
         for part in range(4):
             rows = slice(128 * part, 128 * part + 128)

time: 93.3 us -> 93.6 us (level)
  no operation moved by 1% of the time
where the time goes in v12:
time: 93.6 us; the launch traced here: 93.4 us
  blocking collectives  76.5 us (82%)
  Pallas kernels  8.33 us (9%)
  starting transfers between devices  6.33 us (7%)
  between operations  2.02 us (2%)
    all_to_all x2, blocking collectives, exchange(): return lax.all_to_all(x, axes, split_axis=0, concat_axis=0, tiled=True)  76.5 us
    pallas_call x5, Pallas kernels, call(): return kernel(*args)  8.33 us
    ppermute x2, starting transfers between devices, swap(): return lax.ppermute(x, 'col', [(k, k ^ 1) for k in range(N)])  6.33 us
  transfers between devices with their start and end apart: 2, of which 1 were waited for; matrix products, arithmetic and copies ran while one was open for 0% of the time, Pallas kernels for 3%

profile of v12, /device:TPU:1, one launch (start us, length us, event | category | flops | bytes accessed | tf_op | source)
XLA Modules:
  0.0 93.4 jit_solution(17203376242983878115)
XLA Ops:
  1.9 1.6 %pack.1 = bf16[64,40,128]{2,1,0:T(8,128)(2,1)S(1)} custom-call(f32[8,512]{1,0:T(8,128)} %bitcast.20, bf16[64,96]{1,0:T(8,128)(2,1)} %bitcast.21, bf16[64,96]{1,0:T(8,128)(2,1)} %bitcast.22, bf16[64,96]{1,0:T(8,128)(2,1)} %bitcast.23, bf16[64,96]{1,0:T(8,128)(2,1)} %bitcast.24, bf16[96,512]{1,0:T(8,128)(2,1)} %bitcast.18, bf16[96,512]{1,0:T(8,128)(2,1)} %bitcast.19, ...), custom_call_target="tpu_custom_call" | custom-call | tf_op jit(solution)/shard_map/do_pack/pack/pallas_call | solution.py:38
  3.6 0.0 copy-start
  3.6 35.0 %all_to_all.10.got = bf16[64,40,128]{2,1,0:T(8,128)(2,1)S(1)} all-to-all(bf16[64,40,128]{2,1,0:T(8,128)(2,1)S(1)} %pack.1), channel_id=1, replica_groups=mesh['pair'=4,'side'=2,'row'=8,'col'=8] {'row','col'}, dimensions={0} | all-to-all | bytes 1310720 | tf_op jit(solution)/shard_map/scatter/all_to_all | solution.py:392
  38.6 2.5 %collective-permute-start = (bf16[64,24,128]{2,1,0:T(8,128)(2,1)S(1)}, bf16[64,24,128]{2,1,0:T(8,128)(2,1)S(1)}, u32[]{:S(2)}, u32[]{:S(2)}) collective-permute-start(bf16[64,24,128]{2,1,0:T(8,128)(2,1)S(1)} %slice.8), channel_id=1, source_target_pairs={{0,1},{1,0},{2,3},{3,2},{4,5},{5,4},{6,7},{7,6},{8,9},{9,8},{10,11... | collective-permute-start | bytes 1179656 | tf_op jit(solution)/shard_map/ppermute | solution.py:396
  41.0 1.7 %sort.1 = (f32[81,8,128]{2,1,0:T(8,128)S(1)}, f32[81,8,128]{2,1,0:T(8,128)S(1)}, f32[81,8,128]{2,1,0:T(8,128)S(1)}, f32[64,512]{1,0:T(8,128)S(1)}, f32[18,8,512]...) custom-call(bf16[64,40,128]{2,1,0:T(8,128)(2,1)S(1)} %all_to_all.10.got), custom_call_target="tpu_custom_call" | custom-call | tf_op jit(solution)/shard_map/do_sort/sort/pallas_call | solution.py:38
  42.7 0.0 collective-permute-done.other
  42.7 0.0 copy-done
  42.8 1.7 %route.1 = bf16[128,40,128]{2,1,0:T(8,128)(2,1)S(1)} custom-call(bf16[64,24,128]{2,1,0:T(8,128)(2,1)S(1)} %collective-permute-done.other, f32[81,8,128]{2,1,0:T(8,128)S(1)} %get-tuple-element.20.t0, f32[81,8,128]{2,1,0:T(8,128)S(1)} %get-tuple-element.21.g0, f32[81,8,128]{2,1,0:T(8,128)S(1)} %get-tuple-element.22.g1, f32[64,512]{1,0:T(8,128)S(1)} %get-tuple-element.23.left, ...), custom_call_target="tpu_custom_call" | custom-call | tf_op jit(solution)/shard_map/do_route/route/pallas_call | solution.py:38
  44.5 41.5 %all_to_all.11.blocks = bf16[128,40,128]{2,1,0:T(8,128)(2,1)S(1)} all-to-all(bf16[128,40,128]{2,1,0:T(8,128)(2,1)S(1)} %route.1), channel_id=1, replica_groups=mesh['pair'=4,'side'=2,'row'=8,'col'=8] {'side','row','col'}, dimensions={0} | all-to-all | bytes 2621440 | tf_op jit(solution)/shard_map/gather/all_to_all | solution.py:392
  86.0 3.9 %collective-permute-start.1 = (bf16[128,8,128]{2,1,0:T(8,128)(2,1)S(1)}, bf16[128,8,128]{2,1,0:T(8,128)(2,1)S(1)}, u32[]{:S(2)}, u32[]{:S(2)}) collective-permute-start(bf16[128,8,128]{2,1,0:T(8,128)(2,1)S(1)} %slice.9), channel_id=1, source_target_pairs={{0,1},{1,0},{2,3},{3,2},{4,5},{5,4},{6,7},{7,6},{8,9},{9,8},{10,11... | collective-permute-start | bytes 786440 | tf_op jit(solution)/shard_map/ppermute | solution.py:396
  89.9 1.0 %gather_up.1 = (bf16[2,256,512]{2,1,0:T(8,128)(2,1)S(1)}, bf16[2,256,512]{2,1,0:T(8,128)(2,1)S(1)}, bf16[256,512]{1,0:T(8,128)(2,1)S(1)}, bf16[4,128,128]{2,1,0:...) custom-call(bf16[128,40,128]{2,1,0:T(8,128)(2,1)S(1)} %all_to_all.11.blocks), custom_call_target="tpu_custom_call" | custom-call | tf_op jit(solution)/shard_map/do_gather_up/gather_up/pallas_call | solution.py:38
  90.9 0.1 collective-permute-done.1.twin
  91.1 2.3 %finish.1 = bf16[2,512,512]{2,1,0:T(8,128)(2,1)} custom-call(bf16[128,8,128]{2,1,0:T(8,128)(2,1)S(1)} %collective-permute-done.1.twin, bf16[2,256,512]{2,1,0:T(8,128)(2,1)S(1)} %get-tuple-element.29.lefts, bf16[2,256,512]{2,1,0:T(8,128)(2,1)S(1)} %get-tuple-element.30.rights, bf16[256,512]{1,0:T(8,128)(2,1)S(1)} %get-tuple-element.31.row_v, ...), custom_call_target="tpu_custom_call" | custom-call | tf_op jit(solution)/shard_map/do_finish/finish/pallas_call | solution.py:38
  (2 shorter events, 0.1 us)
Async XLA Ops:
  3.6 39.2 %copy-start = (s32[1,8]{1,0:T(1,128)S(1)}, s32[1,8]{1,0:T(1,128)}, u32[]{:S(2)}) copy-start(s32[1,8]{1,0:T(1,128)} %mapping.1) | copy-start | bytes 100
  38.6 4.2 %collective-permute-start = (bf16[64,24,128]{2,1,0:T(8,128)(2,1)S(1)}, bf16[64,24,128]{2,1,0:T(8,128)(2,1)S(1)}, u32[]{:S(2)}, u32[]{:S(2)}) collective-permute-start(bf16[64,24,128]{2,1,0:T(8,128)(2,1)S(1)} %slice.8), channel_id=1, source_target_pairs={{0,1},{1,0},{2,3},{3,2},{4,5},{5,4},{6,7},{7,6},{8,9},{9,8},{10,11... | collective-permute-start | bytes 1179656 | tf_op jit(solution)/shard_map/ppermute | solution.py:396
  86.0 5.0 %collective-permute-start.1 = (bf16[128,8,128]{2,1,0:T(8,128)(2,1)S(1)}, bf16[128,8,128]{2,1,0:T(8,128)(2,1)S(1)}, u32[]{:S(2)}, u32[]{:S(2)}) collective-permute-start(bf16[128,8,128]{2,1,0:T(8,128)(2,1)S(1)} %slice.9), channel_id=1, source_target_pairs={{0,1},{1,0},{2,3},{3,2},{4,5},{5,4},{6,7},{7,6},{8,9},{9,8},{10,11... | collective-permute-start | bytes 786440 | tf_op jit(solution)/shard_map/ppermute | solution.py:396
